TPU v7x, 8 devices: a whole 2x2x1 slice. The times are simulated.
8 devices in a mesh: dp: 1 (over z), tp: 8 (over y, x, core).
Axes of the slice: x: 2, y: 2, z: 1, core: 2. Of those that a mesh axis runs over, the one named last changes fastest.
Arguments:
- x_in: bfloat16 [32, 512, 1024], P('dp', 'tp')
- grad_y: bfloat16 [32, 512, 1024], P('dp', 'tp')
- pad_mask: int32 [32, 512], P('dp')
- ln1_gain: float32 [1024], replicated
- ln1_bias: float32 [1024], replicated
- w_qkv: bfloat16 [3, 1024, 16, 64], P(None, None, 'tp')
- b_qkv: float32 [3, 16, 64], P(None, 'tp')
- w_out: bfloat16 [16, 64, 1024], P('tp')
- b_out: float32 [1024], replicated
- ln2_gain: float32 [1024], replicated
- ln2_bias: float32 [1024], replicated
- w_up: bfloat16 [1024, 4096], P(None, 'tp')
- b_up: float32 [4096], P('tp')
- w_down: bfloat16 [4096, 1024], P('tp')
- b_down: float32 [1024], replicated
Outputs:
- output 1: bfloat16 [32, 512, 1024], P('dp', 'tp')
- output 2: bfloat16 [32, 512, 1024], P('dp', 'tp')
- output 3: float32 [1024], P('dp')
- output 4: float32 [1024], P('dp')
- output 5: float32 [3, 1024, 16, 64], P('dp', None, 'tp')
- output 6: float32 [3, 16, 64], P('dp', 'tp')
- output 7: float32 [16, 64, 1024], P(('dp', 'tp'))
- output 8: float32 [1024], P('dp')
- output 9: float32 [1024], P('dp')
- output 10: float32 [1024], P('dp')
- output 11: float32 [1024, 4096], P('dp', 'tp')
- output 12: float32 [4096], P(('dp', 'tp'))
- output 13: float32 [4096, 1024], P(('dp', 'tp'))
- output 14: float32 [1024], P('dp')
All inputs are finite; a program needn't handle non-finite values.
Results may differ from a plain program's by a relative error of at most 0.0121107.
Values are sent between devices in bfloat16 or wider.
A program may use at most 1 GiB of HBM per device.

v0:
```python
import jax
import jax.numpy as jnp
from jax import lax
from jax.sharding import PartitionSpec as P

LN_EPS = 1e-5
ROPE_BASE = 10000.0
INV_SQRT2 = 0.7071067811865476
INV_SQRT_2PI = 0.3989422804014327
NEG_LARGE = -1e30


def layer_norm(values, ln_gain, ln_bias):
    centered = values - jnp.mean(values, axis=-1, keepdims=True)
    inv_std = lax.rsqrt(jnp.mean(centered * centered, axis=-1, keepdims=True) + LN_EPS)
    x_hat = centered * inv_std
    return x_hat * ln_gain + ln_bias, x_hat, inv_std


def layer_norm_grad(d_out, x_hat, inv_std, ln_gain):
    d_hat = d_out * ln_gain
    return inv_std * (d_hat - jnp.mean(d_hat, axis=-1, keepdims=True) - x_hat * jnp.mean(d_hat * x_hat, axis=-1, keepdims=True))


def rope_tables(seq_len, head_dim):
    half_dim = head_dim // 2
    inv_freq = ROPE_BASE ** (-2.0 * jnp.arange(half_dim, dtype=jnp.float32) / head_dim)
    angles = jnp.arange(seq_len, dtype=jnp.float32)[:, None] * inv_freq[None, :]
    angles = jnp.concatenate([angles, angles], axis=-1)
    return jnp.cos(angles)[:, None, :], jnp.sin(angles)[:, None, :]


def rotate(tensor, cos_tab, sin_tab):
    half_dim = tensor.shape[-1] // 2
    swapped = jnp.concatenate([-tensor[..., half_dim:], tensor[..., :half_dim]], axis=-1)
    return tensor * cos_tab + swapped * sin_tab


def rotate_back(grad_in, cos_tab, sin_tab):
    half_dim = grad_in.shape[-1] // 2
    scaled = grad_in * sin_tab
    swapped = jnp.concatenate([scaled[..., half_dim:], -scaled[..., :half_dim]], axis=-1)
    return grad_in * cos_tab + swapped


def solution(mesh):
    act_spec = P('dp', 'tp', None)
    rep_vec = P(None)
    part_vec = P('dp')
    in_specs = (act_spec, act_spec, P('dp', None), rep_vec, rep_vec, P(None, None, 'tp', None), P(None, 'tp', None),
                P('tp', None, None), rep_vec, rep_vec, rep_vec, P(None, 'tp'), P('tp'), P('tp', None), rep_vec)
    out_specs = (act_spec, act_spec, part_vec, part_vec, P('dp', None, 'tp', None), P('dp', 'tp', None),
                 P(('dp', 'tp'), None, None), part_vec, part_vec, part_vec, P('dp', 'tp'), P(('dp', 'tp')),
                 P(('dp', 'tp'), None), part_vec)

    def device_step(x_in, grad_y, pad_mask, ln1_gain, ln1_bias, w_qkv, b_qkv, w_out, b_out, ln2_gain, ln2_bias, w_up, b_up, w_down, b_down):
        seq_len = pad_mask.shape[1]
        head_dim = w_qkv.shape[3]
        q_scale = head_dim ** -0.5
        cos_tab, sin_tab = rope_tables(seq_len, head_dim)
        key_ok = (pad_mask > 0)[:, None, None, :]
        x_f = x_in.astype(jnp.float32)
        h1_f, x_hat1, inv_std1 = layer_norm(x_f, ln1_gain, ln1_bias)
        h1_full = lax.all_gather(h1_f.astype(jnp.bfloat16), 'tp', axis=1, tiled=True)
        qkv_all = jnp.einsum('bsd,idhk->ibshk', h1_full, w_qkv, preferred_element_type=jnp.float32) + b_qkv[:, None, None]
        q_rot = rotate(qkv_all[0] * q_scale, cos_tab, sin_tab).astype(jnp.bfloat16)
        k_rot = rotate(qkv_all[1], cos_tab, sin_tab).astype(jnp.bfloat16)
        v_heads = qkv_all[2].astype(jnp.bfloat16)
        scores = jnp.einsum('bqhk,bshk->bhqs', q_rot, k_rot, preferred_element_type=jnp.float32)
        attn_probs = jax.nn.softmax(jnp.where(key_ok, scores, NEG_LARGE), axis=-1)
        probs_low = attn_probs.astype(jnp.bfloat16)
        attn_o = jnp.einsum('bhqs,bshk->bqhk', probs_low, v_heads, preferred_element_type=jnp.float32).astype(jnp.bfloat16)
        attn_part = jnp.einsum('cril,ile->cre', attn_o, w_out, preferred_element_type=jnp.float32)
        attn_sum = lax.psum_scatter(attn_part, 'tp', scatter_dimension=1, tiled=True)
        x1_f = (x_f + (attn_sum + b_out)).astype(jnp.bfloat16).astype(jnp.float32)
        h2_f, x_hat2, inv_std2 = layer_norm(x1_f, ln2_gain, ln2_bias)
        h2_full = lax.all_gather(h2_f.astype(jnp.bfloat16), 'tp', axis=1, tiled=True)
        pre_act = jnp.einsum('bsd,df->bsf', h2_full, w_up, preferred_element_type=jnp.float32) + b_up
        erf_term = lax.erf(pre_act * INV_SQRT2)
        act_b = (0.5 * pre_act * (1.0 + erf_term)).astype(jnp.bfloat16)
        gelu_slope = 0.5 * (1.0 + erf_term) + pre_act * jnp.exp(-0.5 * pre_act * pre_act) * INV_SQRT_2PI
        mlp_part = jnp.einsum('bsf,fd->bsd', act_b, w_down, preferred_element_type=jnp.float32)
        mlp_sum = lax.psum_scatter(mlp_part, 'tp', scatter_dimension=1, tiled=True)
        y_out = (x1_f + (mlp_sum + b_down)).astype(jnp.bfloat16)
        dy_full = lax.all_gather(grad_y, 'tp', axis=1, tiled=True)
        dy_f = grad_y.astype(jnp.float32)
        grad_w_down = jnp.einsum('bsf,bsd->fd', act_b, dy_full, preferred_element_type=jnp.float32)
        d_act = jnp.einsum('bsd,fd->bsf', dy_full, w_down, preferred_element_type=jnp.float32)
        d_pre = d_act * gelu_slope
        grad_b_up = jnp.sum(d_pre, axis=(0, 1))
        d_pre_b = d_pre.astype(jnp.bfloat16)
        grad_w_up = jnp.einsum('bsd,bsf->df', h2_full, d_pre_b, preferred_element_type=jnp.float32)
        d_h2_part = jnp.einsum('bsf,df->bsd', d_pre_b, w_up, preferred_element_type=jnp.float32)
        d_h2 = lax.psum_scatter(d_h2_part, 'tp', scatter_dimension=1, tiled=True)
        d_x1 = dy_f + layer_norm_grad(d_h2, x_hat2, inv_std2, ln2_gain)
        mid_sums = lax.psum(jnp.stack([jnp.sum(dy_f, axis=(0, 1)), jnp.sum(d_h2 * x_hat2, axis=(0, 1)),
                                       jnp.sum(d_h2, axis=(0, 1)), jnp.sum(d_x1, axis=(0, 1))]), 'tp')
        d_x1_full = lax.all_gather(d_x1.astype(jnp.bfloat16), 'tp', axis=1, tiled=True)
        grad_w_out = jnp.einsum('bshk,bsd->hkd', attn_o, d_x1_full, preferred_element_type=jnp.float32)
        d_attn_o = jnp.einsum('bsd,hkd->bshk', d_x1_full, w_out, preferred_element_type=jnp.float32).astype(jnp.bfloat16)
        d_value = jnp.einsum('bhqs,bqhk->bshk', probs_low, d_attn_o, preferred_element_type=jnp.float32)
        d_probs = jnp.einsum('bqhk,bshk->bhqs', d_attn_o, v_heads, preferred_element_type=jnp.float32)
        d_scores = (attn_probs * (d_probs - jnp.sum(d_probs * attn_probs, axis=-1, keepdims=True))).astype(jnp.bfloat16)
        d_query = jnp.einsum('bhqs,bshk->bqhk', d_scores, k_rot, preferred_element_type=jnp.float32)
        d_key = jnp.einsum('bhqs,bqhk->bshk', d_scores, q_rot, preferred_element_type=jnp.float32)
        d_qkv = jnp.stack([rotate_back(d_query, cos_tab, sin_tab) * q_scale, rotate_back(d_key, cos_tab, sin_tab), d_value])
        grad_b_qkv = jnp.sum(d_qkv, axis=(1, 2))
        d_qkv_b = d_qkv.astype(jnp.bfloat16)
        grad_w_qkv = jnp.einsum('bsd,ibshk->idhk', h1_full, d_qkv_b, preferred_element_type=jnp.float32)
        d_h1_part = jnp.einsum('ibshk,idhk->bsd', d_qkv_b, w_qkv, preferred_element_type=jnp.float32)
        d_h1 = lax.psum_scatter(d_h1_part, 'tp', scatter_dimension=1, tiled=True)
        ln1_sums = lax.psum(jnp.stack([jnp.sum(d_h1 * x_hat1, axis=(0, 1)), jnp.sum(d_h1, axis=(0, 1))]), 'tp')
        grad_x = (d_x1 + layer_norm_grad(d_h1, x_hat1, inv_std1, ln1_gain)).astype(jnp.bfloat16)
        return (y_out, grad_x, ln1_sums[0], ln1_sums[1], grad_w_qkv, grad_b_qkv, grad_w_out, mid_sums[3],
                mid_sums[1], mid_sums[2], grad_w_up, grad_b_up, grad_w_down, mid_sums[0])

    return jax.shard_map(device_step, mesh=mesh, in_specs=in_specs, out_specs=out_specs, check_vma=False)
```

profile of v0, /device:TPU:0, one launch (start us, length us, event | category | flops | bytes accessed | tf_op | source)
XLA Modules:
  0.0 2721.6 jit_solution(17835847716153234272)
XLA Ops:
  7.3 2.9 convert_reduce_fusion.1
  10.3 3.1 fusion.54
  14.0 3.0 fusion.47
  17.8 157.5 %all-gather.5.cloned.1.call-done = bf16[32,512,1024]{2,1,0:T(8,128)(2,1)} async-done(((bf16[32,64,1024]{2,1,0:T(8,128)(2,1)}), bf16[32,512,1024]{2,1,0:T(8,128)(2,1)}) %all-gather.5.cloned.1.call-update) | async-done | bytes 33554448 | tf_op jit(solution)/shard_map/all_gather | solution.py:64
  175.2 47.3 %add_bitcast_fusion = f32[3,32,512,2,64]{2,4,3,0,1:T(8,128)} fusion(f32[3,2,64]{2,1,0:T(2,128)S(1)} %copy-done.39, bf16[32,512,1024]{2,1,0:T(8,128)(2,1)} %all-gather.5.cloned.1.call-done, bf16[3,1024,2,64]{1,3,2,0:T(8,128)(2,1)S(1)} %copy-done.37), kind=kOutput, calls=%fused_computation.28 | convolution fusion | flops 12891193344 | bytes 59508224 | tf_op jit(solution)/shard_map/bsd,idhk->ibshk/dot_general | solution.py:65
  222.5 4.4 fusion.68
  227.0 4.5 slice_bitcast_fusion
  231.4 6.4 slice_negate_fusion.2
  237.8 17.3 fusion.60
  255.1 31.5 %fusion.118 = (f32[32,2,512]{2,1,0:T(2,128)S(1)}, f32[32,2,512,512]{2,3,1,0:T(8,128)}) fusion(pred[32,512]{1,0:T(8,128)(4,1)S(1)} %broadcast_compare_fusion, bf16[32,512,2,64]{1,3,2,0:T(8,128)(2,1)} %get-tuple-element.29, bf16[32,512,2,64]{1,3,2,0:T(8,128)(2,1)} %get-tuple-element.28), kind=kOutput, calls=%fused_computation.147 | convolution fusion | flops 2197815808 | bytes 75644928 | tf_op jit(solution)/shard_map/sub | solution.py:70
  286.6 26.5 fusion.77
  313.1 25.3 convolution_bitcast_fusion
  338.7 374.6 %reduce-scatter.5.cloned.1.call-done = f32[32,64,1024]{2,1,0:T(8,128)} async-done(((f32[32,512,1024]{2,1,0:T(8,128)}), f32[32,64,1024]{2,1,0:T(8,128)}) %reduce-scatter.5.cloned.1.call-update) | async-done | bytes 8388624 | tf_op jit(solution)/shard_map/reduce_scatter | solution.py:74
  713.3 5.9 convert_reduce_fusion
  719.2 1.4 fusion.45
  721.8 3.0 fusion.40
  725.4 154.7 %all-gather.7.cloned.1.call-done = bf16[32,512,1024]{2,1,0:T(8,128)(2,1)} async-done(((bf16[32,64,1024]{2,1,0:T(8,128)(2,1)}), bf16[32,512,1024]{2,1,0:T(8,128)(2,1)}) %all-gather.7.cloned.1.call-update) | async-done | bytes 33554448 | tf_op jit(solution)/shard_map/all_gather | solution.py:77
  880.2 35.2 %multiply_convert_fusion.1 = (bf16[32,512,512]{2,1,0:T(8,128)(2,1)}, f32[32,512,512]{2,1,0:T(8,128)}) fusion(f32[512]{0:T(512)S(1)} %copy-done.40, bf16[32,512,1024]{2,1,0:T(8,128)(2,1)} %all-gather.7.cloned.1.call-done, bf16[1024,512]{1,0:T(8,128)(2,1)S(1)} %copy-done), kind=kOutput, calls=%fused_computation.20 | convolution fusion | flops 17230200832 | bytes 84936704 | tf_op jit(solution)/shard_map/bsd,df->bsf/dot_general | solution.py:78
  915.4 121.8 %all-gather.9.cloned.1.call-done = bf16[32,512,1024]{2,1,0:T(8,128)(2,1)} async-done(((bf16[32,64,1024]{2,1,0:T(8,128)(2,1)}), bf16[32,512,1024]{2,1,0:T(8,128)(2,1)}) %all-gather.9.cloned.1.call-update) | async-done | bytes 33554448 | tf_op jit(solution)/shard_map/all_gather | solution.py:85
  1037.1 39.1 %fusion.119 = (f32[512]{0:T(512)}, bf16[32,512,512]{2,1,0:T(8,128)(2,1)}) fusion(f32[32,512,512]{2,1,0:T(8,128)} %get-tuple-element.56, f32[512]{0:T(512)S(1)} %copy-done.40, bf16[32,512,1024]{2,1,0:T(8,128)(2,1)} %all-gather.9.cloned.1.call-done, bf16[512,1024]{1,0:T(8,128)(2,1)S(1)} %copy-done.36), kind=kOutput, calls=%fused_computation.148 | convolution fusion | flops 17280532480 | bytes 84938752 | tf_op jit(solution)/shard_map/bsd,fd->bsf/dot_general | solution.py:88
  1076.2 31.7 %fusion.66 = f32[32,512,1024]{2,1,0:T(8,128)} fusion(bf16[32,512,512]{2,1,0:T(8,128)(2,1)} %get-tuple-element.61, bf16[1024,512]{1,0:T(8,128)(2,1)S(1)} %copy-done), kind=kOutput, calls=%fused_computation.94 | convolution fusion | flops 17179869184 | bytes 84934656 | tf_op jit(solution)/shard_map/bsf,df->bsd/dot_general | solution.py:93
  1108.0 31.5 %fusion.98 = f32[32,512,1024]{2,1,0:T(8,128)} fusion(bf16[32,512,512]{2,1,0:T(8,128)(2,1)} %get-tuple-element.55, bf16[512,1024]{1,0:T(8,128)(2,1)S(1)} %copy-done.36), kind=kOutput, calls=%fused_computation.115 | convolution fusion | flops 17179869184 | bytes 84934656 | tf_op jit(solution)/shard_map/bsf,fd->bsd/dot_general | solution.py:82
  1139.6 343.2 %reduce-scatter.9.cloned.1.call-done = f32[32,64,1024]{2,1,0:T(8,128)} async-done(((f32[32,512,1024]{2,1,0:T(8,128)}), f32[32,64,1024]{2,1,0:T(8,128)}) %reduce-scatter.9.cloned.1.call-update) | async-done | bytes 8388624 | tf_op jit(solution)/shard_map/reduce_scatter | solution.py:94
  1482.8 7.8 fusion.44
  1490.5 370.3 %reduce-scatter.7.cloned.1.call-done = f32[32,64,1024]{2,1,0:T(8,128)} async-done(((f32[32,512,1024]{2,1,0:T(8,128)}), f32[32,64,1024]{2,1,0:T(8,128)}) %reduce-scatter.7.cloned.1.call-update) | async-done | bytes 8388624 | tf_op jit(solution)/shard_map/reduce_scatter | solution.py:83
  1860.9 13.2 fusion.112
  1874.0 3.3 copy-done.4
  1877.3 2.6 convert_element_type.76
  1880.0 155.3 %all-gather.11.cloned.1.call-done = bf16[32,512,1024]{2,1,0:T(8,128)(2,1)} async-done(((bf16[32,64,1024]{2,1,0:T(8,128)(2,1)}), bf16[32,512,1024]{2,1,0:T(8,128)(2,1)}) %all-gather.11.cloned.1.call-update) | async-done | bytes 33554448 | tf_op jit(solution)/shard_map/all_gather | solution.py:98
  2035.4 23.7 fusion.80
  2059.1 28.1 %fusion.74 = f32[1,32,512,2,64]{2,4,3,1,0:T(8,128)} fusion(bf16[32,512,2,64]{1,3,2,0:T(8,128)(2,1)} %fusion.80, f32[32,2,512,512]{2,3,1,0:T(8,128)} %get-tuple-element.54, f32[32,2,512]{2,1,0:T(2,128)S(1)} %copy-done.22), kind=kOutput, calls=%fused_computation.106 | convolution fusion | flops 2181038080 | bytes 79822848 | tf_op jit(solution)/shard_map/bhqs,bqhk->bshk/dot_general | solution.py:101
  2087.2 47.8 %multiply_reduce_fusion = (f32[32,2,512]{2,1,0:T(2,128)S(1)}, f32[32,2,512,512]{2,3,1,0:T(8,128)}) fusion(f32[32,2,512,512]{2,3,1,0:T(8,128)} %get-tuple-element.54, f32[32,2,512]{2,1,0:T(2,128)S(1)} %copy-done.22, bf16[32,512,2,64]{1,3,2,0:T(8,128)(2,1)} %fusion.80, f32[3,32,512,2,64]{2,4,3,0,1:T(8,128)} %add_bitcast_fusion), kind=kOutput, calls=%fused_computation.2 | convolution fusion | flops 2197782528 | bytes 142868480 | tf_op jit(solution)/shard_map/bqhk,bshk->bhqs/dot_general | solution.py:102
  2135.0 52.6 %multiply_convert_fusion = bf16[32,2,512,512]{2,3,1,0:T(8,128)(2,1)} fusion(f32[32,2,512,512]{2,3,1,0:T(8,128)} %get-tuple-element.58, f32[32,2,512]{2,1,0:T(2,128)S(1)} %get-tuple-element.57, f32[32,2,512,512]{2,3,1,0:T(8,128)} %get-tuple-element.54, f32[32,2,512]{2,1,0:T(2,128)S(1)} %copy-done.22), kind=kLoop, calls=%fused_computation.1 | loop fusion | flops 67108864 | bytes 168034304 | tf_op jit(solution)/shard_map/convert_element_type | solution.py:103
  2187.5 19.8 fusion.120
  2207.4 24.9 bitcast_multiply_fusion.2
  2232.3 8.8 fusion.114
  2241.1 4.3 fusion.115
  2245.4 19.5 fusion.62
  2264.9 33.8 %convolution_bitcast_fusion.1 = f32[32,512,1024]{2,1,0:T(8,128)} fusion(bf16[3,1024,2,64]{1,3,2,0:T(8,128)(2,1)S(1)} %copy-done.38, f32[1,32,512,2,64]{2,4,3,1,0:T(8,128)} %fusion.74, f32[1,32,512,2,64]{2,4,3,1,0:T(8,128)} %get-tuple-element.41, f32[1,32,512,2,64]{2,4,3,1,0:T(8,128)} %get-tuple-element.40), kind=kOutput, calls=%fused_computation.26 | convolution fusion | flops 12897484800 | bytes 93061120 | tf_op jit(solution)/shard_map/ibshk,idhk->bsd/dot_general | solution.py:110
  2298.6 27.2 convolution_bitcast_fusion.2
  2325.9 27.6 %fusion.83 = f32[1024,512]{1,0:T(8,128)} fusion(bf16[32,512,1024]{2,1,0:T(8,128)(2,1)} %all-gather.7.cloned.1.call-done, bf16[32,512,512]{2,1,0:T(8,128)(2,1)} %get-tuple-element.61), kind=kOutput, calls=%fused_computation.109 | convolution fusion | flops 17179869184 | bytes 52428800 | tf_op jit(solution)/shard_map/bsd,bsf->df/dot_general | solution.py:92
  2353.6 9.9 fusion.19
  2363.5 13.9 fusion.92
  2377.3 24.0 fusion.89
  2401.3 272.2 %reduce-scatter.11.cloned.1.call-done = f32[32,64,1024]{2,1,0:T(8,128)} async-done(((f32[32,512,1024]{2,1,0:T(8,128)}), f32[32,64,1024]{2,1,0:T(8,128)}) %reduce-scatter.11.cloned.1.call-update) | async-done | bytes 8388624 | tf_op jit(solution)/shard_map/reduce_scatter | solution.py:111
  2673.5 6.8 fusion.53
  2680.3 22.5 all-reduce
  2704.1 10.5 fusion.52
  (113 shorter events, 5.0 us)
Async XLA Ops:
  7.2 873.0 %copy-start = (bf16[1024,512]{1,0:T(8,128)(2,1)S(1)}, bf16[1024,512]{1,0:T(8,128)(2,1)}, u32[]{:S(2)}) copy-start(bf16[1024,512]{1,0:T(8,128)(2,1)} %param.26) | copy-start | bytes 3145732
  7.2 6.8 copy-start.26
  7.2 6.8 copy-start.32
  7.2 168.0 %all-gather.5.cloned.1.call-start = ((), (), s32[]{:S(2)}) async-start(), calls=%async_computation.4 | async-start | bytes 37748736 | tf_op jit(solution)/shard_map/all_gather | solution.py:64
  7.3 6.7 copy-start.2
  10.2 3.1 copy-start.13
  10.2 7.5 copy-start.23
  10.3 165.0 %copy-start.37 = (bf16[3,1024,2,64]{1,3,2,0:T(8,128)(2,1)S(1)}, bf16[3,1024,2,64]{1,3,2,0:T(8,128)(2,1)}, u32[]{:S(2)}) copy-start(bf16[3,1024,2,64]{1,3,2,0:T(8,128)(2,1)} %param.20) | copy-start | bytes 2359300
  10.3 165.0 %copy-start.39 = (f32[3,2,64]{2,1,0:T(2,128)S(1)}, f32[3,2,64]{2,1,0:T(2,128)}, u32[]{:S(2)}) copy-start(f32[3,2,64]{2,1,0:T(2,128)} %param.21) | copy-start | bytes 4612
  17.0 696.3 %reduce-scatter.5.cloned.1.call-start = ((), (), s32[]{:S(2)}) async-start(), calls=%async_computation.5 | async-start | bytes 75497472 | tf_op jit(solution)/shard_map/reduce_scatter | solution.py:74
  17.7 220.1 %copy-start.7 = (f32[512,64]{0,1:T(8,128)}, f32[512,64]{0,1:T(8,128)S(1)}, u32[]{:S(2)}) copy-start(f32[512,64]{0,1:T(8,128)S(1)} %get-tuple-element.46) | copy-start | bytes 393220
  17.7 220.1 %copy-start.9 = (f32[512,64]{0,1:T(8,128)}, f32[512,64]{0,1:T(8,128)S(1)}, u32[]{:S(2)}) copy-start(f32[512,64]{0,1:T(8,128)S(1)} %get-tuple-element.44) | copy-start | bytes 393220
  286.6 26.5 copy-start.21
  286.6 26.5 copy-start.15
  338.5 374.9 %copy-start.35 = (f32[1024]{0:T(1024)S(1)}, f32[1024]{0:T(1024)}, u32[]{:S(2)}) copy-start(f32[1024]{0:T(1024)} %param.23) | copy-start | bytes 12292
  338.5 383.3 %copy-start.24 = (f32[1024]{0:T(1024)S(1)}, f32[1024]{0:T(1024)}, u32[]{:S(2)}) copy-start(f32[1024]{0:T(1024)} %param.24) | copy-start | bytes 12292
  338.5 383.3 %copy-start.33 = (f32[1024]{0:T(1024)S(1)}, f32[1024]{0:T(1024)}, u32[]{:S(2)}) copy-start(f32[1024]{0:T(1024)} %param.25) | copy-start | bytes 12292
  338.5 541.7 %all-gather.7.cloned.1.call-start = ((), (), s32[]{:S(2)}) async-start(), calls=%async_computation.6 | async-start | bytes 37748736 | tf_op jit(solution)/shard_map/all_gather | solution.py:77
  719.2 2.0 copy-start.3
  719.2 1.9 copy-start.11
  721.2 0.6 copy-start.17
  721.8 158.4 %copy-start.40 = (f32[512]{0:T(512)S(1)}, f32[512]{0:T(512)}, u32[]{:S(2)}) copy-start(f32[512]{0:T(512)} %param.27) | copy-start | bytes 6148
  724.8 312.3 %all-gather.9.cloned.1.call-start = ((), (), s32[]{:S(2)}) async-start(), calls=%async_computation.8 | async-start | bytes 37748736 | tf_op jit(solution)/shard_map/all_gather | solution.py:85
  725.4 311.7 %copy-start.36 = (bf16[512,1024]{1,0:T(8,128)(2,1)S(1)}, bf16[512,1024]{1,0:T(8,128)(2,1)}, u32[]{:S(2)}) copy-start(bf16[512,1024]{1,0:T(8,128)(2,1)} %param.28) | copy-start | bytes 3145732
  725.4 757.4 %reduce-scatter.9.cloned.1.call-start = ((), (), s32[]{:S(2)}) async-start(), calls=%async_computation.9 | async-start | bytes 75497472 | tf_op jit(solution)/shard_map/reduce_scatter | solution.py:94
  1107.9 753.0 %reduce-scatter.7.cloned.1.call-start = ((), (), s32[]{:S(2)}) async-start(), calls=%async_computation.7 | async-start | bytes 75497472 | tf_op jit(solution)/shard_map/reduce_scatter | solution.py:83
  1139.5 343.3 %copy-start.12 = (f32[32,64]{1,0:T(8,128)S(1)}, f32[32,64]{1,0:T(8,128)}, u32[]{:S(2)}) copy-start(f32[32,64]{1,0:T(8,128)} %copy-done.11) | copy-start | bytes 24580
  1139.5 343.3 %copy-start.18 = (f32[32,64]{1,0:T(8,128)S(1)}, f32[32,64]{1,0:T(8,128)}, u32[]{:S(2)}) copy-start(f32[32,64]{1,0:T(8,128)} %copy-done.17) | copy-start | bytes 24580
  1139.5 343.3 %copy-start.25 = (f32[1024]{0:T(1024)S(1)}, f32[1024]{0:T(1024)}, u32[]{:S(2)}) copy-start(f32[1024]{0:T(1024)} %param.24) | copy-start | bytes 12292
  1139.5 721.4 %copy-start.34 = (f32[1024]{0:T(1024)S(1)}, f32[1024]{0:T(1024)}, u32[]{:S(2)}) copy-start(f32[1024]{0:T(1024)} %param.29) | copy-start | bytes 12292
  1139.5 895.9 %all-gather.11.cloned.1.call-start = ((), (), s32[]{:S(2)}) async-start(), calls=%async_computation.10 | async-start | bytes 37748736 | tf_op jit(solution)/shard_map/all_gather | solution.py:98
  1874.0 3.3 copy-start.4
  1877.3 158.0 %copy-start.16 = (bf16[2,64,1024]{2,1,0:T(8,128)(2,1)S(1)}, bf16[2,64,1024]{2,1,0:T(8,128)(2,1)}, u32[]{:S(2)}) copy-start(bf16[2,64,1024]{2,1,0:T(8,128)(2,1)} %param.22) | copy-start | bytes 786436
  1880.0 179.1 %copy-start.22 = (f32[32,2,512]{2,1,0:T(2,128)S(1)}, f32[32,2,512]{2,1,0:T(2,128)}, u32[]{:S(2)}) copy-start(f32[32,2,512]{2,1,0:T(2,128)} %copy-done.21) | copy-start | bytes 393220
  1880.0 793.5 %reduce-scatter.11.cloned.1.call-start = ((), (), s32[]{:S(2)}) async-start(), calls=%async_computation.11 | async-start | bytes 75497472 | tf_op jit(solution)/shard_map/reduce_scatter | solution.py:111
  2187.5 19.8 copy-start.8
  2232.3 8.8 copy-start.5
  2241.1 4.3 copy-start.10
  2245.4 19.5 copy-start.38
  2325.8 27.6 %copy-start.28 = (f32[1024]{0:T(1024)S(1)}, f32[1024]{0:T(1024)}, u32[]{:S(2)}) copy-start(f32[1024]{0:T(1024)} %get-tuple-element.14) | copy-start | bytes 12292
  2325.8 27.6 %copy-start.29 = (f32[1024]{0:T(1024)S(1)}, f32[1024]{0:T(1024)}, u32[]{:S(2)}) copy-start(f32[1024]{0:T(1024)} %get-tuple-element.20) | copy-start | bytes 12292
  2325.8 27.6 %copy-start.30 = (f32[1024]{0:T(1024)S(1)}, f32[1024]{0:T(1024)}, u32[]{:S(2)}) copy-start(f32[1024]{0:T(1024)} %get-tuple-element.24) | copy-start | bytes 12292
  2325.9 27.6 %copy-start.31 = (f32[1024]{0:T(1024)S(1)}, f32[1024]{0:T(1024)}, u32[]{:S(2)}) copy-start(f32[1024]{0:T(1024)} %get-tuple-element.38) | copy-start | bytes 12292
  2353.5 9.9 copy-start.6
  2377.3 296.2 %copy-start.14 = (f32[32,64]{1,0:T(8,128)S(1)}, f32[32,64]{1,0:T(8,128)}, u32[]{:S(2)}) copy-start(f32[32,64]{1,0:T(8,128)} %copy-done.13) | copy-start | bytes 24580
  2377.3 296.2 %copy-start.20 = (f32[32,64]{1,0:T(8,128)S(1)}, f32[32,64]{1,0:T(8,128)}, u32[]{:S(2)}) copy-start(f32[32,64]{1,0:T(8,128)} %copy-done.19) | copy-start | bytes 24580
  2377.3 296.2 %copy-start.27 = (f32[1024]{0:T(1024)S(1)}, f32[1024]{0:T(1024)}, u32[]{:S(2)}) copy-start(f32[1024]{0:T(1024)} %param.18) | copy-start | bytes 12292
  2703.5 11.1 copy-start.1
  (1 other events, 0.6 us)
Sparse Core Ops, SparseCore 0:
  17.1 158.0 all-gather.4
  338.6 374.6 reduce-scatter.4
  724.9 155.2 all-gather.6
  881.9 155.2 all-gather.8
  1108.0 374.6 reduce-scatter.8
  1486.1 374.6 reduce-scatter.6
  1880.1 155.1 all-gather.10
  2298.8 374.6 reduce-scatter.10
where the time goes:
time: 2720 us
  waiting for transfers between devices  1950 us (72%)
  matrix products  539 us (20%)
  other arithmetic  184 us (7%)
    reduce_scatter x1, waiting for transfers between devices, device_step(): lax.psum_scatter(attn_part, 'tp', scatter_dimension=1, tiled=True)  375 us
    reduce_scatter x1, waiting for transfers between devices, device_step(): mlp_sum = lax.psum_scatter(mlp_part, 'tp', scatter_dimension=1, tiled=True)  370 us
    reduce_scatter x1, waiting for transfers between devices, device_step(): d_h2 = lax.psum_scatter(d_h2_part, 'tp', scatter_dimension=1, tiled=True)  343 us
    reduce_scatter x1, waiting for transfers between devices, device_step(): d_h1 = lax.psum_scatter(d_h1_part, 'tp', scatter_dimension=1, tiled=True)  272 us
    all_gather x1, waiting for transfers between devices, device_step(): lax.all_gather(h1_f.astype(jnp.bfloat16), 'tp', axis=1, tiled=True)  157 us
    all_gather x1, waiting for transfers between devices, device_step(): lax.all_gather(d_x1.astype(jnp.bfloat16), 'tp', axis=1, tiled=True)  155 us
    all_gather x1, waiting for transfers between devices, device_step(): lax.all_gather(h2_f.astype(jnp.bfloat16), 'tp', axis=1, tiled=True)  155 us
    all_gather x1, waiting for transfers between devices, device_step(): dy_full = lax.all_gather(grad_y, 'tp', axis=1, tiled=True)  122 us
  transfers between devices with their start and end apart: 8, of which 8 were waited for; matrix products, arithmetic and copies ran while one was open for 7% of the time, Pallas kernels for 0%

commit v1 on v0

v1 whole, which is shorter than its diff:
```python
import functools

import jax
import jax.numpy as jnp
from jax import lax
from jax.experimental import pallas as pl
from jax.experimental.pallas import tpu as pltpu
from jax.sharding import PartitionSpec as P

f32 = jnp.float32
bf16 = jnp.bfloat16
LN_EPS = 1e-5
ROPE_BASE = 10000.0
INV_SQRT2 = 0.7071067811865476
INV_SQRT_2PI = 0.3989422804014327
NEG_LARGE = -1e30
MESH = pl.DeviceIdType.MESH
ANY = pl.BlockSpec(memory_space=pl.ANY)
VMEM_LIMIT = 66_000_000

TP = 8
NS = 4
S = 512
D = 1024
PW = 128
HD = 64
HH = HD // 2
FB = 512
SL = 64
QS = HD ** -0.5
R3 = 3 * PW


def dg(a, b, ca, cb):
    return lax.dot_general(a, b, (((ca,), (cb,)), ((), ())), preferred_element_type=f32)


def sds(shape, dtype):
    return jax.ShapeDtypeStruct(shape, dtype)


class Place:
    def __init__(self):
        me = lax.axis_index("tp")
        self.me = me
        self.c = lax.rem(me, 2)
        self.dc = 1 - 2 * self.c
        self.dx = 2 - 4 * lax.rem(lax.div(me, 2), 2)
        self.dy = 4 - 8 * lax.div(me, 4)
        self.partner = me + self.dc
        self.a = me + (1 - self.c) * self.dx + self.c * self.dy
        self.b = me + (1 - self.c) * self.dy + self.c * self.dx

    def peer(self, m):
        return self.me + (m & 1) * self.dc + ((m >> 1) & 1) * self.dx + (m >> 2) * self.dy

    def slot_of(self, m):
        k = self.c if m % 2 == 0 else 1 - self.c
        lo, hi = {0: (6, 7), 1: (0, 5), 2: (4, 1), 3: (2, 3)}[m >> 1]
        return lo + k * (hi - lo)


def remote(src, dst, send_sem, recv_sem, device):
    return pltpu.make_async_remote_copy(src_ref=src, dst_ref=dst, send_sem=send_sem, recv_sem=recv_sem,
                                        device_id={"tp": device}, device_id_type=MESH)


def wait_for(ref, sem):
    pltpu.make_async_copy(ref, ref, sem).wait()


def entry_barrier(pc):
    bar = pltpu.get_barrier_semaphore()
    for m in range(1, TP):
        pl.semaphore_signal(bar, inc=1, device_id={"tp": pc.peer(m)}, device_id_type=MESH)
    pl.semaphore_wait(bar, TP - 1)


class AllToAll:
    def __init__(self, pc, pos_ref, seq_ref, send_sem, recv_sem, inward):
        self.pc, self.pos, self.seq, self.ss, self.rs, self.inward = pc, pos_ref, seq_ref, send_sem, recv_sem, inward

    def _rows(self, dev):
        return pl.ds(pl.multiple_of(dev * SL, SL), SL)

    def _seqs(self, dev):
        return pl.ds(dev * NS, NS)

    def _copy(self, m):
        pc, dev = self.pc, self.pc.peer(m)
        if self.inward:
            src, dst = self.pos.at[self._seqs(dev)], self.seq.at[:, self._rows(pc.me)]
        else:
            src, dst = self.seq.at[:, self._rows(dev)], self.pos.at[self._seqs(pc.me)]
        return remote(src, dst, self.ss.at[m], self.rs.at[m], dev)

    def start(self):
        for m in (6, 7, 2, 3, 4, 5, 1):
            self._copy(m).start()

    def local(self, buf):
        pc = self.pc
        a, b = self.pos.at[self._seqs(pc.me)], self.seq.at[:, self._rows(pc.me)]
        src, dst = (a, b) if self.inward else (b, a)
        return pltpu.make_async_copy(src, buf, self.ss.at[0]), pltpu.make_async_copy(buf, dst, self.rs.at[0])

    def finish(self):
        for m in range(1, TP):
            self._copy(m).wait()


class Gather:
    def __init__(self, pc, src_ref, dst_ref, send_sem, recv_sem):
        self.pc, self.src, self.dst, self.ss, self.rs = pc, src_ref, dst_ref, send_sem, recv_sem

    def _send(self, i, src, slot, dev):
        return remote(src, self.dst.at[slot], self.ss.at[i], self.rs.at[slot], dev)

    def _direct(self):
        pc, c = self.pc, self.pc.c
        return [self._send(0, self.src, c, pc.a), self._send(1, self.src, 4 + c, pc.b),
                self._send(2, self.src, 6 + c, pc.partner)]

    def _hop(self):
        pc, c = self.pc, self.pc.c
        return [self._send(3, self.dst.at[c], 2 + c, pc.b), self._send(4, self.dst.at[c], c, pc.partner),
                self._send(5, self.dst.at[4 + c], 4 + c, pc.partner)]

    def _last(self):
        pc, c = self.pc, self.pc.c
        return self._send(6, self.dst.at[2 + c], 2 + c, pc.partner)

    def start(self):
        for cp in self._direct():
            cp.start()

    def forward(self):
        c = self.pc.c
        hop = self._hop()
        wait_for(self.dst.at[c], self.rs.at[c])
        hop[0].start()
        hop[1].start()
        wait_for(self.dst.at[4 + c], self.rs.at[4 + c])
        hop[2].start()

    def last(self):
        c = self.pc.c
        wait_for(self.dst.at[2 + c], self.rs.at[2 + c])
        self._last().start()

    def local(self, buf):
        c = self.pc.c
        return (pltpu.make_async_copy(self.src, buf, self.ss.at[7]),
                pltpu.make_async_copy(buf, self.dst.at[6 + c], self.rs.at[6 + c]))

    def finish(self):
        o = 1 - self.pc.c
        for j in range(4):
            wait_for(self.dst.at[2 * j + o], self.rs.at[2 * j + o])
        for cp in self._direct() + self._hop() + [self._last()]:
            cp.wait_send()


def row_add(acc, others):
    rows = acc.shape[0]
    step = 64

    def body(i, carry):
        r = pl.ds(pl.multiple_of(i * step, step), step)
        v = acc[r, :]
        for o in others:
            v = v + o[r, :]
        acc[r, :] = v
        return carry

    lax.fori_loop(0, rows // step, body, 0)


class ReduceScatter:
    def __init__(self, pc, part, r0, r1, r2, stage, out, sems, bufs, buf_sem):
        self.pc, self.part, self.r0, self.r1, self.r2, self.stage, self.out = pc, part, r0, r1, r2, stage, out
        self.ss, self.rs = sems
        self.rows = part.shape[1]
        self.bufs, self.bs = bufs, buf_sem

    def _pair(self, j):
        pc = self.pc
        return remote(self.part.at[2 * j + 1 - pc.c], self.r0.at[j], self.ss.at[j], self.rs.at[j], pc.partner)

    def _first(self, j):
        pc = self.pc
        return remote(self.stage.at[j], self.r1.at[j], self.ss.at[4 + j], self.rs.at[4 + j], pc.a)

    def _second(self):
        pc = self.pc
        return remote(self.stage.at[2], self.r2, self.ss.at[6], self.rs.at[6], pc.b)

    def start(self):
        for j in range(4):
            self._pair(j).start()

    def _sum(self, j, srcs, dst):
        bufs = [b.at[pl.ds(0, self.rows)] for b in self.bufs[:len(srcs)]]
        cps = [pltpu.make_async_copy(s, b, self.bs.at[i]) for i, (s, b) in enumerate(zip(srcs, bufs))]
        for cp in cps:
            cp.start()
        for cp in cps:
            cp.wait()
        row_add(bufs[0], bufs[1:])
        out = pltpu.make_async_copy(bufs[0], dst, self.bs.at[0])
        out.start()
        out.wait()

    def first(self, j):
        c = self.pc.c
        wait_for(self.r0.at[j], self.rs.at[j])
        self._sum(j, [self.part.at[2 * j + c], self.r0.at[j]], self.stage.at[j])
        self._first(j).start()

    def second(self):
        c = self.pc.c
        wait_for(self.r0.at[2], self.rs.at[2])
        wait_for(self.r1.at[1], self.rs.at[5])
        self._sum(2, [self.part.at[4 + c], self.r0.at[2], self.r1.at[1]], self.stage.at[2])
        self._second().start()

    def last(self):
        c = self.pc.c
        wait_for(self.r0.at[3], self.rs.at[3])
        wait_for(self.r1.at[0], self.rs.at[4])
        wait_for(self.r2, self.rs.at[6])
        self._sum(3, [self.part.at[6 + c], self.r0.at[3], self.r1.at[0], self.r2], self.out)

    def finish(self):
        for j in range(4):
            self._pair(j).wait_send()
        for j in range(2):
            self._first(j).wait_send()
        self._second().wait_send()


def gather_kernel(x_ref, dy_ref, wq, wo, wu, wd, bs, xs_ref, dys_ref, wq_all, wo_all, wu_all, wd_all, bs_all,
                  act_buf, wbufs_q, wbufs_o, wbufs_u, wbufs_d, wbufs_b, a_ss, a_rs, g_ss, g_rs):
    pc = Place()
    entry_barrier(pc)
    a2a = [AllToAll(pc, p, s, a_ss.at[i], a_rs.at[i], True)
           for i, (p, s) in enumerate(((x_ref, xs_ref), (dy_ref, dys_ref)))]
    gathers = [Gather(pc, s, d, g_ss.at[i], g_rs.at[i])
               for i, (s, d) in enumerate(((bs, bs_all), (wq, wq_all), (wo, wo_all), (wu, wu_all), (wd, wd_all)))]
    for g in gathers[:3]:
        g.start()
    a2a[0].start()
    for g in gathers[3:]:
        g.start()
    a2a[1].start()
    local = [a2a[i].local(act_buf.at[i]) for i in range(2)]
    local += [g.local(b) for g, b in zip(gathers, (wbufs_b, wbufs_q, wbufs_o, wbufs_u, wbufs_d))]
    for load, _ in local:
        load.start()
    for load, store in local:
        load.wait()
        store.start()
    for g in gathers:
        g.forward()
    for g in gathers:
        g.last()
    for _, store in local:
        store.wait()
    for g in gathers:
        g.finish()
    for a in a2a:
        a.finish()


def gather_call(x_in, grad_y, wq, wo, wu, wd, bs):
    return pl.pallas_call(
        gather_kernel,
        in_specs=[ANY] * 7,
        out_specs=[ANY] * 7,
        out_shape=[sds((NS, S, D), bf16), sds((NS, S, D), bf16), sds((TP,) + wq.shape, bf16), sds((TP,) + wo.shape, bf16),
                   sds((TP,) + wu.shape, bf16), sds((TP,) + wd.shape, bf16), sds((TP,) + bs.shape, f32)],
        scratch_shapes=[pltpu.VMEM((2, NS, SL, D), bf16), pltpu.VMEM(wq.shape, bf16), pltpu.VMEM(wo.shape, bf16),
                        pltpu.VMEM(wu.shape, bf16), pltpu.VMEM(wd.shape, bf16), pltpu.VMEM(bs.shape, f32),
                        pltpu.SemaphoreType.DMA((2, 8)), pltpu.SemaphoreType.DMA((2, 8)),
                        pltpu.SemaphoreType.DMA((5, 8)), pltpu.SemaphoreType.DMA((5, 8))],
        compiler_params=pltpu.CompilerParams(collective_id=0, has_side_effects=True),
        name="gather_in",
    )(x_in, grad_y, wq, wo, wu, wd, bs)


def ln_stats(v):
    c = v - jnp.mean(v, axis=-1, keepdims=True)
    inv = lax.rsqrt(jnp.mean(c * c, axis=-1, keepdims=True) + LN_EPS)
    return c * inv, inv


def ln_grad(d_out, x_hat, inv, gain):
    dh = d_out * gain
    return inv * (dh - jnp.mean(dh, axis=-1, keepdims=True) - x_hat * jnp.mean(dh * x_hat, axis=-1, keepdims=True))


def masked_scores(q, k, ok):
    return jnp.where(ok, dg(k, q, 0, 0), NEG_LARGE)


def key_mask(mask_ref):
    return jnp.concatenate([mask_ref[0]] * (S // PW), axis=1) > 0


def attn_fwd_kernel(x_ref, mask_ref, cos_ref, sin_ref, g1_ref, b1_ref, wq_ref, bq_ref, wo_ref, bo_ref, g2_ref, b2_ref,
                    qkv_ref, m_ref, l_ref, o_ref, x1_ref, h2_ref, h1_s, o_s):
    g = pl.program_id(1)

    @pl.when(g == 0)
    def _():
        xh, _ = ln_stats(x_ref[0].astype(f32))
        h1_s[...] = (xh * g1_ref[...] + b1_ref[...]).astype(bf16)

    qkv = dg(wq_ref[g], h1_s[...], 1, 1) + bq_ref[g]
    cos, sin = cos_ref[...], sin_ref[...]
    ok = key_mask(mask_ref)

    def rot(t):
        a, b = t[:HH], t[HH:]
        return jnp.concatenate([a * cos - b * sin, b * cos + a * sin], axis=0).astype(bf16)

    for h in range(2):
        r = h * HD
        q = rot(qkv[r:r + HD] * QS)
        k = rot(qkv[PW + r:PW + r + HD])
        v = qkv[2 * PW + r:2 * PW + r + HD].astype(bf16)
        qkv_ref[0, 0, r:r + HD, :] = q
        qkv_ref[0, 0, PW + r:PW + r + HD, :] = k
        qkv_ref[0, 0, 2 * PW + r:2 * PW + r + HD, :] = v
        s = masked_scores(q, k, ok)
        m = jnp.max(s, axis=0, keepdims=True)
        e = jnp.exp(s - m)
        li = 1.0 / jnp.sum(e, axis=0, keepdims=True)
        p = (e * li).astype(bf16)
        m_ref[0, 0, h:h + 1, :] = m
        l_ref[0, 0, h:h + 1, :] = li
        o = dg(v, p, 1, 0).astype(bf16)
        o_ref[0, 0, r:r + HD, :] = o
        o_s[pl.ds(pl.multiple_of(g * PW + r, HD), HD), :] = o

    @pl.when(g == TP - 1)
    def _():
        attn = dg(o_s[...], wo_ref[...], 0, 0)
        x1 = (x_ref[0].astype(f32) + (attn + bo_ref[...])).astype(bf16)
        x1_ref[0] = x1
        xh, _ = ln_stats(x1.astype(f32))
        h2_ref[0] = (xh * g2_ref[...] + b2_ref[...]).astype(bf16)


def whole(shape):
    return pl.BlockSpec(shape, lambda s, g: (0,) * len(shape), pipeline_mode=pl.Buffered(1))


def per_seq(shape):
    return pl.BlockSpec((1,) + shape, lambda s, g: (s,) + (0,) * len(shape))


def per_pair(shape):
    return pl.BlockSpec((1, 1) + shape, lambda s, g: (s, g) + (0,) * len(shape))


def attn_fwd_call(x, mask, cos, sin, g1, b1, wq, bq, wo, bo, g2, b2):
    return pl.pallas_call(
        attn_fwd_kernel,
        grid=(NS, TP),
        in_specs=[per_seq((S, D)), per_seq((S, PW)), whole((HH, S)), whole((HH, S)), whole((1, D)), whole((1, D)),
                  whole((TP, R3, D)), whole((TP, R3, 1)), whole((D, D)), whole((1, D)), whole((1, D)), whole((1, D))],
        out_specs=[per_pair((R3, S)), per_pair((2, S)), per_pair((2, S)), per_pair((PW, S)), per_seq((S, D)), per_seq((S, D))],
        out_shape=[sds((NS, TP, R3, S), bf16), sds((NS, TP, 2, S), f32), sds((NS, TP, 2, S), f32), sds((NS, TP, PW, S), bf16),
                   sds((NS, S, D), bf16), sds((NS, S, D), bf16)],
        scratch_shapes=[pltpu.VMEM((S, D), bf16), pltpu.VMEM((D, S), bf16)],
        compiler_params=pltpu.CompilerParams(dimension_semantics=("arbitrary", "arbitrary"), vmem_limit_bytes=VMEM_LIMIT),
        name="attn_fwd",
    )(x, mask, cos, sin, g1, b1, wq, bq, wo, bo, g2, b2)


def mlp_kernel(h2_ref, dy_ref, x1_ref, wu_ref, wd_ref, bu_ref, bd_ref, y_ref, dh_ref, gd_ref, gu_ref, gb_ref, yacc, dacc):
    i, t = pl.program_id(0), pl.program_id(1)
    rows = pl.ds(pl.multiple_of(t * S, S), S)
    h2, dy = h2_ref[rows, :], dy_ref[rows, :]
    wu, wd = wu_ref[0], wd_ref[0]
    pre = dg(h2, wu, 1, 0) + bu_ref[0]
    d_act = dg(dy, wd, 1, 1)
    cdf = 0.5 * (1.0 + lax.erf(pre * INV_SQRT2))
    act = (pre * cdf).astype(bf16)
    d_pre = d_act * (cdf + pre * jnp.exp(-0.5 * pre * pre) * INV_SQRT_2PI)
    d_pre_b = d_pre.astype(bf16)
    yp = dg(act, wd, 1, 0)
    dp = dg(d_pre_b, wu, 1, 1)
    gd = dg(act, dy, 0, 0)
    gu = dg(d_pre_b, h2, 0, 0)
    gb = jnp.sum(d_pre, axis=0, keepdims=True)

    @pl.when(i == 0)
    def _():
        yacc[rows, :] = yp
        dacc[rows, :] = dp

    @pl.when(i > 0)
    def _():
        yacc[rows, :] += yp
        dacc[rows, :] += dp

    @pl.when(t == 0)
    def _():
        gd_ref[0] = gd
        gu_ref[0] = gu
        gb_ref[0] = gb

    @pl.when(t > 0)
    def _():
        gd_ref[0] += gd
        gu_ref[0] += gu
        gb_ref[0] += gb

    @pl.when(i == TP - 1)
    def _():
        y_ref[...] = (x1_ref[...].astype(f32) + (yacc[rows, :] + bd_ref[...])).astype(bf16)
        dh_ref[...] = dacc[rows, :]


def mlp_call(h2, dy, x1, wu, wd, bu, bd):
    T = NS * S
    res = pl.BlockSpec((T, D), lambda i, t: (0, 0), pipeline_mode=pl.Buffered(1))
    last = pl.BlockSpec((S, D), lambda i, t: (jnp.where(i == TP - 1, t, 0), 0))
    blk = lambda shape: pl.BlockSpec((1,) + shape, lambda i, t: (i, 0, 0))
    return pl.pallas_call(
        mlp_kernel,
        grid=(TP, NS),
        in_specs=[res, res, last, blk((D, FB)), blk((FB, D)), blk((1, FB)), whole((1, D))],
        out_specs=[last, last, blk((FB, D)), blk((FB, D)), blk((1, FB))],
        out_shape=[sds((T, D), bf16), sds((T, D), f32), sds((TP, FB, D), f32), sds((TP, FB, D), f32), sds((TP, 1, FB), f32)],
        scratch_shapes=[pltpu.VMEM((T, D), f32), pltpu.VMEM((T, D), f32)],
        compiler_params=pltpu.CompilerParams(dimension_semantics=("arbitrary", "arbitrary"), vmem_limit_bytes=VMEM_LIMIT),
        name="mlp",
    )(h2, dy, x1, wu, wd, bu, bd)


def attn_bwd_kernel(x_ref, x1_ref, dy_ref, dh2_ref, mask_ref, cos_ref, sin_ref, g1_ref, b1_ref, g2_ref, wq_ref, wo_ref,
                    qkv_ref, m_ref, l_ref, o_ref, gx_ref, gq_ref, go_ref, gbq_ref, vec_ref,
                    h1_s, dx1_s, dx1_b, do_s, dq_s, gq_a, go_a, gb_a, v_a):
    sq, g = pl.program_id(0), pl.program_id(1)

    @pl.when((g == 0) & (sq == 0))
    def _():
        gq_a[...] = jnp.zeros_like(gq_a)
        go_a[...] = jnp.zeros_like(go_a)
        gb_a[...] = jnp.zeros_like(gb_a)
        v_a[...] = jnp.zeros_like(v_a)

    @pl.when(g == 0)
    def _():
        dy, dh2 = dy_ref[0].astype(f32), dh2_ref[0]
        xh2, inv2 = ln_stats(x1_ref[0].astype(f32))
        d = dy + ln_grad(dh2, xh2, inv2, g2_ref[...])
        dx1_s[...] = d
        db = d.astype(bf16)
        dx1_b[...] = db
        v_a[0:1, :] += jnp.sum(dy, axis=0, keepdims=True)
        v_a[1:2, :] += jnp.sum(dh2 * xh2, axis=0, keepdims=True)
        v_a[2:3, :] += jnp.sum(dh2, axis=0, keepdims=True)
        v_a[3:4, :] += jnp.sum(d, axis=0, keepdims=True)
        xh, _ = ln_stats(x_ref[0].astype(f32))
        h1_s[...] = (xh * g1_ref[...] + b1_ref[...]).astype(bf16)
        do_s[...] = dg(wo_ref[...], db, 1, 1).astype(bf16)

    go_a[pl.ds(pl.multiple_of(g * PW, PW), PW), :] += dg(o_ref[0, 0], dx1_b[...], 1, 0)
    cos, sin = cos_ref[...], sin_ref[...]
    ok = key_mask(mask_ref)

    def rot_back(t):
        a, b = t[:HH], t[HH:]
        return jnp.concatenate([a * cos + b * sin, b * cos - a * sin], axis=0)

    base = pl.multiple_of(g * R3, PW)
    for h in range(2):
        r = h * HD
        q = qkv_ref[0, 0, r:r + HD, :]
        k = qkv_ref[0, 0, PW + r:PW + r + HD, :]
        v = qkv_ref[0, 0, 2 * PW + r:2 * PW + r + HD, :]
        do = do_s[pl.ds(pl.multiple_of(g * PW + r, HD), HD), :]
        s = masked_scores(q, k, ok)
        p = jnp.exp(s - m_ref[0, 0, h:h + 1, :]) * l_ref[0, 0, h:h + 1, :]
        dp = dg(v, do, 0, 0)
        ds = (p * (dp - jnp.sum(dp * p, axis=0, keepdims=True))).astype(bf16)
        dv = dg(do, p.astype(bf16), 1, 1)
        dk = rot_back(dg(q, ds, 1, 1))
        dq = rot_back(dg(k, ds, 1, 0)) * QS
        for j, t in enumerate((dq, dk, dv)):
            dq_s[pl.ds(base + j * PW + r, HD), :] = t.astype(bf16)
            gb_a[pl.ds(base + j * PW + r, HD), :] += jnp.sum(t, axis=1, keepdims=True)
    gq_a[g] += dg(dq_s[pl.ds(base, R3), :], h1_s[...], 1, 0)

    @pl.when(g == TP - 1)
    def _():
        dh1 = dg(dq_s[...], wq_ref[...].reshape(TP * R3, D), 0, 0)
        xh, inv = ln_stats(x_ref[0].astype(f32))
        v_a[4:5, :] += jnp.sum(dh1 * xh, axis=0, keepdims=True)
        v_a[5:6, :] += jnp.sum(dh1, axis=0, keepdims=True)
        gx_ref[0] = (dx1_s[...] + ln_grad(dh1, xh, inv, g1_ref[...])).astype(bf16)

    @pl.when(sq == NS - 1)
    def _():
        gq_ref[0] = gq_a[g]
        go_ref[0] = go_a[pl.ds(pl.multiple_of(g * PW, PW), PW), :]
        gbq_ref[0] = gb_a[pl.ds(base, R3), :]
        vec_ref[...] = v_a[...]


def attn_bwd_call(x, x1, dy, dh2, mask, cos, sin, g1, b1, g2, wq, wo, qkv, m, l, o):
    last = lambda shape: pl.BlockSpec((1,) + shape, lambda s, g: (jnp.where(s == NS - 1, g, 0), 0, 0))
    return pl.pallas_call(
        attn_bwd_kernel,
        grid=(NS, TP),
        in_specs=[per_seq((S, D))] * 4 + [per_seq((S, PW)), whole((HH, S)), whole((HH, S)), whole((1, D)), whole((1, D)),
                  whole((1, D)), whole((TP, R3, D)), whole((D, D)), per_pair((R3, S)), per_pair((2, S)), per_pair((2, S)),
                  per_pair((PW, S))],
        out_specs=[per_seq((S, D)), last((R3, D)), last((PW, D)), last((R3, 1)), pl.BlockSpec((8, D), lambda s, g: (0, 0))],
        out_shape=[sds((NS, S, D), bf16), sds((TP, R3, D), f32), sds((TP, PW, D), f32), sds((TP, R3, 1), f32), sds((8, D), f32)],
        scratch_shapes=[pltpu.VMEM((S, D), bf16), pltpu.VMEM((S, D), f32), pltpu.VMEM((S, D), bf16), pltpu.VMEM((D, S), bf16),
                        pltpu.VMEM((TP * R3, S), bf16), pltpu.VMEM((TP, R3, D), f32), pltpu.VMEM((D, D), f32),
                        pltpu.VMEM((TP * R3, 1), f32), pltpu.VMEM((8, D), f32)],
        compiler_params=pltpu.CompilerParams(dimension_semantics=("arbitrary", "arbitrary"), vmem_limit_bytes=VMEM_LIMIT),
        name="attn_bwd",
    )(x, x1, dy, dh2, mask, cos, sin, g1, b1, g2, wq, wo, qkv, m, l, o)


N_RS = 4


def scatter_kernel(y_ref, gx_ref, msg_ref, *refs):
    parts, refs = refs[:N_RS], refs[N_RS:]
    yo_ref, gxo_ref, small_ref, refs = refs[0], refs[1], refs[2], refs[3:]
    outs, refs = refs[:N_RS], refs[N_RS:]
    hbm, refs = refs[:4 * N_RS], refs[4 * N_RS:]
    act_buf, bufs, msgs, buf_sem, a_ss, a_rs, r_ss, r_rs, m_ss, m_rs = refs
    pc = Place()
    entry_barrier(pc)
    rs = [ReduceScatter(pc, parts[i], *hbm[4 * i:4 * i + 4], outs[i], (r_ss.at[i], r_rs.at[i]),
                        [bufs.at[j] for j in range(4)], buf_sem) for i in range(N_RS)]
    a2a = [AllToAll(pc, p, s, a_ss.at[i], a_rs.at[i], False)
           for i, (p, s) in enumerate(((yo_ref, y_ref), (gxo_ref, gx_ref)))]
    for r in rs:
        r.start()
    small = [remote(msg_ref.at[pc.slot_of(m)], msgs.at[pc.me], m_ss.at[m], m_rs.at[m], pc.peer(m)) for m in range(1, TP)]
    for cp in small:
        cp.start()
    own = pltpu.make_async_copy(msg_ref.at[pc.slot_of(0)], msgs.at[pc.me], m_ss.at[0])
    own.start()
    local = [a2a[i].local(act_buf.at[i]) for i in range(2)]
    for load, _ in local:
        load.start()
    for load, store in local:
        load.wait()
        store.start()
    for r in rs:
        r.first(1)
        r.first(0)
    for a in a2a:
        a.start()
    for r in rs:
        r.second()
    for r in rs:
        r.last()
    own.wait()
    for m, cp in enumerate(small):
        cp.wait_send()
        wait_for(msgs.at[pc.peer(m + 1)], m_rs.at[m + 1])
    total = msgs[0]
    for j in range(1, TP):
        total = total + msgs[j]
    small_ref[...] = total
    for _, store in local:
        store.wait()
    for r in rs:
        r.finish()
    for a in a2a:
        a.finish()


def scatter_call(y, gx, msg, parts):
    rows = [p.shape[1] for p in parts]
    hbm = []
    for r in rows:
        hbm += [sds((4, r, D), f32), sds((2, r, D), f32), sds((r, D), f32), sds((3, r, D), f32)]
    out = pl.pallas_call(
        scatter_kernel,
        in_specs=[ANY] * (3 + N_RS),
        out_specs=[ANY, ANY, pl.BlockSpec(memory_space=pltpu.VMEM)] + [ANY] * (N_RS + len(hbm)),
        out_shape=[sds((TP * NS, SL, D), bf16), sds((TP * NS, SL, D), bf16), sds((8, D), f32)]
        + [sds((r, D), f32) for r in rows] + hbm,
        scratch_shapes=[pltpu.VMEM((2, NS, SL, D), bf16), pltpu.VMEM((4, max(rows), D), f32), pltpu.VMEM((TP, 8, D), f32),
                        pltpu.SemaphoreType.DMA((4,)), pltpu.SemaphoreType.DMA((2, 8)), pltpu.SemaphoreType.DMA((2, 8)),
                        pltpu.SemaphoreType.DMA((N_RS, 7)), pltpu.SemaphoreType.DMA((N_RS, 7)),
                        pltpu.SemaphoreType.DMA((8,)), pltpu.SemaphoreType.DMA((8,))],
        compiler_params=pltpu.CompilerParams(collective_id=1, has_side_effects=True, vmem_limit_bytes=VMEM_LIMIT),
        name="scatter_out",
    )(y, gx, msg, *parts)
    return out[0], out[1], out[2], out[3:3 + N_RS]


def rope_tables():
    inv_freq = ROPE_BASE ** (-2.0 * jnp.arange(HH, dtype=f32) / HD)
    angles = jnp.arange(S, dtype=f32)[:, None] * inv_freq[None, :]
    return jnp.cos(angles).T, jnp.sin(angles).T


def solution(mesh):
    act_spec = P('dp', 'tp', None)
    rep_vec = P(None)
    part_vec = P('dp')
    in_specs = (act_spec, act_spec, P('dp', None), rep_vec, rep_vec, P(None, None, 'tp', None), P(None, 'tp', None),
                P('tp', None, None), rep_vec, rep_vec, rep_vec, P(None, 'tp'), P('tp'), P('tp', None), rep_vec)
    out_specs = (act_spec, act_spec, part_vec, part_vec, P('dp', None, 'tp', None), P('dp', 'tp', None),
                 P(('dp', 'tp'), None, None), part_vec, part_vec, part_vec, P('dp', 'tp'), P(('dp', 'tp')),
                 P(('dp', 'tp'), None), part_vec)

    def device_step(x_in, grad_y, pad_mask, ln1_gain, ln1_bias, w_qkv, b_qkv, w_out, b_out, ln2_gain, ln2_bias, w_up, b_up, w_down, b_down):
        assert x_in.shape == (TP * NS, SL, D) and w_qkv.shape == (3, D, 2, HD) and w_up.shape == (D, FB)
        me = lax.axis_index('tp')
        row = lambda v: v.reshape(1, D)
        wq = w_qkv.transpose(0, 2, 3, 1).reshape(R3, D)
        wo = w_out.reshape(PW, D)
        bs = jnp.concatenate([b_qkv.reshape(R3), b_up, jnp.zeros((8 * 128 - R3 - FB,), f32)]).reshape(8, 128)
        x, dy, wq, wo, wu, wd, bs = gather_call(x_in, grad_y, wq, wo, w_up, w_down, bs)
        bs = bs.reshape(TP, 8 * 128)
        bq = bs[:, :R3, None]
        bu = bs[:, None, R3:R3 + FB]
        mask = lax.dynamic_slice_in_dim(pad_mask, me * NS, NS, 0)
        mask = jnp.broadcast_to(mask[:, :, None], (NS, S, PW))
        cos, sin = rope_tables()
        wo2 = wo.reshape(TP * PW, D)
        qkv, m, l, o, x1, h2 = attn_fwd_call(x, mask, cos, sin, row(ln1_gain), row(ln1_bias), wq, bq, wo2, row(b_out),
                                             row(ln2_gain), row(ln2_bias))
        flat = lambda t: t.reshape(NS * S, D)
        y, dh2, gd, gu, gbu = mlp_call(flat(h2), flat(dy), flat(x1), wu, wd, bu, row(b_down))
        gx, gq, go, gbq, vec = attn_bwd_call(x, x1, dy, dh2.reshape(NS, S, D), mask, cos, sin, row(ln1_gain), row(ln1_bias),
                                             row(ln2_gain), wq, wo2, qkv, m, l, o)
        msg = jnp.concatenate([jnp.broadcast_to(vec[:6], (TP, 6, D)),
                               jnp.concatenate([gbq.reshape(TP, R3), gbu.reshape(TP, FB), jnp.zeros((TP, D - R3 - FB), f32)],
                                               axis=1)[:, None, :], jnp.zeros((TP, 1, D), f32)], axis=1)
        y_out, grad_x, small, (gd, gu, gq, go) = scatter_call(y.reshape(NS, S, D), gx, msg, [gd, gu, gq, go])
        return (y_out, grad_x, small[4], small[5], gq.reshape(3, 2, HD, D).transpose(0, 3, 1, 2), small[6, :R3].reshape(3, 2, HD),
                go.reshape(2, HD, D), small[3], small[1], small[2], gu.T, small[6, R3:R3 + FB], gd, small[0])

    return jax.shard_map(device_step, mesh=mesh, in_specs=in_specs, out_specs=out_specs, check_vma=False)
```

time: 2720 us -> 898 us (0.33)
  waiting for transfers between devices: 1950 us -> 0 us
  Pallas kernels: 0 us -> 867 us
  matrix products: 539 us -> 0 us
  other arithmetic: 184 us -> 4.94 us
    reduce_scatter x4 -> x0, waiting for transfers between devices: 1360 us -> none  [the longest x1 375 us: device_step(): lax.psum_scatter(attn_part, 'tp', scatter_dimension=1, tiled=True)]
    pallas_call x0 -> x5, Pallas kernels: none -> 867 us  [the longest x1 308 us: scatter_call(): pl.pallas_call(scatter_kernel, in_specs=[ANY] * (3 + N_RS), out_specs=[AN...]
    all_gather x4 -> x0, waiting for transfers between devices: 589 us -> none  [the longest x1 157 us: device_step(): lax.all_gather(h1_f.astype(jnp.bfloat16), 'tp', axis=1, tiled=True)]
    dot_general x17 -> x0, matrix products: 507 us -> none  [the longest x1 47.8 us: device_step(): jnp.einsum('bqhk,bshk->bhqs', d_attn_o, v_heads, preferred_element_type=j...]
    convert_element_type x6 -> x0, other arithmetic: 89 us -> none  [the longest x1 52.6 us: device_step(): (attn_probs * (d_probs - jnp.sum(d_probs * attn_probs, axis=-1, keepdims=...]
    reduce_sum x8 -> x0, other arithmetic: 50.9 us -> none  [the longest x1 13.2 us: device_step(): jnp.sum(d_x1, axis=(0, 1))]
    sub x1 -> x0, matrix products: 31.5 us -> none  [device_step(): attn_probs = jax.nn.softmax(jnp.where(key_ok, scores, NEG_LARGE), axis=-1)]
  transfers between devices with their start and end apart: 8 -> 0, of which waited for: 8 -> 0; matrix products, arithmetic and copies ran while one was open for 7% -> 0% of each run, Pallas kernels for 0% -> 0%
where the time goes in v1:
time: 898 us; the launch traced here: 897 us
  Pallas kernels  867 us (97%)
  local copies, waits for them, and re-layouts  24.3 us (3%)
    pallas_call x1, Pallas kernels, scatter_call(): pl.pallas_call(scatter_kernel, in_specs=[ANY] * (3 + N_RS), out_specs=[AN...  308 us
    pallas_call x1, Pallas kernels, gather_call(): pl.pallas_call(gather_kernel, in_specs=[ANY] * 7, out_specs=[ANY] * 7, ou...  200 us
    pallas_call x1, Pallas kernels, mlp_call(): pl.pallas_call(mlp_kernel, grid=(TP, NS), in_specs=[res, res, last, blk((...  154 us
    pallas_call x1, Pallas kernels, attn_bwd_call(): pl.pallas_call(attn_bwd_kernel, grid=(NS, TP), in_specs=[per_seq((S, D))]...  124 us
    pallas_call x1, Pallas kernels, attn_fwd_call(): pl.pallas_call(attn_fwd_kernel, grid=(NS, TP), in_specs=[per_seq((S, D)),...  80.8 us

profile of v1, /device:TPU:0, one launch (start us, length us, event | category | flops | bytes accessed | tf_op | source)
XLA Modules:
  0.0 897.2 jit_solution(13522774895491612118)
XLA Ops:
  0.6 0.0 copy-start
  0.7 0.1 pad.2.clone
  0.8 0.8 reshape.102
  1.5 1.3 fusion.3
  2.8 0.0 copy-done
  2.8 1.0 fusion
  3.8 1.3 broadcast_in_dim.30.mask_ref
  5.1 200.3 %gather_in.1 = (bf16[4,512,1024]{2,1,0:T(8,128)(2,1)}, bf16[4,512,1024]{2,1,0:T(8,128)(2,1)}, bf16[8,384,1024]{2,1,0:T(8,128)(2,1)}, bf16[8,128,1024]{2,1,0:T(8,...) custom-call(bf16[32,64,1024]{2,1,0:T(8,128)(2,1)} %x_ref.1, ...), custom_call_target="tpu_custom_call" | custom-call | tf_op jit(solution)/shard_map/gather_in/pallas_call | solution.py:276
  205.4 0.8 copy.37
  206.2 0.6 broadcast_in_dim.32.bu_ref
  206.8 1.7 copy.31.bq_ref
  208.5 80.8 %attn_fwd.1 = (bf16[4,8,384,512]{3,2,1,0:T(8,128)(2,1)}, f32[4,8,2,512]{3,2,1,0:T(2,128)}, f32[4,8,2,512]{3,2,1,0:T(2,128)}, bf16[4,8,128,512]{3,2,1,0:T(8,128)(...) custom-call(bf16[4,512,1024]{2,1,0:T(8,128)(2,1)} %get-tuple-element.44.x_ref, ...), custom_call_target="tpu_custom_call" | custom-call | tf_op jit(solution)/shard_map/attn_fwd/pallas_call | solution.py:368
  289.3 153.7 %mlp.1 = (bf16[2048,1024]{1,0:T(8,128)(2,1)}, f32[2048,1024]{1,0:T(8,128)}, f32[8,512,1024]{2,1,0:T(8,128)}, f32[8,512,1024]{2,1,0:T(8,128)}, f32[8,1,512]{2,1,0:T(1,128)}) custom-call(bf16[2048,1024]{1,0:T(8,128)(2,1)} %bitcast.47, bf16[2048,1024]{1,0:T(8,128)(2,1)} %bitcast.41, bf16[2048,1024]{1,0:T(8,128)(2,1)} %bitcast.42, ...), custom_call_target="tpu_custom_call" | custom-call | tf_op jit(solution)/shard_map/mlp/pallas_call | solution.py:432
  443.0 0.0 copy-start.6
  443.0 124.1 %attn_bwd.1 = (bf16[4,512,1024]{2,1,0:T(8,128)(2,1)}, f32[8,384,1024]{2,1,0:T(8,128)}, f32[8,128,1024]{2,1,0:T(8,128)}, f32[8,384,1]{2,1,0:T(8,128)}, f32[8,1024]{1,0:T(8,128)}) custom-call(bf16[4,512,1024]{2,1,0:T(8,128)(2,1)} %get-tuple-element.44.x_ref, bf16[4,512,1024]{2,1,0:T(8,128)(2,1)} %get-tuple-element.50.x1_ref, ...), custom_call_target="tpu_custom_call" | custom-call | tf_op jit(solution)/shard_map/attn_bwd/pallas_call | solution.py:517
  567.1 1.9 reduce
  568.9 0.0 copy-done.6
  569.0 0.8 broadcast_in_dim.33
  569.8 0.8 maximum_maximum_fusion.msg_ref
  570.6 308.3 %scatter_out.1 = (bf16[32,64,1024]{2,1,0:T(8,128)(2,1)}, bf16[32,64,1024]{2,1,0:T(8,128)(2,1)}, f32[8,1024]{1,0:T(8,128)}, f32[512,1024]{1,0:T(8,128)}, f32[512,...) custom-call(bf16[4,512,1024]{2,1,0:T(8,128)(2,1)} %bitcast.46, ...), custom_call_target="tpu_custom_call" | custom-call | tf_op jit(solution)/shard_map/scatter_out/pallas_call | solution.py:591
  878.9 0.7 slice_reduce_fusion
  879.6 0.7 reshape_squeeze.3
  880.3 1.3 slice.42
  881.6 1.6 fusion.2
  883.2 2.9 copy.32
  886.0 0.0 copy-start.2
  886.0 5.1 copy.44
  891.1 0.0 copy-done.2
  891.1 0.0 copy-start.4
  891.1 0.0 copy-start.5
  891.1 0.0 copy-start.1
  891.1 2.1 copy.45
  893.3 0.4 copy-done.4
  893.6 0.0 copy-start.3
  893.6 1.1 copy.46
  894.8 0.0 copy-done.5
  894.8 0.8 copy.47
  895.6 0.3 copy-done.3
  895.9 1.3 copy.48
  897.2 0.0 copy-done.1
  (8 shorter events, 0.1 us)
Async XLA Ops:
  0.6 2.2 copy-start
  443.0 126.0 %copy-start.6 = (f32[8,1,512]{2,1,0:T(1,128)S(1)}, f32[8,1,512]{2,1,0:T(1,128)}, u32[]{:S(2)}) copy-start(f32[8,1,512]{2,1,0:T(1,128)} %get-tuple-element.62) | copy-start | bytes 49156
  886.0 5.1 copy-start.2
  891.1 2.5 copy-start.4
  891.1 3.7 copy-start.5
  891.1 6.1 copy-start.1
  893.6 2.3 copy-start.3

commit v2 on v0

v2 whole, which is shorter than its diff:
```python
import jax
import jax.numpy as jnp
import numpy as np
from jax import lax
from jax.experimental import pallas as pl
from jax.experimental.pallas import tpu as pltpu
from jax.sharding import PartitionSpec as P

f32 = jnp.float32
bf16 = jnp.bfloat16
LN_EPS = 1e-5
ROPE_BASE = 10000.0
INV_SQRT2 = 0.7071067811865476
INV_SQRT_2PI = 0.3989422804014327
NEG_LARGE = -1e30
MESH = pl.DeviceIdType.MESH
ANY = pl.BlockSpec(memory_space=pl.ANY)
VMEM_LIMIT = 66_000_000

TP = 8
NS = 4
S = 512
D = 1024
PW = 128
HD = 64
HH = HD // 2
FB = 512
SL = 64
QS = HD ** -0.5
R3 = 3 * PW


def dg(a, b, ca, cb):
    return lax.dot_general(a, b, (((ca,), (cb,)), ((), ())), preferred_element_type=f32)


def nn(a, b):
    return dg(a, b, 1, 0)


def nt(a, b):
    return dg(a, b, 1, 1)


def tn(a, b):
    return dg(a, b, 0, 0)


def over_rows(reduce, v):
    return reduce(v, axis=0, keepdims=True)


def over_cols(reduce, v):
    return reduce(v, axis=1, keepdims=True)


def sds(shape, dtype):
    return jax.ShapeDtypeStruct(shape, dtype)


class Place:
    def __init__(self):
        me = lax.axis_index("tp")
        self.me = me
        self.c = lax.rem(me, 2)
        self.dc = 1 - 2 * self.c
        self.dx = 2 - 4 * lax.rem(lax.div(me, 2), 2)
        self.dy = 4 - 8 * lax.div(me, 4)
        self.partner = me + self.dc
        self.a = me + (1 - self.c) * self.dx + self.c * self.dy
        self.b = me + (1 - self.c) * self.dy + self.c * self.dx

    def peer(self, m):
        return self.me + (m & 1) * self.dc + ((m >> 1) & 1) * self.dx + (m >> 2) * self.dy

    def slot_of(self, m):
        k = self.c if m % 2 == 0 else 1 - self.c
        lo, hi = {0: (6, 7), 1: (0, 5), 2: (4, 1), 3: (2, 3)}[m >> 1]
        return lo + k * (hi - lo)


def remote(src, dst, send_sem, recv_sem, device):
    return pltpu.make_async_remote_copy(src_ref=src, dst_ref=dst, send_sem=send_sem, recv_sem=recv_sem,
                                        device_id={"tp": device}, device_id_type=MESH)


def wait_for(ref, sem):
    pltpu.make_async_copy(ref, ref, sem).wait()


def entry_barrier(pc):
    bar = pltpu.get_barrier_semaphore()
    for m in range(1, TP):
        pl.semaphore_signal(bar, inc=1, device_id={"tp": pc.peer(m)}, device_id_type=MESH)
    pl.semaphore_wait(bar, TP - 1)


class AllToAll:
    def __init__(self, pc, pos_ref, seq_ref, send_sem, recv_sem, inward):
        self.pc, self.pos, self.seq, self.ss, self.rs, self.inward = pc, pos_ref, seq_ref, send_sem, recv_sem, inward

    def _rows(self, dev):
        return pl.ds(pl.multiple_of(dev * SL, SL), SL)

    def _copy(self, s, m):
        pc, dev = self.pc, self.pc.peer(m)
        if self.inward:
            src, dst = self.pos.at[dev * NS + s], self.seq.at[s, self._rows(pc.me)]
        else:
            src, dst = self.seq.at[s, self._rows(dev)], self.pos.at[pc.me * NS + s]
        return remote(src, dst, self.ss.at[s, m], self.rs.at[s, m], dev)

    def start(self, s):
        for m in (2, 3, 4, 5, 6, 7, 1):
            self._copy(s, m).start()

    def finish(self, s):
        for m in range(1, TP):
            self._copy(s, m).wait()

    def local_in(self, buf):
        pc = self.pc
        return (pltpu.make_async_copy(self.pos.at[pl.ds(pc.me * NS, NS)], buf, self.ss.at[0, 0]),
                pltpu.make_async_copy(buf, self.seq.at[:, self._rows(pc.me)], self.rs.at[0, 0]))

    def local_out(self, s, src):
        return pltpu.make_async_copy(src.at[s, self._rows(self.pc.me)], self.pos.at[self.pc.me * NS + s], self.ss.at[s, 0])


class Gather:
    def __init__(self, pc, src_ref, dst_ref, send_sem, recv_sem):
        self.pc, self.src, self.dst, self.ss, self.rs = pc, src_ref, dst_ref, send_sem, recv_sem

    def _send(self, i, src, slot, dev):
        return remote(src, self.dst.at[slot], self.ss.at[i], self.rs.at[slot], dev)

    def _direct(self):
        pc, c = self.pc, self.pc.c
        return [self._send(0, self.src, c, pc.a), self._send(2, self.src, 6 + c, pc.partner),
                self._send(1, self.src, 4 + c, pc.b)]

    def _hop(self):
        pc, c = self.pc, self.pc.c
        return [self._send(3, self.dst.at[c], 2 + c, pc.b), self._send(4, self.dst.at[c], c, pc.partner),
                self._send(5, self.dst.at[4 + c], 4 + c, pc.partner)]

    def _last(self):
        pc, c = self.pc, self.pc.c
        return self._send(6, self.dst.at[2 + c], 2 + c, pc.partner)

    def arrived(self, slot):
        wait_for(self.dst.at[slot], self.rs.at[slot])

    def start(self):
        self.start_a()
        self.start_b()

    def start_a(self):
        for cp in self._direct()[:2]:
            cp.start()

    def start_b(self):
        self._direct()[2].start()

    def forward(self):
        self.forward_a()
        self.forward_b()

    def forward_a(self):
        hop = self._hop()
        self.arrived(self.pc.c)
        hop[0].start()
        hop[1].start()

    def forward_b(self):
        self.arrived(4 + self.pc.c)
        self._hop()[2].start()

    def last(self):
        self.arrived(2 + self.pc.c)
        self._last().start()

    def local(self, buf):
        return (pltpu.make_async_copy(self.src, buf, self.ss.at[7]),
                pltpu.make_async_copy(buf, self.dst.at[6 + self.pc.c], self.rs.at[6 + self.pc.c]))

    def arrived_rest(self):
        for j in range(4):
            self.arrived(2 * j + 1 - self.pc.c)
        self.arrived(6 + self.pc.c)

    def sent(self):
        for cp in self._direct() + self._hop() + [self._last()]:
            cp.wait_send()


def row_add(acc, others):
    step = 64

    def body(i, carry):
        r = pl.ds(pl.multiple_of(i * step, step), step)
        v = acc[r, :]
        for o in others:
            v = v + o[r, :]
        acc[r, :] = v
        return carry

    lax.fori_loop(0, acc.shape[0] // step, body, 0)


class GradScatter:
    def __init__(self, pc, acc, landing, stage, r1, r2, sems, free):
        self.pc, self.acc, self.landing, self.stage, self.r1, self.r2 = pc, acc, landing, stage, r1, r2
        self.sem, self.free = sems, free

    def _pair(self, b):
        return remote(self.acc.at[b], self.landing, self.sem.at[0], self.sem.at[1], self.pc.partner)

    def _first(self, j):
        return remote(self.stage.at[j], self.r1.at[j], self.sem.at[2 + j], self.sem.at[4 + j], self.pc.a)

    def _second(self):
        return remote(self.stage.at[2], self.r2, self.sem.at[6], self.sem.at[7], self.pc.b)

    def block_done(self, slot, b, needs_credit):
        @pl.when(lax.rem(slot, 2) != self.pc.c)
        def _():
            @pl.when(needs_credit)
            def _():
                pl.semaphore_wait(self.free, 1)

            self._pair(b).start()

    def settle(self, slot, b, gives_credit):
        c = self.pc.c
        own = lax.rem(slot, 2) == c
        j = lax.div(slot, 2)

        @pl.when(own)
        def _():
            wait_for(self.landing, self.sem.at[1])
            row_add(self.acc.at[b], [self.landing])

            @pl.when(gives_credit)
            def _():
                pl.semaphore_signal(self.free, inc=1, device_id={"tp": self.pc.partner}, device_id_type=MESH)

            store = pltpu.make_async_copy(self.acc.at[b], self.stage.at[j], self.sem.at[8])
            store.start()
            store.wait()

            @pl.when(j < 2)
            def _():
                self._first(j).start()

        @pl.when(jnp.logical_not(own))
        def _():
            self._pair(b).wait_send()

    def second(self, bufs, chunk_sem):
        n = chunk_sem.shape[1]
        size = bufs[0].shape[0]
        rows = size // n
        part = lambda ref, k: ref.at[pl.ds(k * rows, rows)]
        wait_for(self.r1.at[1], self.sem.at[5])
        for p in range(self.r2.shape[0] // size):
            mine, theirs = (ref.at[pl.ds(p * size, size)] for ref in (self.stage.at[2], self.r1.at[1]))
            loads = [[pltpu.make_async_copy(part(src, k), part(buf, k), chunk_sem.at[x, k])
                      for x, (src, buf) in enumerate(zip((mine, theirs), bufs))] for k in range(n)]
            stores = [pltpu.make_async_copy(part(bufs[0], k), part(mine, k), chunk_sem.at[2, k]) for k in range(n)]
            for group in loads:
                for cp in group:
                    cp.start()
            for k in range(n):
                for cp in loads[k]:
                    cp.wait()
                row_add(part(bufs[0], k), [part(bufs[1], k)])
                stores[k].start()
            for cp in stores:
                cp.wait()
        self._second().start()

    def finish(self):
        wait_for(self.r1.at[0], self.sem.at[4])
        for j in range(2):
            self._first(j).wait_send()
        self._second().wait()


def ln_stats(v):
    c = v - over_cols(jnp.mean, v)
    inv = lax.rsqrt(over_cols(jnp.mean, c * c) + LN_EPS)
    return c * inv, inv


def ln_grad(d_out, x_hat, inv, gain):
    dh = d_out * gain
    return inv * (dh - over_cols(jnp.mean, dh) - x_hat * over_cols(jnp.mean, dh * x_hat))


def masked_scores(q, k, ok):
    return jnp.where(ok, tn(k, q), NEG_LARGE)


def key_mask(mask):
    return jnp.concatenate([mask] * (S // PW), axis=1) > 0


def column(row):
    return jnp.broadcast_to(row, (128, row.shape[1])).T[:, :1]


def load_all(pairs, sem):
    cps = [pltpu.make_async_copy(s, d, sem.at[i]) for i, (s, d) in enumerate(pairs)]
    for cp in cps:
        cp.start()
    return cps


def vm(*shape, dtype=f32):
    return pltpu.VMEM(shape, dtype)


TT = 1024
NT = NS * S // TT
IN_NAMES = ("x_in", "dy_in", "wq", "wo", "wu", "wd", "bqkv", "bup", "pad", "cos", "sin", "gain1", "bias1", "gain2", "bias2",
            "b_out", "b_down")
OUT_SHAPES = {
    "y_out": ((TP * NS, SL, D), bf16), "gx_out": ((TP * NS, SL, D), bf16), "small": ((8, D), f32), "gd": ((FB, D), f32), "gu": ((D, FB), f32),
    "a_stage": ((4, R3 + PW, D), f32), "a_r1": ((2, R3 + PW, D), f32), "a_r2": ((R3 + PW, D), f32),
    "m_stage": ((4, 2 * FB, D), f32), "m_r1": ((2, 2 * FB, D), f32), "m_r2": ((2 * FB, D), f32),
    "xs": ((NS, S, D), bf16), "dys": ((NS, S, D), bf16), "wq_all": ((TP, R3, D), bf16), "wo_all": ((TP, PW, D), bf16),
    "wu_all": ((TP, D, FB), bf16), "wd_all": ((TP, FB, D), bf16),
    "qkv": ((NS, TP, R3, S), bf16), "ml": ((NS, TP, 4, S), f32), "o": ((NS, TP, PW, S), bf16),
    "x1": ((NS, S, D), bf16), "h2": ((NS, S, D), bf16), "y_seq": ((NS, S, D), bf16),
}
DMA = pltpu.SemaphoreType.DMA
SCRATCH = {
    "bs_all": vm(TP, 8, 128), "bs": vm(8, 128), "mask": vm(NS, S, PW), "dacc": vm(NS * S, D), "landing": vm(2 * FB, D), "gbu": vm(TP, 1, FB), "va": vm(8, D),
    "msg": vm(TP, 8, D), "msgs": vm(TP, 8, D),
    "free": pltpu.SemaphoreType.REGULAR,
    "x_ss": DMA((NS, 8)), "x_rs": DMA((NS, 8)), "dy_ss": DMA((NS, 8)), "dy_rs": DMA((NS, 8)),
    "y_ss": DMA((NS, 8)), "y_rs": DMA((NS, 8)), "gx_ss": DMA((NS, 8)), "gx_rs": DMA((NS, 8)),
    "g_ss": DMA((5, 8)), "g_rs": DMA((5, 8)), "m_sem": DMA((9,)), "a_sem": DMA((9,)), "s_ss": DMA((8,)), "s_rs": DMA((8,)),
    "tmp": DMA((8,)), "chunk": DMA((3, 4)), "w_sem": DMA((2, 2)),
}


class Refs:
    def __init__(self, names, refs):
        for n, r in zip(names, refs):
            setattr(self, n, r)


def layer_kernel(*refs):
    r = Refs(IN_NAMES + tuple(OUT_SHAPES) + tuple(SCRATCH), refs)
    pc = Place()
    for i in range(3):
        for h in range(2):
            r.bs[i:i + 1, h * HD:(h + 1) * HD] = r.bqkv[i, h:h + 1, :]
    for k in range(4):
        r.bs[4 + k:5 + k, :] = r.bup[:, k * 128:(k + 1) * 128]
    entry_barrier(pc)
    x_a2a = AllToAll(pc, r.x_in, r.xs, r.x_ss, r.x_rs, True)
    dy_a2a = AllToAll(pc, r.dy_in, r.dys, r.dy_ss, r.dy_rs, True)
    y_a2a = AllToAll(pc, r.y_out, r.y_seq, r.y_ss, r.y_rs, False)
    g_bs, g_wq, g_wo, g_wu, g_wd = [
        Gather(pc, s, d, r.g_ss.at[i], r.g_rs.at[i])
        for i, (s, d) in enumerate(((r.bs, r.bs_all), (r.wq, r.wq_all), (r.wo, r.wo_all), (r.wu, r.wu_all), (r.wd, r.wd_all)))]
    gain1, bias1, gain2, bias2, b_out, b_down = r.gain1, r.bias1, r.gain2, r.bias2, r.b_out, r.b_down

    def arrivals(b_x, b_dy, b_q, b_o, b_u, b_d):
        first = (g_bs, g_wq, g_wo)
        for g in first:
            g.start()
        x_a2a.start(0)
        own_bs = pltpu.make_async_copy(r.bs, r.bs_all.at[6 + pc.c], r.g_rs.at[0, 6 + pc.c])
        own_bs.start()
        local = [x_a2a.local_in(b_x), dy_a2a.local_in(b_dy)]
        local += [g.local(b) for g, b in ((g_wq, b_q), (g_wo, b_o), (g_wu, b_u), (g_wd, b_d))]
        for load, _ in local:
            load.start()
        for s in range(NS):
            keys = jnp.broadcast_to(r.pad[pl.ds(pc.me * NS + s, 1), :].astype(f32), (PW, S))
            r.mask[s] = keys.T
        for load, store in local:
            load.wait()
            store.start()
        for g in first:
            g.forward_a()
        for g in first:
            g.forward_b()
        x_a2a.finish(0)
        x_a2a.start(1)
        for g in first:
            g.last()
        for s in range(2, NS):
            x_a2a.start(s)
        for s in range(NS):
            dy_a2a.start(s)
        g_wu.start_a()
        g_wd.start_a()
        for g in first:
            g.arrived_rest()
        for g in (g_wu, g_wd):
            g.arrived(6 + pc.c)
        local[0][1].wait()
        local[1][1].wait()

    act = vm(NS, SL, D, dtype=bf16)
    pl.run_scoped(arrivals, act, act, vm(R3, D, dtype=bf16), vm(PW, D, dtype=bf16), vm(D, FB, dtype=bf16), vm(FB, D, dtype=bf16))

    def attn_fwd(wq_v, wo_v, h1_s, o_s):
        cps = load_all([(r.wq_all, wq_v), (r.wo_all, wo_v)], r.tmp)
        for cp in cps:
            cp.wait()

        def body(x_ref, qkv_ref, ml_ref, o_ref, x1_ref, h2_ref):
            s, g = pl.program_id(0), pl.program_id(1)

            @pl.when(g == 0)
            def _():
                xh, _ = ln_stats(x_ref[0].astype(f32))
                h1_s[...] = (xh * gain1[...] + bias1[...]).astype(bf16)

            bias = r.bs_all[g]
            bias = jnp.concatenate([column(bias[i:i + 1]) for i in range(3)], axis=0)
            qkv = nt(wq_v[g], h1_s[...]) + bias
            cos, sin = r.cos[...], r.sin[...]
            ok = key_mask(r.mask[s])

            def rot(t):
                a, b = t[:HH], t[HH:]
                return jnp.concatenate([a * cos - b * sin, b * cos + a * sin], axis=0).astype(bf16)

            for h in range(2):
                lo = h * HD
                q = rot(qkv[lo:lo + HD] * QS)
                k = rot(qkv[PW + lo:PW + lo + HD])
                v = qkv[2 * PW + lo:2 * PW + lo + HD].astype(bf16)
                qkv_ref[0, 0, lo:lo + HD, :] = q
                qkv_ref[0, 0, PW + lo:PW + lo + HD, :] = k
                qkv_ref[0, 0, 2 * PW + lo:2 * PW + lo + HD, :] = v
                sc = masked_scores(q, k, ok)
                m = over_rows(jnp.max, sc)
                e = jnp.exp(sc - m)
                li = 1.0 / over_rows(jnp.sum, e)
                p = (e * li).astype(bf16)
                ml_ref[0, 0, h:h + 1, :] = m
                ml_ref[0, 0, 2 + h:3 + h, :] = li
                o = nn(v, p).astype(bf16)
                o_ref[0, 0, lo:lo + HD, :] = o
                o_s[pl.ds(pl.multiple_of(g * PW + lo, HD), HD), :] = o

            @pl.when(g == TP - 1)
            def _():
                attn = tn(o_s[...], wo_v[...].reshape(TP * PW, D))
                x1 = (x_ref[0].astype(f32) + (attn + b_out[...])).astype(bf16)
                x1_ref[0] = x1
                xh, _ = ln_stats(x1.astype(f32))
                h2_ref[0] = (xh * gain2[...] + bias2[...]).astype(bf16)

            for k in range(1, NS):
                @pl.when((s == k - 1) & (g == TP - 2))
                def _():
                    x_a2a.finish(k)

        seq = pl.BlockSpec((1, S, D), lambda s, g: (s, 0, 0))
        pair = lambda n: pl.BlockSpec((1, 1, n, S), lambda s, g: (s, g, 0, 0))
        pltpu.emit_pipeline(body, grid=(NS, TP), in_specs=[seq], out_specs=[pair(R3), pair(4), pair(PW), seq, seq])(
            r.xs, r.qkv, r.ml, r.o, r.x1, r.h2)

    pl.run_scoped(attn_fwd, vm(TP, R3, D, dtype=bf16), vm(TP, PW, D, dtype=bf16), vm(S, D, dtype=bf16), vm(D, S, dtype=bf16))

    def mlp(h2_v, dy_v, yacc, wu_v, wd_v, acc):
        rs = GradScatter(pc, acc, r.landing, r.m_stage, r.m_r1, r.m_r2, r.m_sem, r.free)
        slot_at = lambda i: lax.rem(i + 6, TP)
        cps = load_all([(r.h2.at[s], h2_v.at[pl.ds(s * S, S)]) for s in range(NS)], r.tmp)
        for s in range(NS):
            dy_a2a.finish(s)
        cps += [pltpu.make_async_copy(r.dys.at[s], dy_v.at[pl.ds(s * S, S)], r.tmp.at[NS + s]) for s in range(NS)]
        for cp in cps[NS:]:
            cp.start()

        def weights(slot, b):
            return (pltpu.make_async_copy(r.wu_all.at[slot], wu_v.at[b], r.w_sem.at[0, b]),
                    pltpu.make_async_copy(r.wd_all.at[slot], wd_v.at[b], r.w_sem.at[1, b]))

        def fetch(i):
            slot = slot_at(i)

            @pl.when(lax.rem(slot, 2) != pc.c)
            def _():
                g_wu.arrived(slot)
                g_wd.arrived(slot)

            for cp in weights(slot, lax.rem(i, 2)):
                cp.start()

        fetch(jnp.int32(0))
        for cp in cps:
            cp.wait()

        def step(n, carry):
            i, t = lax.div(n, NT), lax.rem(n, NT)
            b = lax.rem(i, 2)
            slot = slot_at(i)

            @pl.when(t == 0)
            def _():
                for cp in weights(slot, b):
                    cp.wait()

            @pl.when((t == NT - 1) & (i < TP - 1))
            def _():
                fetch(i + 1)

            rows = pl.ds(pl.multiple_of(t * TT, TT), TT)
            h2, dy = h2_v[rows, :], dy_v[rows, :]
            wu, wd = wu_v[b], wd_v[b]
            bias = r.bs_all[slot]
            bias = jnp.concatenate([bias[4 + k:5 + k] for k in range(FB // 128)], axis=1)
            pre = nn(h2, wu) + bias
            d_act = nt(dy, wd)
            cdf = 0.5 * (1.0 + lax.erf(pre * INV_SQRT2))
            act = (pre * cdf).astype(bf16)
            d_pre = d_act * (cdf + pre * jnp.exp(-0.5 * pre * pre) * INV_SQRT_2PI)
            d_pre_b = d_pre.astype(bf16)
            yp = nn(act, wd)
            dp = nt(d_pre_b, wu)
            gd = tn(act, dy)
            gu = tn(d_pre_b, h2)
            gb = over_rows(jnp.sum, d_pre)

            @pl.when(i == 0)
            def _():
                yacc[rows, :] = yp
                r.dacc[rows, :] = dp

            @pl.when(i > 0)
            def _():
                yacc[rows, :] += yp
                r.dacc[rows, :] += dp

            @pl.when(t == 0)
            def _():
                acc[b, 0:FB, :] = gd
                acc[b, FB:2 * FB, :] = gu
                r.gbu[slot] = gb

            @pl.when(t > 0)
            def _():
                acc[b, 0:FB, :] += gd
                acc[b, FB:2 * FB, :] += gu
                r.gbu[slot] += gb

            @pl.when(t == NT - 1)
            def _():
                rs.block_done(slot, b, i >= 2)

            @pl.when((t == 0) & (i > 0))
            def _():
                rs.settle(slot_at(i - 1), 1 - b, True)

            for when, hops in ((2, ("forward_a", "start_b")), (5, ("last",)), (9, ("forward_b",))):
                @pl.when(n == when)
                def _():
                    for hop in hops:
                        for gather in (g_wu, g_wd):
                            getattr(gather, hop)()

            return carry

        lax.fori_loop(0, TP * NT, step, 0)
        cps = load_all([(r.x1.at[s], h2_v.at[pl.ds(s * S, S)]) for s in range(NS)], r.tmp)
        stores = []
        for s in range(NS):
            rows = pl.ds(s * S, S)
            cps[s].wait()
            dy_v[rows, :] = (h2_v[rows, :].astype(f32) + (yacc[rows, :] + b_down[...])).astype(bf16)
            cp = pltpu.make_async_copy(dy_v.at[rows], r.y_seq.at[s], r.tmp.at[NS + s])
            cp.start()
            stores.append(cp)
        for s in range(NS):
            stores[s].wait()
            y_a2a.start(s)
        last = jnp.int32(TP - 1)
        rs.settle(slot_at(last), lax.rem(last, 2), True)

    tok = vm(NS * S, D, dtype=bf16)
    pl.run_scoped(mlp, tok, tok, vm(NS * S, D), vm(2, D, FB, dtype=bf16), vm(2, FB, D, dtype=bf16), vm(2, 2 * FB, D))

    rs_m = GradScatter(pc, None, None, r.m_stage, r.m_r1, r.m_r2, r.m_sem, r.free)
    rs_a = GradScatter(pc, None, None, r.a_stage, r.a_r1, r.a_r2, r.a_sem, r.free)

    def attn_bwd(h1_s, do_s, go_a, gb_a):
        gx_a2a = AllToAll(pc, r.gx_out, h1_s, r.gx_ss, r.gx_rs, False)

        def open_bwd(wo_v):
            wo_cp = pltpu.make_async_copy(r.wo_all, wo_v, r.tmp.at[0])
            wo_cp.start()
            wo_cp.wait()
            r.va[...] = jnp.zeros_like(r.va)

            def body(x_ref, x1_ref, dy_ref, o_ref):
                s = pl.program_id(0)
                rows = pl.ds(pl.multiple_of(s * S, S), S)
                dy, dh2 = dy_ref[0].astype(f32), r.dacc[rows, :]
                xh2, inv2 = ln_stats(x1_ref[0].astype(f32))
                d = dy + ln_grad(dh2, xh2, inv2, gain2[...])
                r.dacc[rows, :] = d
                db = d.astype(bf16)
                r.va[0:1, :] += over_rows(jnp.sum, dy)
                r.va[1:2, :] += over_rows(jnp.sum, dh2 * xh2)
                r.va[2:3, :] += over_rows(jnp.sum, dh2)
                r.va[3:4, :] += over_rows(jnp.sum, d)
                xh, _ = ln_stats(x_ref[0].astype(f32))
                h1_s[s] = (xh * gain1[...] + bias1[...]).astype(bf16)
                do_s[s] = nt(wo_v[...].reshape(TP * PW, D), db).astype(bf16)
                go = nn(o_ref[0].reshape(TP * PW, S), db)

                @pl.when(s == 0)
                def _():
                    go_a[...] = go

                @pl.when(s > 0)
                def _():
                    go_a[...] += go

            seq = pl.BlockSpec((1, S, D), lambda s: (s, 0, 0))
            pltpu.emit_pipeline(body, grid=(NS,), in_specs=[seq, seq, seq, pl.BlockSpec((1, TP, PW, S), lambda s: (s, 0, 0, 0))])(
                r.xs, r.x1, r.dys, r.o)

        pl.run_scoped(open_bwd, vm(TP, PW, D, dtype=bf16))
        def heads(dq_s, wq_v):
            wq_cp = pltpu.make_async_copy(r.wq_all, wq_v, r.tmp.at[1])
            wq_cp.start()

            def pairs(acc, buf):
                rs = GradScatter(pc, acc, r.landing.at[pl.ds(0, R3 + PW)], r.a_stage, r.a_r1, r.a_r2, r.a_sem, r.free)

                def body(qkv_ref, ml_ref):
                    g, s = pl.program_id(0), pl.program_id(1)
                    b = lax.rem(g, 2)
                    cos, sin = r.cos[...], r.sin[...]
                    ok = key_mask(r.mask[s])

                    def rot_back(t):
                        a, b = t[:HH], t[HH:]
                        return jnp.concatenate([a * cos + b * sin, b * cos - a * sin], axis=0)

                    base = pl.multiple_of(g * R3, PW)
                    for h in range(2):
                        lo = h * HD
                        q = qkv_ref[0, 0, lo:lo + HD, :]
                        k = qkv_ref[0, 0, PW + lo:PW + lo + HD, :]
                        v = qkv_ref[0, 0, 2 * PW + lo:2 * PW + lo + HD, :]
                        do = do_s[s, pl.ds(pl.multiple_of(g * PW + lo, HD), HD), :]
                        sc = masked_scores(q, k, ok)
                        p = jnp.exp(sc - ml_ref[0, 0, h:h + 1, :]) * ml_ref[0, 0, 2 + h:3 + h, :]
                        dp = tn(v, do)
                        ds = (p * (dp - over_rows(jnp.sum, dp * p))).astype(bf16)
                        dv = nt(do, p.astype(bf16))
                        dk = rot_back(nt(q, ds))
                        dq = rot_back(nn(k, ds)) * QS
                        for j, t in enumerate((dq, dk, dv)):
                            at = pl.ds(base + j * PW + lo, HD)
                            dq_s[s, at, :] = t.astype(bf16)
                            tot = over_cols(jnp.sum, t)

                            @pl.when(s == 0)
                            def _():
                                gb_a[at, :] = tot

                            @pl.when(s > 0)
                            def _():
                                gb_a[at, :] += tot

                    gq = nn(dq_s[s, pl.ds(base, R3), :], h1_s[s])

                    @pl.when(s == 0)
                    def _():
                        acc[b, 0:R3, :] = gq
                        acc[b, R3:R3 + PW, :] = go_a[pl.ds(pl.multiple_of(g * PW, PW), PW), :]

                    @pl.when(s > 0)
                    def _():
                        acc[b, 0:R3, :] += gq

                    @pl.when(s == NS - 1)
                    def _():
                        rs.block_done(g, b, True)

                    @pl.when((s == 2) & (g > 0))
                    def _():
                        rs.settle(g - 1, 1 - b, g < TP - 1)

                    @pl.when((s == 0) & (g == 3))
                    def _():
                        rs_m.second([buf, r.landing.at[pl.ds(FB, FB)]], r.chunk)

                pair = lambda n: pl.BlockSpec((1, 1, n, S), lambda g, s: (s, g, 0, 0))
                pltpu.emit_pipeline(body, grid=(TP, NS), in_specs=[pair(R3), pair(4)])(r.qkv, r.ml)
                last = jnp.int32(TP - 1)
                rs.settle(last, lax.rem(last, 2), False)

            pl.run_scoped(pairs, vm(2, R3 + PW, D), vm(FB, D))
            wq_cp.wait()

            def close_bwd(x_ref):
                s = pl.program_id(0)
                rows = pl.ds(pl.multiple_of(s * S, S), S)
                dh1 = tn(dq_s[s], wq_v[...].reshape(TP * R3, D))
                xh, inv = ln_stats(x_ref[0].astype(f32))
                r.va[4:5, :] += over_rows(jnp.sum, dh1 * xh)
                r.va[5:6, :] += over_rows(jnp.sum, dh1)
                h1_s[s] = (r.dacc[rows, :] + ln_grad(dh1, xh, inv, gain1[...])).astype(bf16)
                gx_a2a.start(s)
                gx_a2a.local_out(s, h1_s).start()

            pltpu.emit_pipeline(close_bwd, grid=(NS,), in_specs=[pl.BlockSpec((1, S, D), lambda s: (s, 0, 0))])(r.xs)

        pl.run_scoped(heads, vm(NS, TP * R3, S, dtype=bf16), vm(TP, R3, D, dtype=bf16))

        for g in range(TP):
            r.msg[g] = r.va[...]
            for j in range(3):
                cols = jnp.broadcast_to(gb_a[g * R3 + j * PW:g * R3 + (j + 1) * PW, :], (PW, 128))
                r.msg[g, 6:7, j * PW:(j + 1) * PW] = cols.T[0:1, :]
            r.msg[g, 6:7, R3:R3 + FB] = r.gbu[g]
        small = [remote(r.msg.at[pc.slot_of(m)], r.msgs.at[pc.me], r.s_ss.at[m], r.s_rs.at[m], pc.peer(m)) for m in range(1, TP)]
        for cp in small:
            cp.start()
        own = pltpu.make_async_copy(r.msg.at[pc.slot_of(0)], r.msgs.at[pc.me], r.s_ss.at[0])
        own.start()

        def tail(bufs, act_v, turned):
            b0, b1, b2 = (bufs.at[i] for i in range(3))
            rs_a.second([b0, b1], r.chunk)
            y_own = [(pltpu.make_async_copy(r.y_seq.at[s, y_a2a._rows(pc.me)], act_v.at[s], r.tmp.at[s]),
                      pltpu.make_async_copy(act_v.at[s], r.y_out.at[pc.me * NS + s], r.tmp.at[NS + s])) for s in range(NS)]
            for load, _ in y_own:
                load.start()
            for load, store in y_own:
                load.wait()
                store.start()
            own.wait()
            for m, cp in enumerate(small):
                cp.wait_send()
                wait_for(r.msgs.at[pc.peer(m + 1)], r.s_rs.at[m + 1])
            total = r.msgs[0]
            for j in range(1, TP):
                total = total + r.msgs[j]
            r.small[...] = total
            for g in (g_bs, g_wq, g_wo, g_wu, g_wd):
                g.sent()
            for _, store in y_own:
                store.wait()
            rs_m.finish()
            for p in range(2):
                half = pl.ds(p * FB, FB)
                cps = load_all([(r.m_stage.at[3, half], b0), (r.m_r1.at[0, half], b1), (r.m_r2.at[half], b2)], r.tmp)
                for cp in cps:
                    cp.wait()
                row_add(b0, [b1, b2])
                if p == 0:
                    cp = pltpu.make_async_copy(b0, r.gd, r.tmp.at[0])
                else:
                    for k in range(D // FB):
                        cols = slice(k * FB, (k + 1) * FB)
                        turned[cols, :] = b0[:, cols].T
                    cp = pltpu.make_async_copy(turned, r.gu, r.tmp.at[0])
                cp.start()
                cp.wait()
            for s in range(NS):
                y_a2a.finish(s)
            for s in range(NS):
                gx_a2a.local_out(s, h1_s).wait()
                gx_a2a.finish(s)
            rs_a.finish()

        pl.run_scoped(tail, vm(3, FB, D), vm(NS, SL, D, dtype=bf16), vm(D, FB))

    seqs = vm(NS, S, D, dtype=bf16)
    pl.run_scoped(attn_bwd, seqs, vm(NS, D, S, dtype=bf16), vm(D, D), vm(TP * R3, 1))


def layer_call(*args):
    in_vmem = IN_NAMES[IN_NAMES.index("bqkv"):]
    vmem = pl.BlockSpec(memory_space=pltpu.VMEM)
    out = pl.pallas_call(
        layer_kernel,
        in_specs=[vmem if n in in_vmem else ANY for n in IN_NAMES],
        out_specs=[vmem if n == "small" else ANY for n in OUT_SHAPES],
        out_shape=[sds(*v) for v in OUT_SHAPES.values()],
        scratch_shapes=list(SCRATCH.values()),
        compiler_params=pltpu.CompilerParams(collective_id=0, has_side_effects=True, vmem_limit_bytes=VMEM_LIMIT),
        name="layer",
    )(*args)
    return out[:8]


FINAL = {"y": ((TP * NS, SL, D), bf16), "gx": ((TP * NS, SL, D), bf16), "gd": ((FB, D), f32), "gu": ((D, FB), f32),
         "gq": ((R3, D), f32), "go": ((PW, D), f32), "gbq": ((3, 2, HD), f32), "gbu": ((1, FB), f32)}
N_VEC = 6


def final_kernel(y_in, gx_in, small, gd_in, gu_in, stage, r1, r2, *refs):
    outs, vecs, refs = Refs(FINAL, refs[:len(FINAL)]), refs[len(FINAL):len(FINAL) + N_VEC], refs[len(FINAL) + N_VEC:]
    act, gv, sums, ld, st = refs
    n = act.shape[1]
    size = TP * NS // n
    moves = []
    terms = (stage.at[3], r1.at[0], r2)
    for p, (lo, rows, dst) in enumerate(((0, R3, outs.gq), (R3, PW, outs.go))):
        part = pl.ds(lo, rows)
        moves.append(([(t.at[part], sums.at[x, part]) for x, t in enumerate(terms)], sums.at[0, part], dst))
    for x, (src, dst) in enumerate(((y_in, outs.y), (gx_in, outs.gx))):
        for k in range(n):
            part = pl.ds(k * size, size)
            moves.append(([(src.at[part], act.at[x, k])], act.at[x, k], dst.at[part]))
    moves.append(([(gd_in, gv.at[0])], gv.at[0], outs.gd))
    moves.append(([(gu_in.at[pl.ds(0, FB)], gv.at[1, :, pl.ds(0, FB)])], gv.at[1, :, pl.ds(0, FB)], outs.gu.at[pl.ds(0, FB)]))
    moves.append(([(gu_in.at[pl.ds(FB, FB)], gv.at[1, :, pl.ds(FB, FB)])], gv.at[1, :, pl.ds(FB, FB)], outs.gu.at[pl.ds(FB, FB)]))
    loads = [[pltpu.make_async_copy(s, d, ld.at[i, x]) for x, (s, d) in enumerate(m[0])] for i, m in enumerate(moves)]
    stores = [pltpu.make_async_copy(m[1], m[2], st.at[i]) for i, m in enumerate(moves)]
    order = list(range(2, len(moves))) + [0, 1]
    for i in order:
        for cp in loads[i]:
            cp.start()
    for v, i in zip(vecs, (4, 5, 3, 1, 2, 0)):
        v[...] = small[i:i + 1, :]
    for i in range(3):
        for h in range(2):
            lo = i * PW + h * HD
            outs.gbq[i, h:h + 1, :] = small[6:7, lo:lo + HD]
    outs.gbu[...] = small[6:7, R3:R3 + FB]
    for i in order:
        for cp in loads[i]:
            cp.wait()
        for x in range(1, len(loads[i])):
            row_add(moves[i][1], [moves[i][0][x][1]])
        stores[i].start()
    for cp in stores:
        cp.wait()


def final_call(y, gx, small, gd, gu, stage, r1, r2):
    vmem = pl.BlockSpec(memory_space=pltpu.VMEM)
    n, moves = 4, 13
    return pl.pallas_call(
        final_kernel,
        in_specs=[ANY, ANY, vmem] + [ANY] * 5,
        out_specs=[vmem if k in ("gbq", "gbu") else ANY for k in FINAL] + [vmem] * N_VEC,
        out_shape=[sds(*v) for v in FINAL.values()] + [sds((1, D), f32)] * N_VEC,
        scratch_shapes=[vm(2, n, TP * NS // n, SL, D, dtype=bf16), vm(2, FB, D), vm(3, R3 + PW, D), DMA((moves, 3)), DMA((moves,))],
        compiler_params=pltpu.CompilerParams(vmem_limit_bytes=VMEM_LIMIT),
        name="results",
    )(y, gx, small, gd, gu, stage, r1, r2)


def rope_tables():
    inv_freq = (ROPE_BASE ** (-2.0 * np.arange(HH, dtype=np.float32) / HD)).astype(np.float32)
    angles = inv_freq[:, None] * np.arange(S, dtype=np.float32)[None, :]
    return np.cos(angles), np.sin(angles)


def solution(mesh):
    no = None
    act_spec = P('dp', 'tp', no)
    rep, part = P(no), P('dp')
    in_specs = (act_spec, act_spec, P('dp', no), rep, rep, P(no, no, 'tp', no), P(no, 'tp', no),
                P('tp', no, no), rep, rep, rep, P(no, 'tp'), P('tp'), P('tp', no), rep)
    out_specs = (act_spec, act_spec, part, part, P('dp', no, 'tp', no), P('dp', 'tp', no), P(('dp', 'tp'), no, no),
                 part, part, part, P('dp', 'tp'), P(('dp', 'tp')), P(('dp', 'tp'), no), part)

    def device_step(x_in, grad_y, pad_mask, ln1_gain, ln1_bias, w_qkv, b_qkv, w_out, b_out, ln2_gain, ln2_bias, w_up, b_up, w_down, b_down):
        assert x_in.shape == (TP * NS, SL, D) and w_qkv.shape == (3, D, 2, HD) and w_up.shape == (D, FB)
        row = lambda v: v.reshape(1, -1)
        wq = w_qkv.transpose(0, 2, 3, 1).reshape(R3, D)
        cos, sin = rope_tables()
        parts = layer_call(
            x_in, grad_y, wq, w_out.reshape(PW, D), w_up, w_down, b_qkv, row(b_up), pad_mask, cos, sin,
            row(ln1_gain), row(ln1_bias), row(ln2_gain), row(ln2_bias), row(b_out), row(b_down))
        y, gx, gd, gu, gq, go, gbq, gbu, *vecs = final_call(*parts)
        g1, b1, bo, g2, b2, bd = (v.reshape(D) for v in vecs)
        return (y, gx, g1, b1, gq.reshape(3, 2, HD, D).transpose(0, 3, 1, 2), gbq, go.reshape(2, HD, D), bo, g2, b2,
                gu, gbu.reshape(FB), gd, bd)

    return jax.shard_map(device_step, mesh=mesh, in_specs=in_specs, out_specs=out_specs, check_vma=False)
```

time: 2720 us -> 548 us (0.20)
  waiting for transfers between devices: 1950 us -> 0 us
  Pallas kernels: 0 us -> 546 us
  matrix products: 539 us -> 0 us
  other arithmetic: 184 us -> 0 us
    reduce_scatter x4 -> x0, waiting for transfers between devices: 1360 us -> none  [the longest x1 375 us: device_step(): lax.psum_scatter(attn_part, 'tp', scatter_dimension=1, tiled=True)]
    all_gather x4 -> x0, waiting for transfers between devices: 589 us -> none  [the longest x1 157 us: device_step(): lax.all_gather(h1_f.astype(jnp.bfloat16), 'tp', axis=1, tiled=True)]
    pallas_call x0 -> x2, Pallas kernels: none -> 546 us  [the longest x1 532 us: layer_call(): pl.pallas_call(layer_kernel, in_specs=[vmem if n in in_vmem else ANY for...]
    dot_general x17 -> x0, matrix products: 507 us -> none  [the longest x1 47.8 us: device_step(): jnp.einsum('bqhk,bshk->bhqs', d_attn_o, v_heads, preferred_element_type=j...]
    convert_element_type x6 -> x0, other arithmetic: 89 us -> none  [the longest x1 52.6 us: device_step(): (attn_probs * (d_probs - jnp.sum(d_probs * attn_probs, axis=-1, keepdims=...]
    reduce_sum x8 -> x0, other arithmetic: 50.9 us -> none  [the longest x1 13.2 us: device_step(): jnp.sum(d_x1, axis=(0, 1))]
    sub x1 -> x0, matrix products: 31.5 us -> none  [device_step(): attn_probs = jax.nn.softmax(jnp.where(key_ok, scores, NEG_LARGE), axis=-1)]
  transfers between devices with their start and end apart: 8 -> 0, of which waited for: 8 -> 0; matrix products, arithmetic and copies ran while one was open for 7% -> 0% of each run, Pallas kernels for 0% -> 0%
where the time goes in v2:
time: 548 us; the launch traced here: 547 us
  Pallas kernels  546 us (100%)
    pallas_call x1, Pallas kernels, layer_call(): pl.pallas_call(layer_kernel, in_specs=[vmem if n in in_vmem else ANY for...  532 us
    pallas_call x1, Pallas kernels, final_call(): pl.pallas_call(final_kernel, in_specs=[ANY, ANY, vmem] + [ANY] * 5, out_s...  14 us

profile of v2, /device:TPU:0, one launch (start us, length us, event | category | flops | bytes accessed | tf_op | source)
XLA Modules:
  0.0 547.1 jit_solution(14014611809251386320)
XLA Ops:
  0.7 532.2 %layer.1 = (bf16[32,64,1024]{2,1,0:T(8,128)(2,1)}, bf16[32,64,1024]{2,1,0:T(8,128)(2,1)}, f32[8,1024]{1,0:T(8,128)}, f32[512,1024]{1,0:T(8,128)}, f32[1024,512]{...) custom-call(bf16[32,64,1024]{2,1,0:T(8,128)(2,1)} %refs_0_.1, ...), custom_call_target="tpu_custom_call" | custom-call | tf_op jit(solution)/shard_map/layer/pallas_call | solution.py:791
  532.9 14.0 %results.1 = (bf16[32,64,1024]{2,1,0:T(8,128)(2,1)}, bf16[32,64,1024]{2,1,0:T(8,128)(2,1)}, f32[512,1024]{1,0:T(8,128)}, f32[1024,512]{1,0:T(8,128)}, f32[384,10...) custom-call(bf16[32,64,1024]{2,1,0:T(8,128)(2,1)} %get-tuple-element, ...), custom_call_target="tpu_custom_call" | custom-call | tf_op jit(solution)/shard_map/results/pallas_call | solution.py:851

commit v3 on v2

--- a/solution.py
+++ b/solution.py
@@ -1,3 +1,5 @@
+import functools
+
 import jax
 import jax.numpy as jnp
 import numpy as np
@@ -184,10 +186,13 @@
         return (pltpu.make_async_copy(self.src, buf, self.ss.at[7]),
                 pltpu.make_async_copy(buf, self.dst.at[6 + self.pc.c], self.rs.at[6 + self.pc.c]))
 
-    def arrived_rest(self):
-        for j in range(4):
+    def arrived_near(self):
+        for j in (0, 2, 3):
             self.arrived(2 * j + 1 - self.pc.c)
         self.arrived(6 + self.pc.c)
+
+    def arrived_far(self):
+        self.arrived(3 - self.pc.c)
 
     def sent(self):
         for cp in self._direct() + self._hop() + [self._last()]:
@@ -310,6 +315,11 @@
     return jnp.broadcast_to(row, (128, row.shape[1])).T[:, :1]
 
 
+def clear(*refs):
+    for ref in refs:
+        ref[...] = jnp.zeros(ref.shape, ref.dtype)
+
+
 def load_all(pairs, sem):
     cps = [pltpu.make_async_copy(s, d, sem.at[i]) for i, (s, d) in enumerate(pairs)]
     for cp in cps:
@@ -332,7 +342,7 @@
     "xs": ((NS, S, D), bf16), "dys": ((NS, S, D), bf16), "wq_all": ((TP, R3, D), bf16), "wo_all": ((TP, PW, D), bf16),
     "wu_all": ((TP, D, FB), bf16), "wd_all": ((TP, FB, D), bf16),
     "qkv": ((NS, TP, R3, S), bf16), "ml": ((NS, TP, 4, S), f32), "o": ((NS, TP, PW, S), bf16),
-    "x1": ((NS, S, D), bf16), "h2": ((NS, S, D), bf16), "y_seq": ((NS, S, D), bf16),
+    "x1": ((NS, S, D), bf16), "y_seq": ((NS, S, D), bf16),
 }
 DMA = pltpu.SemaphoreType.DMA
 SCRATCH = {
@@ -357,9 +367,9 @@
     pc = Place()
     for i in range(3):
         for h in range(2):
-            r.bs[i:i + 1, h * HD:(h + 1) * HD] = r.bqkv[i, h:h + 1, :]
-    for k in range(4):
-        r.bs[4 + k:5 + k, :] = r.bup[:, k * 128:(k + 1) * 128]
+            r.bs[pl.ds(i, 1), pl.ds(h * HD, HD)] = r.bqkv[i, pl.ds(h, 1), :]
+    for k in range(FB // PW):
+        r.bs[pl.ds(4 + k, 1), :] = r.bup[:, pl.ds(k * PW, PW)]
     entry_barrier(pc)
     x_a2a = AllToAll(pc, r.x_in, r.xs, r.x_ss, r.x_rs, True)
     dy_a2a = AllToAll(pc, r.dy_in, r.dys, r.dy_ss, r.dy_rs, True)
@@ -393,6 +403,14 @@
         x_a2a.finish(0)
         x_a2a.start(1)
         for g in first:
+            g.arrived_near()
+        for g in (g_wu, g_wd):
+            g.arrived(6 + pc.c)
+        local[0][1].wait()
+        local[1][1].wait()
+
+    def later_arrivals():
+        for g in (g_bs, g_wq, g_wo):
             g.last()
         for s in range(2, NS):
             x_a2a.start(s)
@@ -400,25 +418,27 @@
             dy_a2a.start(s)
         g_wu.start_a()
         g_wd.start_a()
-        for g in first:
-            g.arrived_rest()
-        for g in (g_wu, g_wd):
-            g.arrived(6 + pc.c)
-        local[0][1].wait()
-        local[1][1].wait()
+        for g in (g_bs, g_wq, g_wo):
+            g.arrived_far()
 
     act = vm(NS, SL, D, dtype=bf16)
     pl.run_scoped(arrivals, act, act, vm(R3, D, dtype=bf16), vm(PW, D, dtype=bf16), vm(D, FB, dtype=bf16), vm(FB, D, dtype=bf16))
 
-    def attn_fwd(wq_v, wo_v, h1_s, o_s):
-        cps = load_all([(r.wq_all, wq_v), (r.wo_all, wo_v)], r.tmp)
-        for cp in cps:
-            cp.wait()
-
-        def body(x_ref, qkv_ref, ml_ref, o_ref, x1_ref, h2_ref):
-            s, g = pl.program_id(0), pl.program_id(1)
-
-            @pl.when(g == 0)
+    def attn_fwd(h2_v, wq_v, wo_v, h1_s, o_s):
+        def fetch(*pairs):
+            for cp in load_all(pairs, r.tmp):
+                cp.wait()
+
+        fetch(*[(r.wq_all.at[pl.ds(k, 2)], wq_v.at[pl.ds(k, 2)]) for k in (6, 0, 4)])
+
+        def slot_at(n):
+            return jnp.where(n < 2, n + 6, jnp.where(n < 4, n - 2, jnp.where(n < 6, n, n - 4)))
+
+        def body(x_ref, qkv_ref, ml_ref, o_ref, x1_ref):
+            s, n = pl.program_id(0), pl.program_id(1)
+            g = slot_at(n)
+
+            @pl.when(n == 0)
             def _():
                 xh, _ = ln_stats(x_ref[0].astype(f32))
                 h1_s[...] = (xh * gain1[...] + bias1[...]).astype(bf16)
@@ -435,12 +455,10 @@
 
             for h in range(2):
                 lo = h * HD
-                q = rot(qkv[lo:lo + HD] * QS)
-                k = rot(qkv[PW + lo:PW + lo + HD])
-                v = qkv[2 * PW + lo:2 * PW + lo + HD].astype(bf16)
-                qkv_ref[0, 0, lo:lo + HD, :] = q
-                qkv_ref[0, 0, PW + lo:PW + lo + HD, :] = k
-                qkv_ref[0, 0, 2 * PW + lo:2 * PW + lo + HD, :] = v
+                at_q, at_k, at_v = (slice(j * PW + lo, j * PW + lo + HD) for j in range(3))
+                q, k, v = rot(qkv[at_q] * QS), rot(qkv[at_k]), qkv[at_v].astype(bf16)
+                for at, t in ((at_q, q), (at_k, k), (at_v, v)):
+                    qkv_ref[0, 0, at, :] = t
                 sc = masked_scores(q, k, ok)
                 m = over_rows(jnp.max, sc)
                 e = jnp.exp(sc - m)
@@ -452,36 +470,34 @@
                 o_ref[0, 0, lo:lo + HD, :] = o
                 o_s[pl.ds(pl.multiple_of(g * PW + lo, HD), HD), :] = o
 
-            @pl.when(g == TP - 1)
+            @pl.when((s == 0) & (n == 5))
+            def _():
+                later_arrivals()
+                fetch((r.wq_all.at[pl.ds(2, 2)], wq_v.at[pl.ds(2, 2)]), (r.wo_all, wo_v))
+
+            @pl.when(n == TP - 1)
             def _():
                 attn = tn(o_s[...], wo_v[...].reshape(TP * PW, D))
                 x1 = (x_ref[0].astype(f32) + (attn + b_out[...])).astype(bf16)
                 x1_ref[0] = x1
                 xh, _ = ln_stats(x1.astype(f32))
-                h2_ref[0] = (xh * gain2[...] + bias2[...]).astype(bf16)
+                h2_v[pl.ds(pl.multiple_of(s * S, S), S), :] = (xh * gain2[...] + bias2[...]).astype(bf16)
 
             for k in range(1, NS):
-                @pl.when((s == k - 1) & (g == TP - 2))
+                @pl.when((s == k - 1) & (n == TP - 2))
                 def _():
                     x_a2a.finish(k)
 
-        seq = pl.BlockSpec((1, S, D), lambda s, g: (s, 0, 0))
-        pair = lambda n: pl.BlockSpec((1, 1, n, S), lambda s, g: (s, g, 0, 0))
-        pltpu.emit_pipeline(body, grid=(NS, TP), in_specs=[seq], out_specs=[pair(R3), pair(4), pair(PW), seq, seq])(
-            r.xs, r.qkv, r.ml, r.o, r.x1, r.h2)
-
-    pl.run_scoped(attn_fwd, vm(TP, R3, D, dtype=bf16), vm(TP, PW, D, dtype=bf16), vm(S, D, dtype=bf16), vm(D, S, dtype=bf16))
-
-    def mlp(h2_v, dy_v, yacc, wu_v, wd_v, acc):
+        seq = pl.BlockSpec((1, S, D), lambda s, n: (s, 0, 0))
+        pair = lambda rows: pl.BlockSpec((1, 1, rows, S), lambda s, n: (s, slot_at(n), 0, 0))
+        pltpu.emit_pipeline(body, grid=(NS, TP), in_specs=[seq], out_specs=[pair(R3), pair(4), pair(PW), seq])(
+            r.xs, r.qkv, r.ml, r.o, r.x1)
+
+    def mlp(h2_v, dy_v, wu_v, wd_v, yacc, acc):
         rs = GradScatter(pc, acc, r.landing, r.m_stage, r.m_r1, r.m_r2, r.m_sem, r.free)
-        slot_at = lambda i: lax.rem(i + 6, TP)
-        cps = load_all([(r.h2.at[s], h2_v.at[pl.ds(s * S, S)]) for s in range(NS)], r.tmp)
-        for s in range(NS):
-            dy_a2a.finish(s)
-        cps += [pltpu.make_async_copy(r.dys.at[s], dy_v.at[pl.ds(s * S, S)], r.tmp.at[NS + s]) for s in range(NS)]
-        for cp in cps[NS:]:
-            cp.start()
-
+
+        def slot_at(i):
+            return jnp.where(i == 0, 6, jnp.where(i == 5, 7, i - 1 - lax.div(i, 6)))
         def weights(slot, b):
             return (pltpu.make_async_copy(r.wu_all.at[slot], wu_v.at[b], r.w_sem.at[0, b]),
                     pltpu.make_async_copy(r.wd_all.at[slot], wd_v.at[b], r.w_sem.at[1, b]))
@@ -498,6 +514,12 @@
                 cp.start()
 
         fetch(jnp.int32(0))
+        cps = []
+        for s in range(NS):
+            dy_a2a.finish(s)
+            cps.append(pltpu.make_async_copy(r.dys.at[s], dy_v.at[pl.ds(s * S, S)], r.tmp.at[s]))
+            cps[s].start()
+        clear(yacc, r.dacc, r.gbu)
         for cp in cps:
             cp.wait()
 
@@ -510,8 +532,9 @@
             def _():
                 for cp in weights(slot, b):
                     cp.wait()
-
-            @pl.when((t == NT - 1) & (i < TP - 1))
+                clear(acc.at[b])
+
+            @pl.when((t == NT - 1) & (i != 0) & (i != 2) & (i < TP - 1))
             def _():
                 fetch(i + 1)
 
@@ -519,55 +542,35 @@
             h2, dy = h2_v[rows, :], dy_v[rows, :]
             wu, wd = wu_v[b], wd_v[b]
             bias = r.bs_all[slot]
-            bias = jnp.concatenate([bias[4 + k:5 + k] for k in range(FB // 128)], axis=1)
+            bias = jnp.concatenate([bias[k:k + 1] for k in range(4, TP)], axis=1)
             pre = nn(h2, wu) + bias
             d_act = nt(dy, wd)
             cdf = 0.5 * (1.0 + lax.erf(pre * INV_SQRT2))
             act = (pre * cdf).astype(bf16)
             d_pre = d_act * (cdf + pre * jnp.exp(-0.5 * pre * pre) * INV_SQRT_2PI)
             d_pre_b = d_pre.astype(bf16)
-            yp = nn(act, wd)
-            dp = nt(d_pre_b, wu)
-            gd = tn(act, dy)
-            gu = tn(d_pre_b, h2)
-            gb = over_rows(jnp.sum, d_pre)
-
-            @pl.when(i == 0)
-            def _():
-                yacc[rows, :] = yp
-                r.dacc[rows, :] = dp
-
-            @pl.when(i > 0)
-            def _():
-                yacc[rows, :] += yp
-                r.dacc[rows, :] += dp
-
-            @pl.when(t == 0)
-            def _():
-                acc[b, 0:FB, :] = gd
-                acc[b, FB:2 * FB, :] = gu
-                r.gbu[slot] = gb
-
-            @pl.when(t > 0)
-            def _():
-                acc[b, 0:FB, :] += gd
-                acc[b, FB:2 * FB, :] += gu
-                r.gbu[slot] += gb
+            yacc[rows, :] += nn(act, wd)
+            r.dacc[rows, :] += nt(d_pre_b, wu)
+            acc[b, :FB, :] += tn(act, dy)
+            acc[b, FB:, :] += tn(d_pre_b, h2)
+            r.gbu[slot] += over_rows(jnp.sum, d_pre)
 
             @pl.when(t == NT - 1)
             def _():
-                rs.block_done(slot, b, i >= 2)
+                rs.block_done(slot, b, i > 2 * (1 - pc.c))
 
             @pl.when((t == 0) & (i > 0))
             def _():
                 rs.settle(slot_at(i - 1), 1 - b, True)
 
-            for when, hops in ((2, ("forward_a", "start_b")), (5, ("last",)), (9, ("forward_b",))):
+            for when, hops in ((1, ("forward_a", "start_b")), (4, ("last",)), (5, ()), (9, ("forward_b",))):
                 @pl.when(n == when)
                 def _():
                     for hop in hops:
                         for gather in (g_wu, g_wd):
                             getattr(gather, hop)()
+                    if when in (1, 5):
+                        fetch(i + 1)
 
             return carry
 
@@ -588,19 +591,24 @@
         rs.settle(slot_at(last), lax.rem(last, 2), True)
 
     tok = vm(NS * S, D, dtype=bf16)
-    pl.run_scoped(mlp, tok, tok, vm(NS * S, D), vm(2, D, FB, dtype=bf16), vm(2, FB, D, dtype=bf16), vm(2, 2 * FB, D))
+
+    def forward_and_mlp(h2_v, dy_v, wu_v, wd_v):
+        pl.run_scoped(functools.partial(attn_fwd, h2_v), vm(TP, R3, D, dtype=bf16), vm(TP, PW, D, dtype=bf16),
+                      vm(S, D, dtype=bf16), vm(D, S, dtype=bf16))
+        pl.run_scoped(functools.partial(mlp, h2_v, dy_v, wu_v, wd_v), vm(NS * S, D), vm(2, 2 * FB, D))
+
+    pl.run_scoped(forward_and_mlp, tok, tok, vm(2, D, FB, dtype=bf16), vm(2, FB, D, dtype=bf16))
 
     rs_m = GradScatter(pc, None, None, r.m_stage, r.m_r1, r.m_r2, r.m_sem, r.free)
-    rs_a = GradScatter(pc, None, None, r.a_stage, r.a_r1, r.a_r2, r.a_sem, r.free)
-
-    def attn_bwd(h1_s, do_s, go_a, gb_a):
+
+    def attn_bwd(h1_s, do_s, acc, gb_a):
         gx_a2a = AllToAll(pc, r.gx_out, h1_s, r.gx_ss, r.gx_rs, False)
 
         def open_bwd(wo_v):
             wo_cp = pltpu.make_async_copy(r.wo_all, wo_v, r.tmp.at[0])
             wo_cp.start()
             wo_cp.wait()
-            r.va[...] = jnp.zeros_like(r.va)
+            clear(r.va, acc, gb_a)
 
             def body(x_ref, x1_ref, dy_ref, o_ref):
                 s = pl.program_id(0)
@@ -617,31 +625,27 @@
                 xh, _ = ln_stats(x_ref[0].astype(f32))
                 h1_s[s] = (xh * gain1[...] + bias1[...]).astype(bf16)
                 do_s[s] = nt(wo_v[...].reshape(TP * PW, D), db).astype(bf16)
-                go = nn(o_ref[0].reshape(TP * PW, S), db)
-
-                @pl.when(s == 0)
-                def _():
-                    go_a[...] = go
-
-                @pl.when(s > 0)
-                def _():
-                    go_a[...] += go
+                acc[:, R3:, :] += nn(o_ref[0].reshape(TP * PW, S), db).reshape(TP, PW, D)
 
             seq = pl.BlockSpec((1, S, D), lambda s: (s, 0, 0))
             pltpu.emit_pipeline(body, grid=(NS,), in_specs=[seq, seq, seq, pl.BlockSpec((1, TP, PW, S), lambda s: (s, 0, 0, 0))])(
                 r.xs, r.x1, r.dys, r.o)
 
         pl.run_scoped(open_bwd, vm(TP, PW, D, dtype=bf16))
-        def heads(dq_s, wq_v):
+        n_half = NS // 2
+        rs = GradScatter(pc, acc, r.landing.at[pl.ds(0, R3 + PW)], r.a_stage, r.a_r1, r.a_r2, r.a_sem, r.free)
+
+        def slot_at(g):
+            return jnp.where(g < 4, lax.rem(g + 2, 4), g)
+
+        def heads(dq_s, wq_v, buf):
             wq_cp = pltpu.make_async_copy(r.wq_all, wq_v, r.tmp.at[1])
             wq_cp.start()
-
-            def pairs(acc, buf):
-                rs = GradScatter(pc, acc, r.landing.at[pl.ds(0, R3 + PW)], r.a_stage, r.a_r1, r.a_r2, r.a_sem, r.free)
-
+            for half in range(2):
                 def body(qkv_ref, ml_ref):
-                    g, s = pl.program_id(0), pl.program_id(1)
-                    b = lax.rem(g, 2)
+                    n, sh = pl.program_id(0), pl.program_id(1)
+                    g = slot_at(n)
+                    s = half * n_half + sh
                     cos, sin = r.cos[...], r.sin[...]
                     ok = key_mask(r.mask[s])
 
@@ -652,75 +656,58 @@
                     base = pl.multiple_of(g * R3, PW)
                     for h in range(2):
                         lo = h * HD
-                        q = qkv_ref[0, 0, lo:lo + HD, :]
-                        k = qkv_ref[0, 0, PW + lo:PW + lo + HD, :]
-                        v = qkv_ref[0, 0, 2 * PW + lo:2 * PW + lo + HD, :]
+                        q, k, v = (qkv_ref[0, 0, j * PW + lo:j * PW + lo + HD, :] for j in range(3))
                         do = do_s[s, pl.ds(pl.multiple_of(g * PW + lo, HD), HD), :]
                         sc = masked_scores(q, k, ok)
                         p = jnp.exp(sc - ml_ref[0, 0, h:h + 1, :]) * ml_ref[0, 0, 2 + h:3 + h, :]
                         dp = tn(v, do)
                         ds = (p * (dp - over_rows(jnp.sum, dp * p))).astype(bf16)
-                        dv = nt(do, p.astype(bf16))
-                        dk = rot_back(nt(q, ds))
+                        dv = nt(p.astype(bf16), do).T
+                        dk = rot_back(nt(ds, q).T)
                         dq = rot_back(nn(k, ds)) * QS
                         for j, t in enumerate((dq, dk, dv)):
                             at = pl.ds(base + j * PW + lo, HD)
-                            dq_s[s, at, :] = t.astype(bf16)
-                            tot = over_cols(jnp.sum, t)
-
-                            @pl.when(s == 0)
+                            dq_s[sh, at, :] = t.astype(bf16)
+                            gb_a[at, :] += over_cols(jnp.sum, t)
+
+                    acc[g, :R3, :] += nn(dq_s[sh, pl.ds(base, R3), :], h1_s[s])
+                    if half == 0:
+                        @pl.when((sh == 0) & (n == 1))
+                        def _():
+                            rs_m.second([buf, r.landing.at[pl.ds(FB, FB)]], r.chunk)
+                    else:
+                        @pl.when(sh == n_half - 1)
+                        def _():
+                            rs.block_done(g, g, True)
+
+                            @pl.when(n > 0)
                             def _():
-                                gb_a[at, :] = tot
-
-                            @pl.when(s > 0)
-                            def _():
-                                gb_a[at, :] += tot
-
-                    gq = nn(dq_s[s, pl.ds(base, R3), :], h1_s[s])
-
-                    @pl.when(s == 0)
-                    def _():
-                        acc[b, 0:R3, :] = gq
-                        acc[b, R3:R3 + PW, :] = go_a[pl.ds(pl.multiple_of(g * PW, PW), PW), :]
-
-                    @pl.when(s > 0)
-                    def _():
-                        acc[b, 0:R3, :] += gq
-
-                    @pl.when(s == NS - 1)
-                    def _():
-                        rs.block_done(g, b, True)
-
-                    @pl.when((s == 2) & (g > 0))
-                    def _():
-                        rs.settle(g - 1, 1 - b, g < TP - 1)
-
-                    @pl.when((s == 0) & (g == 3))
-                    def _():
-                        rs_m.second([buf, r.landing.at[pl.ds(FB, FB)]], r.chunk)
-
-                pair = lambda n: pl.BlockSpec((1, 1, n, S), lambda g, s: (s, g, 0, 0))
-                pltpu.emit_pipeline(body, grid=(TP, NS), in_specs=[pair(R3), pair(4)])(r.qkv, r.ml)
-                last = jnp.int32(TP - 1)
-                rs.settle(last, lax.rem(last, 2), False)
-
-            pl.run_scoped(pairs, vm(2, R3 + PW, D), vm(FB, D))
-            wq_cp.wait()
-
-            def close_bwd(x_ref):
-                s = pl.program_id(0)
-                rows = pl.ds(pl.multiple_of(s * S, S), S)
-                dh1 = tn(dq_s[s], wq_v[...].reshape(TP * R3, D))
-                xh, inv = ln_stats(x_ref[0].astype(f32))
-                r.va[4:5, :] += over_rows(jnp.sum, dh1 * xh)
-                r.va[5:6, :] += over_rows(jnp.sum, dh1)
-                h1_s[s] = (r.dacc[rows, :] + ln_grad(dh1, xh, inv, gain1[...])).astype(bf16)
-                gx_a2a.start(s)
-                gx_a2a.local_out(s, h1_s).start()
-
-            pltpu.emit_pipeline(close_bwd, grid=(NS,), in_specs=[pl.BlockSpec((1, S, D), lambda s: (s, 0, 0))])(r.xs)
-
-        pl.run_scoped(heads, vm(NS, TP * R3, S, dtype=bf16), vm(TP, R3, D, dtype=bf16))
+                                rs.settle(slot_at(n - 1), slot_at(n - 1), n < TP - 1)
+
+                pair = lambda rows: pl.BlockSpec((1, 1, rows, S), lambda n, sh: (half * n_half + sh, slot_at(n), 0, 0))
+                pltpu.emit_pipeline(body, grid=(TP, n_half), in_specs=[pair(R3), pair(4)])(r.qkv, r.ml)
+                if half == 0:
+                    wq_cp.wait()
+
+                def close_bwd(x_ref):
+                    sh = pl.program_id(0)
+                    s = half * n_half + sh
+                    rows = pl.ds(pl.multiple_of(s * S, S), S)
+                    dh1 = tn(dq_s[sh], wq_v[...].reshape(TP * R3, D))
+                    xh, inv = ln_stats(x_ref[0].astype(f32))
+                    r.va[4:5, :] += over_rows(jnp.sum, dh1 * xh)
+                    r.va[5:6, :] += over_rows(jnp.sum, dh1)
+                    h1_s[s] = (r.dacc[rows, :] + ln_grad(dh1, xh, inv, gain1[...])).astype(bf16)
+                    gx_a2a.start(s)
+                    gx_a2a.local_out(s, h1_s).start()
+
+                pltpu.emit_pipeline(close_bwd, grid=(n_half,),
+                                    in_specs=[pl.BlockSpec((1, S, D), lambda sh: (half * n_half + sh, 0, 0))])(r.xs)
+            last = jnp.int32(TP - 1)
+            rs.settle(last, last, False)
+            rs.second([buf, r.landing.at[pl.ds(FB, FB)]], r.chunk)
+
+        pl.run_scoped(heads, vm(n_half, TP * R3, S, dtype=bf16), vm(TP, R3, D, dtype=bf16), vm(FB, D))
 
         for g in range(TP):
             r.msg[g] = r.va[...]
@@ -736,7 +723,6 @@
 
         def tail(bufs, act_v, turned):
             b0, b1, b2 = (bufs.at[i] for i in range(3))
-            rs_a.second([b0, b1], r.chunk)
             y_own = [(pltpu.make_async_copy(r.y_seq.at[s, y_a2a._rows(pc.me)], act_v.at[s], r.tmp.at[s]),
                       pltpu.make_async_copy(act_v.at[s], r.y_out.at[pc.me * NS + s], r.tmp.at[NS + s])) for s in range(NS)]
             for load, _ in y_own:
@@ -744,14 +730,6 @@
             for load, store in y_own:
                 load.wait()
                 store.start()
-            own.wait()
-            for m, cp in enumerate(small):
-                cp.wait_send()
-                wait_for(r.msgs.at[pc.peer(m + 1)], r.s_rs.at[m + 1])
-            total = r.msgs[0]
-            for j in range(1, TP):
-                total = total + r.msgs[j]
-            r.small[...] = total
             for g in (g_bs, g_wq, g_wo, g_wu, g_wd):
                 g.sent()
             for _, store in y_own:
@@ -777,12 +755,20 @@
             for s in range(NS):
                 gx_a2a.local_out(s, h1_s).wait()
                 gx_a2a.finish(s)
-            rs_a.finish()
+            rs.finish()
+            own.wait()
+            for m, cp in enumerate(small):
+                cp.wait_send()
+                wait_for(r.msgs.at[pc.peer(m + 1)], r.s_rs.at[m + 1])
+            total = r.msgs[0]
+            for j in range(1, TP):
+                total = total + r.msgs[j]
+            r.small[...] = total
 
         pl.run_scoped(tail, vm(3, FB, D), vm(NS, SL, D, dtype=bf16), vm(D, FB))
 
     seqs = vm(NS, S, D, dtype=bf16)
-    pl.run_scoped(attn_bwd, seqs, vm(NS, D, S, dtype=bf16), vm(D, D), vm(TP * R3, 1))
+    pl.run_scoped(attn_bwd, seqs, vm(NS, D, S, dtype=bf16), vm(TP, R3 + PW, D), vm(TP * R3, 1))
 
 
 def layer_call(*args):
@@ -820,8 +806,9 @@
             part = pl.ds(k * size, size)
             moves.append(([(src.at[part], act.at[x, k])], act.at[x, k], dst.at[part]))
     moves.append(([(gd_in, gv.at[0])], gv.at[0], outs.gd))
-    moves.append(([(gu_in.at[pl.ds(0, FB)], gv.at[1, :, pl.ds(0, FB)])], gv.at[1, :, pl.ds(0, FB)], outs.gu.at[pl.ds(0, FB)]))
-    moves.append(([(gu_in.at[pl.ds(FB, FB)], gv.at[1, :, pl.ds(FB, FB)])], gv.at[1, :, pl.ds(FB, FB)], outs.gu.at[pl.ds(FB, FB)]))
+    for k in range(D // FB):
+        part = pl.ds(k * FB, FB)
+        moves.append(([(gu_in.at[part], gv.at[1, :, part])], gv.at[1, :, part], outs.gu.at[part]))
     loads = [[pltpu.make_async_copy(s, d, ld.at[i, x]) for x, (s, d) in enumerate(m[0])] for i, m in enumerate(moves)]
     stores = [pltpu.make_async_copy(m[1], m[2], st.at[i]) for i, m in enumerate(moves)]
     order = list(range(2, len(moves))) + [0, 1]
@@ -861,7 +848,7 @@
 
 def rope_tables():
     inv_freq = (ROPE_BASE ** (-2.0 * np.arange(HH, dtype=np.float32) / HD)).astype(np.float32)
-    angles = inv_freq[:, None] * np.arange(S, dtype=np.float32)[None, :]
+    angles = np.outer(inv_freq, np.arange(S, dtype=np.float32))
     return np.cos(angles), np.sin(angles)
 
 

time: 548 us -> 517 us (0.943)
  Pallas kernels: 546 us -> 516 us
    pallas_call x1, Pallas kernels: 532 us -> 502 us  [layer_call(): pl.pallas_call(layer_kernel, in_specs=[vmem if n in in_vmem else ANY for...]
where the time goes in v3:
time: 517 us; the launch traced here: 516 us
  Pallas kernels  516 us (100%)
    pallas_call x1, Pallas kernels, layer_call(): pl.pallas_call(layer_kernel, in_specs=[vmem if n in in_vmem else ANY for...  502 us
    pallas_call x1, Pallas kernels, final_call(): pl.pallas_call(final_kernel, in_specs=[ANY, ANY, vmem] + [ANY] * 5, out_s...  14 us

profile of v3, /device:TPU:0, one launch (start us, length us, event | category | flops | bytes accessed | tf_op | source)
XLA Modules:
  0.0 516.4 jit_solution(15355374853539661692)
XLA Ops:
  0.7 501.6 %layer.1 = (bf16[32,64,1024]{2,1,0:T(8,128)(2,1)}, bf16[32,64,1024]{2,1,0:T(8,128)(2,1)}, f32[8,1024]{1,0:T(8,128)}, f32[512,1024]{1,0:T(8,128)}, f32[1024,512]{...) custom-call(bf16[32,64,1024]{2,1,0:T(8,128)(2,1)} %refs_0_.1, ...), custom_call_target="tpu_custom_call" | custom-call | tf_op jit(solution)/shard_map/layer/pallas_call | solution.py:777
  502.2 14.0 %results.1 = (bf16[32,64,1024]{2,1,0:T(8,128)(2,1)}, bf16[32,64,1024]{2,1,0:T(8,128)(2,1)}, f32[512,1024]{1,0:T(8,128)}, f32[1024,512]{1,0:T(8,128)}, f32[384,10...) custom-call(bf16[32,64,1024]{2,1,0:T(8,128)(2,1)} %get-tuple-element, ...), custom_call_target="tpu_custom_call" | custom-call | tf_op jit(solution)/shard_map/results/pallas_call | solution.py:838

commit v4 on v3

--- a/solution.py
+++ b/solution.py
@@ -110,45 +110,46 @@
             src, dst = self.pos.at[dev * NS + s], self.seq.at[s, self._rows(pc.me)]
         else:
             src, dst = self.seq.at[s, self._rows(dev)], self.pos.at[pc.me * NS + s]
-        return remote(src, dst, self.ss.at[s, m], self.rs.at[s, m], dev)
+        return remote(src, dst, self.ss.at[s], self.rs.at[s], dev)
 
     def start(self, s):
         for m in (2, 3, 4, 5, 6, 7, 1):
             self._copy(s, m).start()
 
     def finish(self, s):
-        for m in range(1, TP):
-            self._copy(s, m).wait()
+        all_rows = self.seq.at[s, pl.ds(0, S - SL)]
+        wait_for(all_rows, self.ss.at[s])
+        wait_for(all_rows, self.rs.at[s])
 
     def local_in(self, buf):
         pc = self.pc
-        return (pltpu.make_async_copy(self.pos.at[pl.ds(pc.me * NS, NS)], buf, self.ss.at[0, 0]),
-                pltpu.make_async_copy(buf, self.seq.at[:, self._rows(pc.me)], self.rs.at[0, 0]))
+        return (pltpu.make_async_copy(self.pos.at[pl.ds(pc.me * NS, NS)], buf, self.ss.at[NS]),
+                pltpu.make_async_copy(buf, self.seq.at[:, self._rows(pc.me)], self.rs.at[NS]))
 
     def local_out(self, s, src):
-        return pltpu.make_async_copy(src.at[s, self._rows(self.pc.me)], self.pos.at[self.pc.me * NS + s], self.ss.at[s, 0])
+        return pltpu.make_async_copy(src.at[s, self._rows(self.pc.me)], self.pos.at[self.pc.me * NS + s], self.ss.at[NS])
 
 
 class Gather:
     def __init__(self, pc, src_ref, dst_ref, send_sem, recv_sem):
         self.pc, self.src, self.dst, self.ss, self.rs = pc, src_ref, dst_ref, send_sem, recv_sem
 
-    def _send(self, i, src, slot, dev):
-        return remote(src, self.dst.at[slot], self.ss.at[i], self.rs.at[slot], dev)
+    def _send(self, src, slot, dev):
+        return remote(src, self.dst.at[slot], self.ss, self.rs.at[slot], dev)
 
     def _direct(self):
         pc, c = self.pc, self.pc.c
-        return [self._send(0, self.src, c, pc.a), self._send(2, self.src, 6 + c, pc.partner),
-                self._send(1, self.src, 4 + c, pc.b)]
+        return [self._send(self.src, c, pc.a), self._send(self.src, 6 + c, pc.partner),
+                self._send(self.src, 4 + c, pc.b)]
 
     def _hop(self):
         pc, c = self.pc, self.pc.c
-        return [self._send(3, self.dst.at[c], 2 + c, pc.b), self._send(4, self.dst.at[c], c, pc.partner),
-                self._send(5, self.dst.at[4 + c], 4 + c, pc.partner)]
+        return [self._send(self.dst.at[c], 2 + c, pc.b), self._send(self.dst.at[c], c, pc.partner),
+                self._send(self.dst.at[4 + c], 4 + c, pc.partner)]
 
     def _last(self):
         pc, c = self.pc, self.pc.c
-        return self._send(6, self.dst.at[2 + c], 2 + c, pc.partner)
+        return self._send(self.dst.at[2 + c], 2 + c, pc.partner)
 
     def arrived(self, slot):
         wait_for(self.dst.at[slot], self.rs.at[slot])
@@ -183,7 +184,7 @@
         self._last().start()
 
     def local(self, buf):
-        return (pltpu.make_async_copy(self.src, buf, self.ss.at[7]),
+        return (pltpu.make_async_copy(self.src, buf, self.rs.at[TP]),
                 pltpu.make_async_copy(buf, self.dst.at[6 + self.pc.c], self.rs.at[6 + self.pc.c]))
 
     def arrived_near(self):
@@ -195,8 +196,7 @@
         self.arrived(3 - self.pc.c)
 
     def sent(self):
-        for cp in self._direct() + self._hop() + [self._last()]:
-            cp.wait_send()
+        wait_for(self.dst.at[pl.ds(0, TP - 1)], self.ss)
 
 
 def row_add(acc, others):
@@ -285,8 +285,16 @@
                 cp.wait()
         self._second().start()
 
+    def own_part(self, b0, b1, sem):
+        wait_for(self.r1.at[0], self.sem.at[4])
+        for cp in load_all([(self.stage.at[3], b0), (self.r1.at[0], b1)], sem):
+            cp.wait()
+        row_add(b0, [b1])
+        cp = pltpu.make_async_copy(b0, self.stage.at[3], sem.at[0])
+        cp.start()
+        cp.wait()
+
     def finish(self):
-        wait_for(self.r1.at[0], self.sem.at[4])
         for j in range(2):
             self._first(j).wait_send()
         self._second().wait()
@@ -333,11 +341,14 @@
 
 TT = 1024
 NT = NS * S // TT
-IN_NAMES = ("x_in", "dy_in", "wq", "wo", "wu", "wd", "bqkv", "bup", "pad", "cos", "sin", "gain1", "bias1", "gain2", "bias2",
-            "b_out", "b_down")
+SMALL = {
+    "bqkv": vm(3, 2, HD), "bup": vm(1, FB), "pad": vm(TP * NS, S, dtype=jnp.int32), "cos": vm(HH, S), "sin": vm(HH, S),
+    "gain1": vm(1, D), "bias1": vm(1, D), "gain2": vm(1, D), "bias2": vm(1, D), "b_out": vm(1, D), "b_down": vm(1, D),
+}
+IN_NAMES = ("x_in", "dy_in", "wq", "wo", "wu", "wd") + tuple("in_" + k for k in SMALL)
 OUT_SHAPES = {
-    "y_out": ((TP * NS, SL, D), bf16), "gx_out": ((TP * NS, SL, D), bf16), "small": ((8, D), f32), "gd": ((FB, D), f32), "gu": ((D, FB), f32),
-    "a_stage": ((4, R3 + PW, D), f32), "a_r1": ((2, R3 + PW, D), f32), "a_r2": ((R3 + PW, D), f32),
+    "y_out": ((TP * NS, SL, D), bf16), "gx_out": ((TP * NS, SL, D), bf16), "msgs": ((TP // 2, 8, D), f32), "gd": ((FB, D), f32), "gu": ((D, FB), f32),
+    "a_stage": ((4, R3 + PW, D), f32), "a_r2": ((R3 + PW, D), f32), "a_r1": ((2, R3 + PW, D), f32),
     "m_stage": ((4, 2 * FB, D), f32), "m_r1": ((2, 2 * FB, D), f32), "m_r2": ((2 * FB, D), f32),
     "xs": ((NS, S, D), bf16), "dys": ((NS, S, D), bf16), "wq_all": ((TP, R3, D), bf16), "wo_all": ((TP, PW, D), bf16),
     "wu_all": ((TP, D, FB), bf16), "wd_all": ((TP, FB, D), bf16),
@@ -345,13 +356,14 @@
     "x1": ((NS, S, D), bf16), "y_seq": ((NS, S, D), bf16),
 }
 DMA = pltpu.SemaphoreType.DMA
-SCRATCH = {
+SCRATCH = SMALL | {
+    "in_sem": DMA((len(SMALL),)),
     "bs_all": vm(TP, 8, 128), "bs": vm(8, 128), "mask": vm(NS, S, PW), "dacc": vm(NS * S, D), "landing": vm(2 * FB, D), "gbu": vm(TP, 1, FB), "va": vm(8, D),
-    "msg": vm(TP, 8, D), "msgs": vm(TP, 8, D),
+    "msg": vm(TP, 8, D), "msg_in": vm(TP, 8, D),
     "free": pltpu.SemaphoreType.REGULAR,
-    "x_ss": DMA((NS, 8)), "x_rs": DMA((NS, 8)), "dy_ss": DMA((NS, 8)), "dy_rs": DMA((NS, 8)),
-    "y_ss": DMA((NS, 8)), "y_rs": DMA((NS, 8)), "gx_ss": DMA((NS, 8)), "gx_rs": DMA((NS, 8)),
-    "g_ss": DMA((5, 8)), "g_rs": DMA((5, 8)), "m_sem": DMA((9,)), "a_sem": DMA((9,)), "s_ss": DMA((8,)), "s_rs": DMA((8,)),
+    "x_ss": DMA((NS + 1,)), "x_rs": DMA((NS + 1,)), "dy_ss": DMA((NS + 1,)), "dy_rs": DMA((NS + 1,)),
+    "y_ss": DMA((NS + 1,)), "y_rs": DMA((NS + 1,)), "gx_ss": DMA((NS + 1,)), "gx_rs": DMA((NS + 1,)),
+    "g_ss": DMA((5,)), "g_rs": DMA((5, TP + 1)), "m_sem": DMA((9,)), "a_sem": DMA((9,)), "s_ss": DMA((3,)), "s_rs": DMA((2,)),
     "tmp": DMA((8,)), "chunk": DMA((3, 4)), "w_sem": DMA((2, 2)),
 }
 
@@ -365,11 +377,7 @@
 def layer_kernel(*refs):
     r = Refs(IN_NAMES + tuple(OUT_SHAPES) + tuple(SCRATCH), refs)
     pc = Place()
-    for i in range(3):
-        for h in range(2):
-            r.bs[pl.ds(i, 1), pl.ds(h * HD, HD)] = r.bqkv[i, pl.ds(h, 1), :]
-    for k in range(FB // PW):
-        r.bs[pl.ds(4 + k, 1), :] = r.bup[:, pl.ds(k * PW, PW)]
+    small_in = load_all([(getattr(r, "in_" + k), getattr(r, k)) for k in SMALL], r.in_sem)
     entry_barrier(pc)
     x_a2a = AllToAll(pc, r.x_in, r.xs, r.x_ss, r.x_rs, True)
     dy_a2a = AllToAll(pc, r.dy_in, r.dys, r.dy_ss, r.dy_rs, True)
@@ -381,11 +389,16 @@
 
     def arrivals(b_x, b_dy, b_q, b_o, b_u, b_d):
         first = (g_bs, g_wq, g_wo)
-        for g in first:
+        for g in first[1:]:
             g.start()
         x_a2a.start(0)
-        own_bs = pltpu.make_async_copy(r.bs, r.bs_all.at[6 + pc.c], r.g_rs.at[0, 6 + pc.c])
-        own_bs.start()
+        for cp in small_in:
+            cp.wait()
+        for i in range(3):
+            for h in range(2):
+                r.bs[pl.ds(i, 1), pl.ds(h * HD, HD)] = r.bqkv[i, pl.ds(h, 1), :]
+        for k in range(FB // PW):
+            r.bs[pl.ds(4 + k, 1), :] = r.bup[:, pl.ds(k * PW, PW)]
         local = [x_a2a.local_in(b_x), dy_a2a.local_in(b_dy)]
         local += [g.local(b) for g, b in ((g_wq, b_q), (g_wo, b_o), (g_wu, b_u), (g_wd, b_d))]
         for load, _ in local:
@@ -393,12 +406,14 @@
         for s in range(NS):
             keys = jnp.broadcast_to(r.pad[pl.ds(pc.me * NS + s, 1), :].astype(f32), (PW, S))
             r.mask[s] = keys.T
+        g_bs.start()
+        pltpu.make_async_copy(r.bs, r.bs_all.at[6 + pc.c], r.g_rs.at[0, 6 + pc.c]).start()
         for load, store in local:
             load.wait()
             store.start()
-        for g in first:
+        for g in (g_wq, g_wo, g_bs):
             g.forward_a()
-        for g in first:
+        for g in (g_wq, g_wo, g_bs):
             g.forward_b()
         x_a2a.finish(0)
         x_a2a.start(1)
@@ -699,7 +714,9 @@
                     r.va[5:6, :] += over_rows(jnp.sum, dh1)
                     h1_s[s] = (r.dacc[rows, :] + ln_grad(dh1, xh, inv, gain1[...])).astype(bf16)
                     gx_a2a.start(s)
-                    gx_a2a.local_out(s, h1_s).start()
+                    cp = gx_a2a.local_out(s, h1_s)
+                    cp.start()
+                    cp.wait()
 
                 pltpu.emit_pipeline(close_bwd, grid=(n_half,),
                                     in_specs=[pl.BlockSpec((1, S, D), lambda sh: (half * n_half + sh, 0, 0))])(r.xs)
@@ -715,10 +732,15 @@
                 cols = jnp.broadcast_to(gb_a[g * R3 + j * PW:g * R3 + (j + 1) * PW, :], (PW, 128))
                 r.msg[g, 6:7, j * PW:(j + 1) * PW] = cols.T[0:1, :]
             r.msg[g, 6:7, R3:R3 + FB] = r.gbu[g]
-        small = [remote(r.msg.at[pc.slot_of(m)], r.msgs.at[pc.me], r.s_ss.at[m], r.s_rs.at[m], pc.peer(m)) for m in range(1, TP)]
+        pair = remote(r.msg, r.msg_in, r.s_ss.at[0], r.s_rs.at[0], pc.partner)
+        pair.start()
+        pair.wait()
+        r.msg_in[...] = r.msg_in[...] + r.msg[...]
+        chip = lax.div(pc.me, 2)
+        small = [remote(r.msg_in.at[pc.slot_of(m)], r.msgs.at[chip], r.s_ss.at[1], r.s_rs.at[1], pc.peer(m)) for m in (2, 4, 6)]
         for cp in small:
             cp.start()
-        own = pltpu.make_async_copy(r.msg.at[pc.slot_of(0)], r.msgs.at[pc.me], r.s_ss.at[0])
+        own = pltpu.make_async_copy(r.msg_in.at[pc.slot_of(0)], r.msgs.at[chip], r.s_ss.at[2])
         own.start()
 
         def tail(bufs, act_v, turned):
@@ -735,10 +757,10 @@
             for _, store in y_own:
                 store.wait()
             rs_m.finish()
+            wait_for(r.m_r1.at[0], r.m_sem.at[4])
             for p in range(2):
                 half = pl.ds(p * FB, FB)
-                cps = load_all([(r.m_stage.at[3, half], b0), (r.m_r1.at[0, half], b1), (r.m_r2.at[half], b2)], r.tmp)
-                for cp in cps:
+                for cp in load_all([(r.m_stage.at[3, half], b0), (r.m_r1.at[0, half], b1), (r.m_r2.at[half], b2)], r.tmp):
                     cp.wait()
                 row_add(b0, [b1, b2])
                 if p == 0:
@@ -750,20 +772,15 @@
                     cp = pltpu.make_async_copy(turned, r.gu, r.tmp.at[0])
                 cp.start()
                 cp.wait()
+            rs.own_part(b0, b1, r.tmp)
             for s in range(NS):
                 y_a2a.finish(s)
             for s in range(NS):
-                gx_a2a.local_out(s, h1_s).wait()
                 gx_a2a.finish(s)
             rs.finish()
             own.wait()
-            for m, cp in enumerate(small):
-                cp.wait_send()
-                wait_for(r.msgs.at[pc.peer(m + 1)], r.s_rs.at[m + 1])
-            total = r.msgs[0]
-            for j in range(1, TP):
-                total = total + r.msgs[j]
-            r.small[...] = total
+            for sem in (r.s_ss.at[1], r.s_rs.at[1]):
+                wait_for(r.msgs.at[pl.ds(0, len(small))], sem)
 
         pl.run_scoped(tail, vm(3, FB, D), vm(NS, SL, D, dtype=bf16), vm(D, FB))
 
@@ -772,78 +789,76 @@
 
 
 def layer_call(*args):
-    in_vmem = IN_NAMES[IN_NAMES.index("bqkv"):]
-    vmem = pl.BlockSpec(memory_space=pltpu.VMEM)
     out = pl.pallas_call(
         layer_kernel,
-        in_specs=[vmem if n in in_vmem else ANY for n in IN_NAMES],
-        out_specs=[vmem if n == "small" else ANY for n in OUT_SHAPES],
+        in_specs=[ANY] * len(IN_NAMES),
+        out_specs=[ANY] * len(OUT_SHAPES),
         out_shape=[sds(*v) for v in OUT_SHAPES.values()],
         scratch_shapes=list(SCRATCH.values()),
         compiler_params=pltpu.CompilerParams(collective_id=0, has_side_effects=True, vmem_limit_bytes=VMEM_LIMIT),
         name="layer",
     )(*args)
-    return out[:8]
+    return out[:7]
 
 
 FINAL = {"y": ((TP * NS, SL, D), bf16), "gx": ((TP * NS, SL, D), bf16), "gd": ((FB, D), f32), "gu": ((D, FB), f32),
          "gq": ((R3, D), f32), "go": ((PW, D), f32), "gbq": ((3, 2, HD), f32), "gbu": ((1, FB), f32)}
-N_VEC = 6
-
-
-def final_kernel(y_in, gx_in, small, gd_in, gu_in, stage, r1, r2, *refs):
-    outs, vecs, refs = Refs(FINAL, refs[:len(FINAL)]), refs[len(FINAL):len(FINAL) + N_VEC], refs[len(FINAL) + N_VEC:]
-    act, gv, sums, ld, st = refs
-    n = act.shape[1]
-    size = TP * NS // n
-    moves = []
-    terms = (stage.at[3], r1.at[0], r2)
-    for p, (lo, rows, dst) in enumerate(((0, R3, outs.gq), (R3, PW, outs.go))):
-        part = pl.ds(lo, rows)
-        moves.append(([(t.at[part], sums.at[x, part]) for x, t in enumerate(terms)], sums.at[0, part], dst))
-    for x, (src, dst) in enumerate(((y_in, outs.y), (gx_in, outs.gx))):
-        for k in range(n):
-            part = pl.ds(k * size, size)
-            moves.append(([(src.at[part], act.at[x, k])], act.at[x, k], dst.at[part]))
-    moves.append(([(gd_in, gv.at[0])], gv.at[0], outs.gd))
-    for k in range(D // FB):
-        part = pl.ds(k * FB, FB)
-        moves.append(([(gu_in.at[part], gv.at[1, :, part])], gv.at[1, :, part], outs.gu.at[part]))
-    loads = [[pltpu.make_async_copy(s, d, ld.at[i, x]) for x, (s, d) in enumerate(m[0])] for i, m in enumerate(moves)]
-    stores = [pltpu.make_async_copy(m[1], m[2], st.at[i]) for i, m in enumerate(moves)]
-    order = list(range(2, len(moves))) + [0, 1]
-    for i in order:
-        for cp in loads[i]:
+VECS = ("bd", "g2", "b2", "bo", "g1", "b1")
+FINAL |= {k: ((1, D), f32) for k in VECS}
+LATE = ("gbq", "gbu") + VECS
+
+
+def final_kernel(y_in, gx_in, msgs, gd_in, gu_in, stage, r2, *refs):
+    outs, refs = Refs(FINAL, refs), refs[len(FINAL):]
+    msg_v, y_v, gx_v, gd_v, gu_v, sums, ld, st = refs[:8]
+    late = Refs(LATE, refs[8:])
+    moves = [([(msgs, msg_v)], [])]
+    moves.append(([(t, sums.at[x]) for x, t in enumerate((stage.at[3], r2))],
+                  [(sums.at[0, pl.ds(0, R3)], outs.gq), (sums.at[0, pl.ds(R3, PW)], outs.go)]))
+    for src, buf, dst in ((gd_in, gd_v, outs.gd), (gu_in, gu_v, outs.gu), (y_in, y_v, outs.y), (gx_in, gx_v, outs.gx)):
+        moves.append(([(src, buf)], [(buf, dst)]))
+    copy = pltpu.make_async_copy
+    loads = [[copy(s, d, ld.at[i, x]) for x, (s, d) in enumerate(m[0])] for i, m in enumerate(moves)]
+    stores = [[copy(s, d, st.at[i, x]) for x, (s, d) in enumerate(m[1])] for i, m in enumerate(moves)]
+    for cps in loads:
+        for cp in cps:
             cp.start()
-    for v, i in zip(vecs, (4, 5, 3, 1, 2, 0)):
-        v[...] = small[i:i + 1, :]
-    for i in range(3):
-        for h in range(2):
-            lo = i * PW + h * HD
-            outs.gbq[i, h:h + 1, :] = small[6:7, lo:lo + HD]
-    outs.gbu[...] = small[6:7, R3:R3 + FB]
-    for i in order:
-        for cp in loads[i]:
+    for i, (cps, outward) in enumerate(zip(loads, stores)):
+        for cp in cps:
             cp.wait()
-        for x in range(1, len(loads[i])):
-            row_add(moves[i][1], [moves[i][0][x][1]])
-        stores[i].start()
-    for cp in stores:
-        cp.wait()
-
-
-def final_call(y, gx, small, gd, gu, stage, r1, r2):
-    vmem = pl.BlockSpec(memory_space=pltpu.VMEM)
-    n, moves = 4, 13
+        if i == 0:
+            small = msg_v[0]
+            for j in range(1, msg_v.shape[0]):
+                small = small + msg_v[j]
+            for j, k in enumerate(VECS):
+                getattr(late, k)[...] = small[j:j + 1, :]
+            for j in range(3):
+                for h in range(2):
+                    lo = j * PW + h * HD
+                    late.gbq[j, h:h + 1, :] = small[6:7, lo:lo + HD]
+            late.gbu[...] = small[6:7, R3:R3 + FB]
+        if i == 1:
+            row_add(sums.at[0], [sums.at[1]])
+        for cp in outward:
+            cp.start()
+    small_out = load_all([(getattr(late, k), getattr(outs, k)) for k in LATE], st.at[len(moves)])
+    for cps in stores + [small_out]:
+        for cp in cps:
+            cp.wait()
+
+
+def final_call(y, gx, msgs, gd, gu, stage, r2):
+    act = vm(*y.shape, dtype=bf16)
     return pl.pallas_call(
         final_kernel,
-        in_specs=[ANY, ANY, vmem] + [ANY] * 5,
-        out_specs=[vmem if k in ("gbq", "gbu") else ANY for k in FINAL] + [vmem] * N_VEC,
-        out_shape=[sds(*v) for v in FINAL.values()] + [sds((1, D), f32)] * N_VEC,
-        scratch_shapes=[vm(2, n, TP * NS // n, SL, D, dtype=bf16), vm(2, FB, D), vm(3, R3 + PW, D), DMA((moves, 3)), DMA((moves,))],
+        in_specs=[ANY] * 7,
+        out_specs=[ANY] * len(FINAL),
+        out_shape=[sds(*v) for v in FINAL.values()],
+        scratch_shapes=[vm(*msgs.shape), act, act, vm(FB, D), vm(D, FB), vm(2, R3 + PW, D), DMA((6, 2)), DMA((7, len(LATE)))]
+        + [vm(*FINAL[k][0]) for k in LATE],
         compiler_params=pltpu.CompilerParams(vmem_limit_bytes=VMEM_LIMIT),
         name="results",
-    )(y, gx, small, gd, gu, stage, r1, r2)
+    )(y, gx, msgs, gd, gu, stage, r2)
 
 
 def rope_tables():
@@ -870,7 +885,7 @@
             x_in, grad_y, wq, w_out.reshape(PW, D), w_up, w_down, b_qkv, row(b_up), pad_mask, cos, sin,
             row(ln1_gain), row(ln1_bias), row(ln2_gain), row(ln2_bias), row(b_out), row(b_down))
         y, gx, gd, gu, gq, go, gbq, gbu, *vecs = final_call(*parts)
-        g1, b1, bo, g2, b2, bd = (v.reshape(D) for v in vecs)
+        bd, g2, b2, bo, g1, b1 = (v.reshape(D) for v in vecs)
         return (y, gx, g1, b1, gq.reshape(3, 2, HD, D).transpose(0, 3, 1, 2), gbq, go.reshape(2, HD, D), bo, g2, b2,
                 gu, gbu.reshape(FB), gd, bd)
 

time: 517 us -> 508 us (0.983)
  Pallas kernels: 516 us -> 507 us
    pallas_call x2, Pallas kernels: 516 us -> 507 us  [the longest x1 496 us: layer_call(): pl.pallas_call(layer_kernel, in_specs=[ANY] * len(IN_NAMES), out_specs=[A...]
where the time goes in v4:
time: 508 us
  Pallas kernels  507 us (100%)
    pallas_call x1, Pallas kernels, layer_call(): pl.pallas_call(layer_kernel, in_specs=[ANY] * len(IN_NAMES), out_specs=[A...  496 us
    pallas_call x1, Pallas kernels, final_call(): pl.pallas_call(final_kernel, in_specs=[ANY] * 7, out_specs=[ANY] * len(FI...  11.2 us

profile of v4, /device:TPU:0, one launch (start us, length us, event | category | flops | bytes accessed | tf_op | source)
XLA Modules:
  0.0 507.7 jit_solution(2059526897113172336)
XLA Ops:
  0.7 495.6 %layer.1 = (bf16[32,64,1024]{2,1,0:T(8,128)(2,1)}, bf16[32,64,1024]{2,1,0:T(8,128)(2,1)}, f32[4,8,1024]{2,1,0:T(8,128)}, f32[512,1024]{1,0:T(8,128)}, f32[1024,5...) custom-call(bf16[32,64,1024]{2,1,0:T(8,128)(2,1)} %refs_0_.1, ...), custom_call_target="tpu_custom_call" | custom-call | tf_op jit(solution)/shard_map/layer/pallas_call | solution.py:792
  496.3 11.2 %results.1 = (bf16[32,64,1024]{2,1,0:T(8,128)(2,1)}, bf16[32,64,1024]{2,1,0:T(8,128)(2,1)}, f32[512,1024]{1,0:T(8,128)}, f32[1024,512]{1,0:T(8,128)}, f32[384,10...) custom-call(bf16[32,64,1024]{2,1,0:T(8,128)(2,1)} %get-tuple-element, ...), custom_call_target="tpu_custom_call" | custom-call | tf_op jit(solution)/shard_map/results/pallas_call | solution.py:852

commit v5 on v4

--- a/solution.py
+++ b/solution.py
@@ -113,7 +113,7 @@
         return remote(src, dst, self.ss.at[s], self.rs.at[s], dev)
 
     def start(self, s):
-        for m in (2, 3, 4, 5, 6, 7, 1):
+        for m in (*range(2, TP), 1):
             self._copy(s, m).start()
 
     def finish(self, s):
@@ -227,40 +227,42 @@
     def _second(self):
         return remote(self.stage.at[2], self.r2, self.sem.at[6], self.sem.at[7], self.pc.b)
 
-    def block_done(self, slot, b, needs_credit):
-        @pl.when(lax.rem(slot, 2) != self.pc.c)
+    def send_pair(self, b, needs_credit):
+        @pl.when(needs_credit)
         def _():
-            @pl.when(needs_credit)
-            def _():
-                pl.semaphore_wait(self.free, 1)
-
-            self._pair(b).start()
-
-    def settle(self, slot, b, gives_credit):
-        c = self.pc.c
-        own = lax.rem(slot, 2) == c
-        j = lax.div(slot, 2)
-
-        @pl.when(own)
+            pl.semaphore_wait(self.free, 1)
+
+        self._pair(b).start()
+
+    def sent_pair(self, b):
+        self._pair(b).wait_send()
+
+    def settle(self, j, b, landed, gives_credit):
+        landed()
+        row_add(self.acc.at[b], [self.landing])
+
+        @pl.when(gives_credit)
         def _():
-            wait_for(self.landing, self.sem.at[1])
-            row_add(self.acc.at[b], [self.landing])
-
-            @pl.when(gives_credit)
-            def _():
-                pl.semaphore_signal(self.free, inc=1, device_id={"tp": self.pc.partner}, device_id_type=MESH)
-
-            store = pltpu.make_async_copy(self.acc.at[b], self.stage.at[j], self.sem.at[8])
-            store.start()
-            store.wait()
-
-            @pl.when(j < 2)
-            def _():
-                self._first(j).start()
-
-        @pl.when(jnp.logical_not(own))
+            pl.semaphore_signal(self.free, inc=1, device_id={"tp": self.pc.partner}, device_id_type=MESH)
+
+        store = pltpu.make_async_copy(self.acc.at[b], self.stage.at[j], self.sem.at[8])
+        store.start()
+        store.wait()
+
+        @pl.when(j < 2)
         def _():
-            self._pair(b).wait_send()
+            self._first(j).start()
+
+    def landed(self):
+        wait_for(self.landing, self.sem.at[1])
+
+    def block_done(self, slot, b):
+        pl.when(lax.rem(slot, 2) != self.pc.c)(lambda: self.send_pair(b, True))
+
+    def later(self, slot, b, gives_credit):
+        own = lax.rem(slot, 2) == self.pc.c
+        pl.when(own)(lambda: self.settle(lax.div(slot, 2), b, self.landed, gives_credit))
+        pl.when(jnp.logical_not(own))(lambda: self.sent_pair(b))
 
     def second(self, bufs, chunk_sem):
         n = chunk_sem.shape[1]
@@ -349,7 +351,7 @@
 OUT_SHAPES = {
     "y_out": ((TP * NS, SL, D), bf16), "gx_out": ((TP * NS, SL, D), bf16), "msgs": ((TP // 2, 8, D), f32), "gd": ((FB, D), f32), "gu": ((D, FB), f32),
     "a_stage": ((4, R3 + PW, D), f32), "a_r2": ((R3 + PW, D), f32), "a_r1": ((2, R3 + PW, D), f32),
-    "m_stage": ((4, 2 * FB, D), f32), "m_r1": ((2, 2 * FB, D), f32), "m_r2": ((2 * FB, D), f32),
+    "m_r0": ((2 * FB, D), f32), "m_stage": ((4, 2 * FB, D), f32), "m_r1": ((2, 2 * FB, D), f32), "m_r2": ((2 * FB, D), f32),
     "xs": ((NS, S, D), bf16), "dys": ((NS, S, D), bf16), "wq_all": ((TP, R3, D), bf16), "wo_all": ((TP, PW, D), bf16),
     "wu_all": ((TP, D, FB), bf16), "wd_all": ((TP, FB, D), bf16),
     "qkv": ((NS, TP, R3, S), bf16), "ml": ((NS, TP, 4, S), f32), "o": ((NS, TP, PW, S), bf16),
@@ -363,7 +365,7 @@
     "free": pltpu.SemaphoreType.REGULAR,
     "x_ss": DMA((NS + 1,)), "x_rs": DMA((NS + 1,)), "dy_ss": DMA((NS + 1,)), "dy_rs": DMA((NS + 1,)),
     "y_ss": DMA((NS + 1,)), "y_rs": DMA((NS + 1,)), "gx_ss": DMA((NS + 1,)), "gx_rs": DMA((NS + 1,)),
-    "g_ss": DMA((5,)), "g_rs": DMA((5, TP + 1)), "m_sem": DMA((9,)), "a_sem": DMA((9,)), "s_ss": DMA((3,)), "s_rs": DMA((2,)),
+    "g_ss": DMA((5,)), "g_rs": DMA((5, TP + 1)), "m_sem": DMA((11,)), "a_sem": DMA((9,)), "s_ss": DMA((3,)), "s_rs": DMA((2,)),
     "tmp": DMA((8,)), "chunk": DMA((3, 4)), "w_sem": DMA((2, 2)),
 }
 
@@ -511,8 +513,27 @@
     def mlp(h2_v, dy_v, wu_v, wd_v, yacc, acc):
         rs = GradScatter(pc, acc, r.landing, r.m_stage, r.m_r1, r.m_r2, r.m_sem, r.free)
 
+        def is_own(i):
+            return (i == 2) | (i == 4) | (i == 5) | (i == 7)
+
+        def role_at(i):
+            return jnp.where((i == 0) | (i == 5), 3, jnp.where(i < 3, 0, jnp.where(i < 5, 1, 2)))
+
         def slot_at(i):
-            return jnp.where(i == 0, 6, jnp.where(i == 5, 7, i - 1 - lax.div(i, 6)))
+            return 2 * role_at(i) + jnp.where(is_own(i), pc.c, 1 - pc.c)
+
+        early = lambda b: remote(acc.at[b], r.m_r0, r.m_sem.at[9], r.m_sem.at[10], pc.partner)
+
+        def landed(i):
+            @pl.when(i == 5)
+            def _():
+                wait_for(r.m_r0, r.m_sem.at[10])
+                cp = pltpu.make_async_copy(r.m_r0, r.landing, r.tmp.at[0])
+                cp.start()
+                cp.wait()
+
+            pl.when(i != 5)(rs.landed)
+
         def weights(slot, b):
             return (pltpu.make_async_copy(r.wu_all.at[slot], wu_v.at[b], r.w_sem.at[0, b]),
                     pltpu.make_async_copy(r.wd_all.at[slot], wd_v.at[b], r.w_sem.at[1, b]))
@@ -520,7 +541,7 @@
         def fetch(i):
             slot = slot_at(i)
 
-            @pl.when(lax.rem(slot, 2) != pc.c)
+            @pl.when(jnp.logical_not(is_own(i)))
             def _():
                 g_wu.arrived(slot)
                 g_wd.arrived(slot)
@@ -570,13 +591,12 @@
             acc[b, FB:, :] += tn(d_pre_b, h2)
             r.gbu[slot] += over_rows(jnp.sum, d_pre)
 
-            @pl.when(t == NT - 1)
-            def _():
-                rs.block_done(slot, b, i > 2 * (1 - pc.c))
-
-            @pl.when((t == 0) & (i > 0))
-            def _():
-                rs.settle(slot_at(i - 1), 1 - b, True)
+            done = (t == NT - 1)
+            pl.when(done & (i == 0))(lambda: early(b).start())
+            pl.when(done & (i > 0) & jnp.logical_not(is_own(i)))(lambda: rs.send_pair(b, i > 1))
+            pl.when(done & is_own(i))(lambda: rs.settle(role_at(i), b, lambda: landed(i), i != 4))
+            pl.when((t == 0) & (i == 1))(lambda: early(1 - b).wait_send())
+            pl.when((t == 0) & (i > 1) & jnp.logical_not(is_own(i - 1)))(lambda: rs.sent_pair(1 - b))
 
             for when, hops in ((1, ("forward_a", "start_b")), (4, ("last",)), (5, ()), (9, ("forward_b",))):
                 @pl.when(n == when)
@@ -602,8 +622,6 @@
         for s in range(NS):
             stores[s].wait()
             y_a2a.start(s)
-        last = jnp.int32(TP - 1)
-        rs.settle(slot_at(last), lax.rem(last, 2), True)
 
     tok = vm(NS * S, D, dtype=bf16)
 
@@ -693,11 +711,11 @@
                     else:
                         @pl.when(sh == n_half - 1)
                         def _():
-                            rs.block_done(g, g, True)
+                            rs.block_done(g, g)
 
                             @pl.when(n > 0)
                             def _():
-                                rs.settle(slot_at(n - 1), slot_at(n - 1), n < TP - 1)
+                                rs.later(slot_at(n - 1), slot_at(n - 1), n < TP - 1)
 
                 pair = lambda rows: pl.BlockSpec((1, 1, rows, S), lambda n, sh: (half * n_half + sh, slot_at(n), 0, 0))
                 pltpu.emit_pipeline(body, grid=(TP, n_half), in_specs=[pair(R3), pair(4)])(r.qkv, r.ml)
@@ -721,7 +739,7 @@
                 pltpu.emit_pipeline(close_bwd, grid=(n_half,),
                                     in_specs=[pl.BlockSpec((1, S, D), lambda sh: (half * n_half + sh, 0, 0))])(r.xs)
             last = jnp.int32(TP - 1)
-            rs.settle(last, last, False)
+            rs.later(last, last, False)
             rs.second([buf, r.landing.at[pl.ds(FB, FB)]], r.chunk)
 
         pl.run_scoped(heads, vm(n_half, TP * R3, S, dtype=bf16), vm(TP, R3, D, dtype=bf16), vm(FB, D))

time: 508 us -> 504 us (level)
  no operation moved by 1% of the time
where the time goes in v5:
time: 504 us; the launch traced here: 503 us
  Pallas kernels  502 us (100%)
    pallas_call x1, Pallas kernels, layer_call(): pl.pallas_call(layer_kernel, in_specs=[ANY] * len(IN_NAMES), out_specs=[A...  491 us
    pallas_call x1, Pallas kernels, final_call(): pl.pallas_call(final_kernel, in_specs=[ANY] * 7, out_specs=[ANY] * len(FI...  11.2 us

profile of v5, /device:TPU:0, one launch (start us, length us, event | category | flops | bytes accessed | tf_op | source)
XLA Modules:
  0.0 503.3 jit_solution(18296924274253411796)
XLA Ops:
  0.7 491.2 %layer.1 = (bf16[32,64,1024]{2,1,0:T(8,128)(2,1)}, bf16[32,64,1024]{2,1,0:T(8,128)(2,1)}, f32[4,8,1024]{2,1,0:T(8,128)}, f32[512,1024]{1,0:T(8,128)}, f32[1024,5...) custom-call(bf16[32,64,1024]{2,1,0:T(8,128)(2,1)} %refs_0_.1, ...), custom_call_target="tpu_custom_call" | custom-call | tf_op jit(solution)/shard_map/layer/pallas_call | solution.py:810
  491.9 11.2 %results.1 = (bf16[32,64,1024]{2,1,0:T(8,128)(2,1)}, bf16[32,64,1024]{2,1,0:T(8,128)(2,1)}, f32[512,1024]{1,0:T(8,128)}, f32[1024,512]{1,0:T(8,128)}, f32[384,10...) custom-call(bf16[32,64,1024]{2,1,0:T(8,128)(2,1)} %get-tuple-element, ...), custom_call_target="tpu_custom_call" | custom-call | tf_op jit(solution)/shard_map/results/pallas_call | solution.py:870

commit v6 on v5

--- a/solution.py
+++ b/solution.py
@@ -30,6 +30,7 @@
 SL = 64
 QS = HD ** -0.5
 R3 = 3 * PW
+ROWS = 8
 
 
 def dg(a, b, ca, cb):
@@ -225,7 +226,9 @@
         return remote(self.stage.at[j], self.r1.at[j], self.sem.at[2 + j], self.sem.at[4 + j], self.pc.a)
 
     def _second(self):
-        return remote(self.stage.at[2], self.r2, self.sem.at[6], self.sem.at[7], self.pc.b)
+        rows = self.r2.shape[0]
+        src = self.stage.at[2, pl.ds(self.stage.shape[1] - rows, rows)]
+        return remote(src, self.r2, self.sem.at[6], self.sem.at[7], self.pc.b)
 
     def send_pair(self, b, needs_credit):
         @pl.when(needs_credit)
@@ -264,17 +267,19 @@
         pl.when(own)(lambda: self.settle(lax.div(slot, 2), b, self.landed, gives_credit))
         pl.when(jnp.logical_not(own))(lambda: self.sent_pair(b))
 
-    def second(self, bufs, chunk_sem):
+    def second(self, bufs, chunk_sem, lead=None):
         n = chunk_sem.shape[1]
         size = bufs[0].shape[0]
         rows = size // n
         part = lambda ref, k: ref.at[pl.ds(k * rows, rows)]
         wait_for(self.r1.at[1], self.sem.at[5])
-        for p in range(self.r2.shape[0] // size):
+        for p in range(self.stage.shape[1] // size):
             mine, theirs = (ref.at[pl.ds(p * size, size)] for ref in (self.stage.at[2], self.r1.at[1]))
             loads = [[pltpu.make_async_copy(part(src, k), part(buf, k), chunk_sem.at[x, k])
                       for x, (src, buf) in enumerate(zip((mine, theirs), bufs))] for k in range(n)]
-            stores = [pltpu.make_async_copy(part(bufs[0], k), part(mine, k), chunk_sem.at[2, k]) for k in range(n)]
+            to_lead = 0 if lead is None else lead.shape[0] // rows
+            stores = [pltpu.make_async_copy(part(bufs[0], k), part(lead if k < to_lead else mine, k), chunk_sem.at[2, k])
+                      for k in range(n)]
             for group in loads:
                 for cp in group:
                     cp.start()
@@ -322,7 +327,7 @@
 
 
 def column(row):
-    return jnp.broadcast_to(row, (128, row.shape[1])).T[:, :1]
+    return jnp.broadcast_to(row, (PW, row.shape[1])).T[:, :1]
 
 
 def clear(*refs):
@@ -349,8 +354,8 @@
 }
 IN_NAMES = ("x_in", "dy_in", "wq", "wo", "wu", "wd") + tuple("in_" + k for k in SMALL)
 OUT_SHAPES = {
-    "y_out": ((TP * NS, SL, D), bf16), "gx_out": ((TP * NS, SL, D), bf16), "msgs": ((TP // 2, 8, D), f32), "gd": ((FB, D), f32), "gu": ((D, FB), f32),
-    "a_stage": ((4, R3 + PW, D), f32), "a_r2": ((R3 + PW, D), f32), "a_r1": ((2, R3 + PW, D), f32),
+    "y_out": ((TP * NS, SL, D), bf16), "gx_out": ((TP * NS, SL, D), bf16), "msgs": ((TP // 2, ROWS, D), f32), "gd": ((FB, D), f32), "gu": ((D, FB), f32),
+    "a_stage": ((4, R3 + PW, D), f32), "a_r2": ((PW, D), f32), "gq_b": ((R3, D), f32), "a_r1": ((2, R3 + PW, D), f32),
     "m_r0": ((2 * FB, D), f32), "m_stage": ((4, 2 * FB, D), f32), "m_r1": ((2, 2 * FB, D), f32), "m_r2": ((2 * FB, D), f32),
     "xs": ((NS, S, D), bf16), "dys": ((NS, S, D), bf16), "wq_all": ((TP, R3, D), bf16), "wo_all": ((TP, PW, D), bf16),
     "wu_all": ((TP, D, FB), bf16), "wd_all": ((TP, FB, D), bf16),
@@ -360,13 +365,13 @@
 DMA = pltpu.SemaphoreType.DMA
 SCRATCH = SMALL | {
     "in_sem": DMA((len(SMALL),)),
-    "bs_all": vm(TP, 8, 128), "bs": vm(8, 128), "mask": vm(NS, S, PW), "dacc": vm(NS * S, D), "landing": vm(2 * FB, D), "gbu": vm(TP, 1, FB), "va": vm(8, D),
-    "msg": vm(TP, 8, D), "msg_in": vm(TP, 8, D),
+    "bs_all": vm(TP, ROWS, PW), "bs": vm(ROWS, PW), "mask": vm(NS, S, PW), "dacc": vm(NS * S, D), "landing": vm(2 * FB, D), "gbu": vm(TP, 1, FB), "va": vm(ROWS, D),
+    "msg": vm(TP, ROWS, D), "msg_in": vm(TP, ROWS, D),
     "free": pltpu.SemaphoreType.REGULAR,
     "x_ss": DMA((NS + 1,)), "x_rs": DMA((NS + 1,)), "dy_ss": DMA((NS + 1,)), "dy_rs": DMA((NS + 1,)),
     "y_ss": DMA((NS + 1,)), "y_rs": DMA((NS + 1,)), "gx_ss": DMA((NS + 1,)), "gx_rs": DMA((NS + 1,)),
     "g_ss": DMA((5,)), "g_rs": DMA((5, TP + 1)), "m_sem": DMA((11,)), "a_sem": DMA((9,)), "s_ss": DMA((3,)), "s_rs": DMA((2,)),
-    "tmp": DMA((8,)), "chunk": DMA((3, 4)), "w_sem": DMA((2, 2)),
+    "tmp": DMA((TP,)), "chunk": DMA((3, 4)), "w_sem": DMA((2, 2)),
 }
 
 
@@ -481,8 +486,9 @@
                 e = jnp.exp(sc - m)
                 li = 1.0 / over_rows(jnp.sum, e)
                 p = (e * li).astype(bf16)
-                ml_ref[0, 0, h:h + 1, :] = m
-                ml_ref[0, 0, 2 + h:3 + h, :] = li
+                ml = ml_ref.at[0, 0]
+                ml[h:h + 1, :] = m
+                ml[2 + h:3 + h, :] = li
                 o = nn(v, p).astype(bf16)
                 o_ref[0, 0, lo:lo + HD, :] = o
                 o_s[pl.ds(pl.multiple_of(g * PW + lo, HD), HD), :] = o
@@ -632,7 +638,7 @@
 
     pl.run_scoped(forward_and_mlp, tok, tok, vm(2, D, FB, dtype=bf16), vm(2, FB, D, dtype=bf16))
 
-    rs_m = GradScatter(pc, None, None, r.m_stage, r.m_r1, r.m_r2, r.m_sem, r.free)
+    rs_m = GradScatter(pc, r.landing, r.landing, r.m_stage, r.m_r1, r.m_r2, r.m_sem, r.free)
 
     def attn_bwd(h1_s, do_s, acc, gb_a):
         gx_a2a = AllToAll(pc, r.gx_out, h1_s, r.gx_ss, r.gx_rs, False)
@@ -689,10 +695,11 @@
                     base = pl.multiple_of(g * R3, PW)
                     for h in range(2):
                         lo = h * HD
-                        q, k, v = (qkv_ref[0, 0, j * PW + lo:j * PW + lo + HD, :] for j in range(3))
+                        qkv, ml = qkv_ref.at[0, 0], ml_ref.at[0, 0]
+                        q, k, v = (qkv[j * PW + lo:j * PW + lo + HD, :] for j in range(3))
                         do = do_s[s, pl.ds(pl.multiple_of(g * PW + lo, HD), HD), :]
                         sc = masked_scores(q, k, ok)
-                        p = jnp.exp(sc - ml_ref[0, 0, h:h + 1, :]) * ml_ref[0, 0, 2 + h:3 + h, :]
+                        p = jnp.exp(sc - ml[h:h + 1, :]) * ml[2 + h:3 + h, :]
                         dp = tn(v, do)
                         ds = (p * (dp - over_rows(jnp.sum, dp * p))).astype(bf16)
                         dv = nt(p.astype(bf16), do).T
@@ -740,14 +747,14 @@
                                     in_specs=[pl.BlockSpec((1, S, D), lambda sh: (half * n_half + sh, 0, 0))])(r.xs)
             last = jnp.int32(TP - 1)
             rs.later(last, last, False)
-            rs.second([buf, r.landing.at[pl.ds(FB, FB)]], r.chunk)
+            rs.second([buf, r.landing.at[pl.ds(FB, FB)]], r.chunk, r.gq_b)
 
         pl.run_scoped(heads, vm(n_half, TP * R3, S, dtype=bf16), vm(TP, R3, D, dtype=bf16), vm(FB, D))
 
         for g in range(TP):
             r.msg[g] = r.va[...]
             for j in range(3):
-                cols = jnp.broadcast_to(gb_a[g * R3 + j * PW:g * R3 + (j + 1) * PW, :], (PW, 128))
+                cols = jnp.broadcast_to(gb_a[g * R3 + j * PW:g * R3 + (j + 1) * PW, :], (PW, PW))
                 r.msg[g, 6:7, j * PW:(j + 1) * PW] = cols.T[0:1, :]
             r.msg[g, 6:7, R3:R3 + FB] = r.gbu[g]
         pair = remote(r.msg, r.msg_in, r.s_ss.at[0], r.s_rs.at[0], pc.partner)
@@ -816,11 +823,11 @@
         compiler_params=pltpu.CompilerParams(collective_id=0, has_side_effects=True, vmem_limit_bytes=VMEM_LIMIT),
         name="layer",
     )(*args)
-    return out[:7]
+    return out[:8]
 
 
 FINAL = {"y": ((TP * NS, SL, D), bf16), "gx": ((TP * NS, SL, D), bf16), "gd": ((FB, D), f32), "gu": ((D, FB), f32),
-         "gq": ((R3, D), f32), "go": ((PW, D), f32), "gbq": ((3, 2, HD), f32), "gbu": ((1, FB), f32)}
+         "go": ((PW, D), f32), "gbq": ((3, 2, HD), f32), "gbu": ((1, FB), f32)}
 VECS = ("bd", "g2", "b2", "bo", "g1", "b1")
 FINAL |= {k: ((1, D), f32) for k in VECS}
 LATE = ("gbq", "gbu") + VECS
@@ -831,8 +838,7 @@
     msg_v, y_v, gx_v, gd_v, gu_v, sums, ld, st = refs[:8]
     late = Refs(LATE, refs[8:])
     moves = [([(msgs, msg_v)], [])]
-    moves.append(([(t, sums.at[x]) for x, t in enumerate((stage.at[3], r2))],
-                  [(sums.at[0, pl.ds(0, R3)], outs.gq), (sums.at[0, pl.ds(R3, PW)], outs.go)]))
+    moves.append(([(t, sums.at[x]) for x, t in enumerate((stage.at[3, pl.ds(R3, PW)], r2))], [(sums.at[0], outs.go)]))
     for src, buf, dst in ((gd_in, gd_v, outs.gd), (gu_in, gu_v, outs.gu), (y_in, y_v, outs.y), (gx_in, gx_v, outs.gx)):
         moves.append(([(src, buf)], [(buf, dst)]))
     copy = pltpu.make_async_copy
@@ -872,9 +878,10 @@
         in_specs=[ANY] * 7,
         out_specs=[ANY] * len(FINAL),
         out_shape=[sds(*v) for v in FINAL.values()],
-        scratch_shapes=[vm(*msgs.shape), act, act, vm(FB, D), vm(D, FB), vm(2, R3 + PW, D), DMA((6, 2)), DMA((7, len(LATE)))]
+        scratch_shapes=[vm(*msgs.shape), act, act, vm(FB, D), vm(D, FB), vm(2, PW, D), DMA((6, 2)), DMA((7, len(LATE)))]
         + [vm(*FINAL[k][0]) for k in LATE],
         compiler_params=pltpu.CompilerParams(vmem_limit_bytes=VMEM_LIMIT),
+        cost_estimate=pl.CostEstimate(flops=10 ** 10, bytes_accessed=3 * 10 ** 7, transcendentals=0),
         name="results",
     )(y, gx, msgs, gd, gu, stage, r2)
 
@@ -902,7 +909,11 @@
         parts = layer_call(
             x_in, grad_y, wq, w_out.reshape(PW, D), w_up, w_down, b_qkv, row(b_up), pad_mask, cos, sin,
             row(ln1_gain), row(ln1_bias), row(ln2_gain), row(ln2_bias), row(b_out), row(b_down))
-        y, gx, gd, gu, gq, go, gbq, gbu, *vecs = final_call(*parts)
+        *parts, gq_b = parts
+        stage = parts[-2]
+        to_b = [(i, i ^ (4 - 2 * (i % 2))) for i in range(TP)]
+        gq = stage[-1, :R3] + lax.ppermute(gq_b, 'tp', to_b)
+        y, gx, gd, gu, go, gbq, gbu, *vecs = final_call(*parts)
         bd, g2, b2, bo, g1, b1 = (v.reshape(D) for v in vecs)
         return (y, gx, g1, b1, gq.reshape(3, 2, HD, D).transpose(0, 3, 1, 2), gbq, go.reshape(2, HD, D), bo, g2, b2,
                 gu, gbu.reshape(FB), gd, bd)

time: 504 us -> 500 us (level)
  Pallas kernels: 502 us -> 485 us
  waiting for transfers between devices: 0 us -> 9.18 us
    pallas_call x1, Pallas kernels: 491 us -> 475 us  [layer_call(): pl.pallas_call(layer_kernel, in_specs=[ANY] * len(IN_NAMES), out_specs=[A...]
    ppermute x0 -> x1, waiting for transfers between devices: none -> 9.18 us  [device_step(): gq = stage[-1, :R3] + lax.ppermute(gq_b, 'tp', to_b)]
  transfers between devices with their start and end apart: 0 -> 1, of which waited for: 0 -> 1; matrix products, arithmetic and copies ran while one was open for 0% -> 0% of each run, Pallas kernels for 0% -> 2%
where the time goes in v6:
time: 500 us
  Pallas kernels  485 us (97%)
  waiting for transfers between devices  9.18 us (2%)
    pallas_call x1, Pallas kernels, layer_call(): pl.pallas_call(layer_kernel, in_specs=[ANY] * len(IN_NAMES), out_specs=[A...  475 us
  transfers between devices with their start and end apart: 1, of which 1 were waited for; matrix products, arithmetic and copies ran while one was open for 0% of the time, Pallas kernels for 2%

profile of v6, /device:TPU:0, one launch (start us, length us, event | category | flops | bytes accessed | tf_op | source)
XLA Modules:
  0.0 499.6 jit_solution(1138732752705823773)
XLA Ops:
  0.7 475.1 %layer.1 = (bf16[32,64,1024]{2,1,0:T(8,128)(2,1)}, bf16[32,64,1024]{2,1,0:T(8,128)(2,1)}, f32[4,8,1024]{2,1,0:T(8,128)}, f32[512,1024]{1,0:T(8,128)}, f32[1024,5...) custom-call(bf16[32,64,1024]{2,1,0:T(8,128)(2,1)} %refs_0_.1, ...), custom_call_target="tpu_custom_call" | custom-call | tf_op jit(solution)/shard_map/layer/pallas_call | solution.py:817
  475.8 1.5 collective-permute-start
  477.3 9.8 %results.1 = (bf16[32,64,1024]{2,1,0:T(8,128)(2,1)}, bf16[32,64,1024]{2,1,0:T(8,128)(2,1)}, f32[512,1024]{1,0:T(8,128)}, f32[1024,512]{1,0:T(8,128)}, f32[128,10...) custom-call(bf16[32,64,1024]{2,1,0:T(8,128)(2,1)} %get-tuple-element, ...), custom_call_target="tpu_custom_call" | custom-call | flops 10000000000 | bytes 30000000 | tf_op jit(solution)/shard_map/results/pallas_call | solution.py:876
  487.0 9.2 %collective-permute-done = f32[384,1024]{1,0:T(8,128)} collective-permute-done((f32[384,1024]{1,0:T(8,128)}, f32[384,1024]{1,0:T(8,128)}, u32[]{:S(2)}, u32[]{:S(2)}) %collective-permute-start) | collective-permute-done | bytes 1572896 | tf_op jit(solution)/shard_map/ppermute | solution.py:915
  496.2 3.4 bitcast_add_fusion
Async XLA Ops:
  475.8 20.4 %collective-permute-start = (f32[384,1024]{1,0:T(8,128)}, f32[384,1024]{1,0:T(8,128)}, u32[]{:S(2)}, u32[]{:S(2)}) collective-permute-start(f32[384,1024]{1,0:T(8,128)} %get-tuple-element.46), channel_id=1, source_target_pairs={{0,4},{1,3},{2,6},{3,1},{4,0},{5,7},{6,2},{7,5}} | collective-permute-start | bytes 4718600 | tf_op jit(solution)/shard_map/ppermute | solution.py:915

commit v7 on v6

--- a/solution.py
+++ b/solution.py
@@ -226,9 +226,7 @@
         return remote(self.stage.at[j], self.r1.at[j], self.sem.at[2 + j], self.sem.at[4 + j], self.pc.a)
 
     def _second(self):
-        rows = self.r2.shape[0]
-        src = self.stage.at[2, pl.ds(self.stage.shape[1] - rows, rows)]
-        return remote(src, self.r2, self.sem.at[6], self.sem.at[7], self.pc.b)
+        return remote(self.stage.at[2], self.r2, self.sem.at[6], self.sem.at[7], self.pc.b)
 
     def send_pair(self, b, needs_credit):
         @pl.when(needs_credit)
@@ -267,19 +265,18 @@
         pl.when(own)(lambda: self.settle(lax.div(slot, 2), b, self.landed, gives_credit))
         pl.when(jnp.logical_not(own))(lambda: self.sent_pair(b))
 
-    def second(self, bufs, chunk_sem, lead=None):
+    def second(self, bufs, chunk_sem, dsts):
         n = chunk_sem.shape[1]
         size = bufs[0].shape[0]
         rows = size // n
         part = lambda ref, k: ref.at[pl.ds(k * rows, rows)]
         wait_for(self.r1.at[1], self.sem.at[5])
+        dsts = [part(d, k) for d in dsts for k in range(d.shape[0] // rows)]
         for p in range(self.stage.shape[1] // size):
             mine, theirs = (ref.at[pl.ds(p * size, size)] for ref in (self.stage.at[2], self.r1.at[1]))
             loads = [[pltpu.make_async_copy(part(src, k), part(buf, k), chunk_sem.at[x, k])
                       for x, (src, buf) in enumerate(zip((mine, theirs), bufs))] for k in range(n)]
-            to_lead = 0 if lead is None else lead.shape[0] // rows
-            stores = [pltpu.make_async_copy(part(bufs[0], k), part(lead if k < to_lead else mine, k), chunk_sem.at[2, k])
-                      for k in range(n)]
+            stores = [pltpu.make_async_copy(part(bufs[0], k), dsts[p * n + k], chunk_sem.at[2, k]) for k in range(n)]
             for group in loads:
                 for cp in group:
                     cp.start()
@@ -290,6 +287,8 @@
                 stores[k].start()
             for cp in stores:
                 cp.wait()
+
+    def send_second(self):
         self._second().start()
 
     def own_part(self, b0, b1, sem):
@@ -301,9 +300,12 @@
         cp.start()
         cp.wait()
 
-    def finish(self):
+    def sent_first(self):
         for j in range(2):
             self._first(j).wait_send()
+
+    def finish(self):
+        self.sent_first()
         self._second().wait()
 
 
@@ -355,7 +357,7 @@
 IN_NAMES = ("x_in", "dy_in", "wq", "wo", "wu", "wd") + tuple("in_" + k for k in SMALL)
 OUT_SHAPES = {
     "y_out": ((TP * NS, SL, D), bf16), "gx_out": ((TP * NS, SL, D), bf16), "msgs": ((TP // 2, ROWS, D), f32), "gd": ((FB, D), f32), "gu": ((D, FB), f32),
-    "a_stage": ((4, R3 + PW, D), f32), "a_r2": ((PW, D), f32), "gq_b": ((R3, D), f32), "a_r1": ((2, R3 + PW, D), f32),
+    "a_stage": ((4, R3 + PW, D), f32), "gq_b": ((R3, D), f32), "go_b": ((PW, D), f32), "a_r1": ((2, R3 + PW, D), f32),
     "m_r0": ((2 * FB, D), f32), "m_stage": ((4, 2 * FB, D), f32), "m_r1": ((2, 2 * FB, D), f32), "m_r2": ((2 * FB, D), f32),
     "xs": ((NS, S, D), bf16), "dys": ((NS, S, D), bf16), "wq_all": ((TP, R3, D), bf16), "wo_all": ((TP, PW, D), bf16),
     "wu_all": ((TP, D, FB), bf16), "wd_all": ((TP, FB, D), bf16),
@@ -672,7 +674,7 @@
 
         pl.run_scoped(open_bwd, vm(TP, PW, D, dtype=bf16))
         n_half = NS // 2
-        rs = GradScatter(pc, acc, r.landing.at[pl.ds(0, R3 + PW)], r.a_stage, r.a_r1, r.a_r2, r.a_sem, r.free)
+        rs = GradScatter(pc, acc, r.landing.at[pl.ds(0, R3 + PW)], r.a_stage, r.a_r1, r.landing, r.a_sem, r.free)
 
         def slot_at(g):
             return jnp.where(g < 4, lax.rem(g + 2, 4), g)
@@ -714,7 +716,8 @@
                     if half == 0:
                         @pl.when((sh == 0) & (n == 1))
                         def _():
-                            rs_m.second([buf, r.landing.at[pl.ds(FB, FB)]], r.chunk)
+                            rs_m.second([buf, r.landing.at[pl.ds(FB, FB)]], r.chunk, [r.m_stage.at[2]])
+                            rs_m.send_second()
                     else:
                         @pl.when(sh == n_half - 1)
                         def _():
@@ -747,7 +750,7 @@
                                     in_specs=[pl.BlockSpec((1, S, D), lambda sh: (half * n_half + sh, 0, 0))])(r.xs)
             last = jnp.int32(TP - 1)
             rs.later(last, last, False)
-            rs.second([buf, r.landing.at[pl.ds(FB, FB)]], r.chunk, r.gq_b)
+            rs.second([buf, r.landing.at[pl.ds(FB, FB)]], r.chunk, [r.gq_b, r.go_b])
 
         pl.run_scoped(heads, vm(n_half, TP * R3, S, dtype=bf16), vm(TP, R3, D, dtype=bf16), vm(FB, D))
 
@@ -802,7 +805,7 @@
                 y_a2a.finish(s)
             for s in range(NS):
                 gx_a2a.finish(s)
-            rs.finish()
+            rs.sent_first()
             own.wait()
             for sem in (r.s_ss.at[1], r.s_rs.at[1]):
                 wait_for(r.msgs.at[pl.ds(0, len(small))], sem)
@@ -827,23 +830,22 @@
 
 
 FINAL = {"y": ((TP * NS, SL, D), bf16), "gx": ((TP * NS, SL, D), bf16), "gd": ((FB, D), f32), "gu": ((D, FB), f32),
-         "go": ((PW, D), f32), "gbq": ((3, 2, HD), f32), "gbu": ((1, FB), f32)}
+         "gbq": ((3, 2, HD), f32), "gbu": ((1, FB), f32)}
 VECS = ("bd", "g2", "b2", "bo", "g1", "b1")
 FINAL |= {k: ((1, D), f32) for k in VECS}
 LATE = ("gbq", "gbu") + VECS
 
 
-def final_kernel(y_in, gx_in, msgs, gd_in, gu_in, stage, r2, *refs):
+def final_kernel(y_in, gx_in, msgs, gd_in, gu_in, *refs):
     outs, refs = Refs(FINAL, refs), refs[len(FINAL):]
-    msg_v, y_v, gx_v, gd_v, gu_v, sums, ld, st = refs[:8]
-    late = Refs(LATE, refs[8:])
+    msg_v, y_v, gx_v, gd_v, gu_v, ld, st = refs[:7]
+    late = Refs(LATE, refs[7:])
     moves = [([(msgs, msg_v)], [])]
-    moves.append(([(t, sums.at[x]) for x, t in enumerate((stage.at[3, pl.ds(R3, PW)], r2))], [(sums.at[0], outs.go)]))
     for src, buf, dst in ((gd_in, gd_v, outs.gd), (gu_in, gu_v, outs.gu), (y_in, y_v, outs.y), (gx_in, gx_v, outs.gx)):
         moves.append(([(src, buf)], [(buf, dst)]))
     copy = pltpu.make_async_copy
-    loads = [[copy(s, d, ld.at[i, x]) for x, (s, d) in enumerate(m[0])] for i, m in enumerate(moves)]
-    stores = [[copy(s, d, st.at[i, x]) for x, (s, d) in enumerate(m[1])] for i, m in enumerate(moves)]
+    loads = [[copy(s, d, ld.at[i]) for s, d in m[0]] for i, m in enumerate(moves)]
+    stores = [[copy(s, d, st.at[i]) for s, d in m[1]] for i, m in enumerate(moves)]
     for cps in loads:
         for cp in cps:
             cp.start()
@@ -861,29 +863,27 @@
                     lo = j * PW + h * HD
                     late.gbq[j, h:h + 1, :] = small[6:7, lo:lo + HD]
             late.gbu[...] = small[6:7, R3:R3 + FB]
-        if i == 1:
-            row_add(sums.at[0], [sums.at[1]])
         for cp in outward:
             cp.start()
-    small_out = load_all([(getattr(late, k), getattr(outs, k)) for k in LATE], st.at[len(moves)])
+    small_out = load_all([(getattr(late, k), getattr(outs, k)) for k in LATE], st.at[pl.ds(len(moves), len(LATE))])
     for cps in stores + [small_out]:
         for cp in cps:
             cp.wait()
 
 
-def final_call(y, gx, msgs, gd, gu, stage, r2):
+def final_call(y, gx, msgs, gd, gu):
     act = vm(*y.shape, dtype=bf16)
     return pl.pallas_call(
         final_kernel,
-        in_specs=[ANY] * 7,
+        in_specs=[ANY] * 5,
         out_specs=[ANY] * len(FINAL),
         out_shape=[sds(*v) for v in FINAL.values()],
-        scratch_shapes=[vm(*msgs.shape), act, act, vm(FB, D), vm(D, FB), vm(2, PW, D), DMA((6, 2)), DMA((7, len(LATE)))]
+        scratch_shapes=[vm(*msgs.shape), act, act, vm(FB, D), vm(D, FB), DMA((5,)), DMA((5 + len(LATE),))]
         + [vm(*FINAL[k][0]) for k in LATE],
         compiler_params=pltpu.CompilerParams(vmem_limit_bytes=VMEM_LIMIT),
         cost_estimate=pl.CostEstimate(flops=10 ** 10, bytes_accessed=3 * 10 ** 7, transcendentals=0),
         name="results",
-    )(y, gx, msgs, gd, gu, stage, r2)
+    )(y, gx, msgs, gd, gu)
 
 
 def rope_tables():
@@ -909,11 +909,13 @@
         parts = layer_call(
             x_in, grad_y, wq, w_out.reshape(PW, D), w_up, w_down, b_qkv, row(b_up), pad_mask, cos, sin,
             row(ln1_gain), row(ln1_bias), row(ln2_gain), row(ln2_bias), row(b_out), row(b_down))
-        *parts, gq_b = parts
-        stage = parts[-2]
+        *parts, stage, gq_b, go_b = parts
         to_b = [(i, i ^ (4 - 2 * (i % 2))) for i in range(TP)]
         gq = stage[-1, :R3] + lax.ppermute(gq_b, 'tp', to_b)
-        y, gx, gd, gu, go, gbq, gbu, *vecs = final_call(*parts)
+        go = lax.ppermute(go_b, 'tp', to_b)
+        gq, stage = lax.optimization_barrier((gq, stage))
+        go = stage[-1, R3:] + go
+        y, gx, gd, gu, gbq, gbu, *vecs = final_call(*parts)
         bd, g2, b2, bo, g1, b1 = (v.reshape(D) for v in vecs)
         return (y, gx, g1, b1, gq.reshape(3, 2, HD, D).transpose(0, 3, 1, 2), gbq, go.reshape(2, HD, D), bo, g2, b2,
                 gu, gbu.reshape(FB), gd, bd)

time: 500 us -> 499 us (level)
  Pallas kernels: 485 us -> 478 us
    pallas_call x1, Pallas kernels: 475 us -> 469 us  [layer_call(): pl.pallas_call(layer_kernel, in_specs=[ANY] * len(IN_NAMES), out_specs=[A...]
  transfers between devices with their start and end apart: 1 -> 2, of which waited for: 1 -> 2; matrix products, arithmetic and copies ran while one was open for 0% -> 1% of each run, Pallas kernels for 2% -> 2%
where the time goes in v7:
time: 499 us; the launch traced here: 498 us
  Pallas kernels  478 us (96%)
  waiting for transfers between devices  11.8 us (2%)
  other arithmetic  5.28 us (1%)
    pallas_call x1, Pallas kernels, layer_call(): pl.pallas_call(layer_kernel, in_specs=[ANY] * len(IN_NAMES), out_specs=[A...  469 us
  transfers between devices with their start and end apart: 2, of which 2 were waited for; matrix products, arithmetic and copies ran while one was open for 1% of the time, Pallas kernels for 2%

profile of v7, /device:TPU:0, one launch (start us, length us, event | category | flops | bytes accessed | tf_op | source)
XLA Modules:
  0.0 498.1 jit_solution(4940353640379598508)
XLA Ops:
  0.7 469.5 %layer.1 = (bf16[32,64,1024]{2,1,0:T(8,128)(2,1)}, bf16[32,64,1024]{2,1,0:T(8,128)(2,1)}, f32[4,8,1024]{2,1,0:T(8,128)}, f32[512,1024]{1,0:T(8,128)}, f32[1024,5...) custom-call(bf16[32,64,1024]{2,1,0:T(8,128)(2,1)} %refs_0_.1, ...), custom_call_target="tpu_custom_call" | custom-call | tf_op jit(solution)/shard_map/layer/pallas_call | solution.py:820
  470.2 1.5 collective-permute-start
  471.6 0.6 collective-permute-start.1
  472.2 8.8 %results.1 = (bf16[32,64,1024]{2,1,0:T(8,128)(2,1)}, bf16[32,64,1024]{2,1,0:T(8,128)(2,1)}, f32[512,1024]{1,0:T(8,128)}, f32[1024,512]{1,0:T(8,128)}, f32[3,2,64...) custom-call(bf16[32,64,1024]{2,1,0:T(8,128)(2,1)} %get-tuple-element, ...), custom_call_target="tpu_custom_call" | custom-call | flops 10000000000 | bytes 30000000 | tf_op jit(solution)/shard_map/results/pallas_call | solution.py:876
  481.1 9.5 %collective-permute-done = f32[384,1024]{1,0:T(8,128)} collective-permute-done((f32[384,1024]{1,0:T(8,128)}, f32[384,1024]{1,0:T(8,128)}, u32[]{:S(2)}, u32[]{:S(2)}) %collective-permute-start) | collective-permute-done | bytes 1572896 | tf_op jit(solution)/shard_map/ppermute | solution.py:914
  490.6 3.4 bitcast_add_fusion
  494.0 2.2 collective-permute-done.1
  496.2 1.9 bitcast_add_fusion.1
Async XLA Ops:
  470.2 20.4 %collective-permute-start = (f32[384,1024]{1,0:T(8,128)}, f32[384,1024]{1,0:T(8,128)}, u32[]{:S(2)}, u32[]{:S(2)}) collective-permute-start(f32[384,1024]{1,0:T(8,128)} %get-tuple-element.46), channel_id=1, source_target_pairs={{0,4},{1,3},{2,6},{3,1},{4,0},{5,7},{6,2},{7,5}} | collective-permute-start | bytes 4718600 | tf_op jit(solution)/shard_map/ppermute | solution.py:914
  471.6 24.6 %collective-permute-start.1 = (f32[128,1024]{1,0:T(8,128)}, f32[128,1024]{1,0:T(8,128)S(1)}, u32[]{:S(2)}, u32[]{:S(2)}) collective-permute-start(f32[128,1024]{1,0:T(8,128)} %get-tuple-element.50), channel_id=1, source_target_pairs={{0,4},{1,3},{2,6},{3,1},{4,0},{5,7},{6,2},{7,5}} | collective-permute-start | bytes 1572872 | tf_op jit(solution)/shard_map/ppermute | solution.py:915

commit v8 on v7

--- a/solution.py
+++ b/solution.py
@@ -111,11 +111,26 @@
             src, dst = self.pos.at[dev * NS + s], self.seq.at[s, self._rows(pc.me)]
         else:
             src, dst = self.seq.at[s, self._rows(dev)], self.pos.at[pc.me * NS + s]
-        return remote(src, dst, self.ss.at[s], self.rs.at[s], dev)
+        one = s if self.inward else 0
+        return remote(src, dst, self.ss.at[one], self.rs.at[one], dev)
 
     def start(self, s):
         for m in (*range(2, TP), 1):
             self._copy(s, m).start()
+
+    def start_all(self):
+        for m in (*range(2, TP), 1):
+            pc, dev = self.pc, self.pc.peer(m)
+            if self.inward:
+                src, dst = self.pos.at[pl.ds(dev * NS, NS)], self.seq.at[:, self._rows(pc.me)]
+            else:
+                src, dst = self.seq.at[:, self._rows(dev)], self.pos.at[pl.ds(pc.me * NS, NS)]
+            remote(src, dst, self.ss.at[0], self.rs.at[0], dev).start()
+
+    def finish_all(self):
+        rest = self.seq.at[:, pl.ds(0, S - SL)]
+        wait_for(rest, self.ss.at[0])
+        wait_for(rest, self.rs.at[0])
 
     def finish(self, s):
         all_rows = self.seq.at[s, pl.ds(0, S - SL)]
@@ -124,11 +139,11 @@
 
     def local_in(self, buf):
         pc = self.pc
-        return (pltpu.make_async_copy(self.pos.at[pl.ds(pc.me * NS, NS)], buf, self.ss.at[NS]),
-                pltpu.make_async_copy(buf, self.seq.at[:, self._rows(pc.me)], self.rs.at[NS]))
+        return (pltpu.make_async_copy(self.pos.at[pl.ds(pc.me * NS, NS)], buf, self.ss.at[self.ss.shape[0] - 1]),
+                pltpu.make_async_copy(buf, self.seq.at[:, self._rows(pc.me)], self.rs.at[self.rs.shape[0] - 1]))
 
     def local_out(self, s, src):
-        return pltpu.make_async_copy(src.at[s, self._rows(self.pc.me)], self.pos.at[self.pc.me * NS + s], self.ss.at[NS])
+        return pltpu.make_async_copy(src.at[s, self._rows(self.pc.me)], self.pos.at[self.pc.me * NS + s], self.ss.at[self.ss.shape[0] - 1])
 
 
 class Gather:
@@ -266,7 +281,7 @@
         pl.when(jnp.logical_not(own))(lambda: self.sent_pair(b))
 
     def second(self, bufs, chunk_sem, dsts):
-        n = chunk_sem.shape[1]
+        n = chunk_sem.shape[0] // 3
         size = bufs[0].shape[0]
         rows = size // n
         part = lambda ref, k: ref.at[pl.ds(k * rows, rows)]
@@ -274,9 +289,9 @@
         dsts = [part(d, k) for d in dsts for k in range(d.shape[0] // rows)]
         for p in range(self.stage.shape[1] // size):
             mine, theirs = (ref.at[pl.ds(p * size, size)] for ref in (self.stage.at[2], self.r1.at[1]))
-            loads = [[pltpu.make_async_copy(part(src, k), part(buf, k), chunk_sem.at[x, k])
+            loads = [[pltpu.make_async_copy(part(src, k), part(buf, k), chunk_sem.at[x * n + k])
                       for x, (src, buf) in enumerate(zip((mine, theirs), bufs))] for k in range(n)]
-            stores = [pltpu.make_async_copy(part(bufs[0], k), dsts[p * n + k], chunk_sem.at[2, k]) for k in range(n)]
+            stores = [pltpu.make_async_copy(part(bufs[0], k), dsts[p * n + k], chunk_sem.at[2 * n + k]) for k in range(n)]
             for group in loads:
                 for cp in group:
                     cp.start()
@@ -366,14 +381,13 @@
 }
 DMA = pltpu.SemaphoreType.DMA
 SCRATCH = SMALL | {
-    "in_sem": DMA((len(SMALL),)),
     "bs_all": vm(TP, ROWS, PW), "bs": vm(ROWS, PW), "mask": vm(NS, S, PW), "dacc": vm(NS * S, D), "landing": vm(2 * FB, D), "gbu": vm(TP, 1, FB), "va": vm(ROWS, D),
     "msg": vm(TP, ROWS, D), "msg_in": vm(TP, ROWS, D),
     "free": pltpu.SemaphoreType.REGULAR,
-    "x_ss": DMA((NS + 1,)), "x_rs": DMA((NS + 1,)), "dy_ss": DMA((NS + 1,)), "dy_rs": DMA((NS + 1,)),
-    "y_ss": DMA((NS + 1,)), "y_rs": DMA((NS + 1,)), "gx_ss": DMA((NS + 1,)), "gx_rs": DMA((NS + 1,)),
+    "x_ss": DMA((NS + 1,)), "x_rs": DMA((NS + 1,)), "dy_ss": DMA((2,)), "dy_rs": DMA((2,)),
+    "y_ss": DMA((1,)), "y_rs": DMA((1,)), "gx_ss": DMA((2,)), "gx_rs": DMA((1,)),
     "g_ss": DMA((5,)), "g_rs": DMA((5, TP + 1)), "m_sem": DMA((11,)), "a_sem": DMA((9,)), "s_ss": DMA((3,)), "s_rs": DMA((2,)),
-    "tmp": DMA((TP,)), "chunk": DMA((3, 4)), "w_sem": DMA((2, 2)),
+    "tmp": DMA((TP,)), "chunk": DMA((12,)), "w_sem": DMA((2, 2)),
 }
 
 
@@ -386,7 +400,7 @@
 def layer_kernel(*refs):
     r = Refs(IN_NAMES + tuple(OUT_SHAPES) + tuple(SCRATCH), refs)
     pc = Place()
-    small_in = load_all([(getattr(r, "in_" + k), getattr(r, k)) for k in SMALL], r.in_sem)
+    small_in = load_all([(getattr(r, "in_" + k), getattr(r, k)) for k in SMALL], r.chunk)
     entry_barrier(pc)
     x_a2a = AllToAll(pc, r.x_in, r.xs, r.x_ss, r.x_rs, True)
     dy_a2a = AllToAll(pc, r.dy_in, r.dys, r.dy_ss, r.dy_rs, True)
@@ -438,8 +452,7 @@
             g.last()
         for s in range(2, NS):
             x_a2a.start(s)
-        for s in range(NS):
-            dy_a2a.start(s)
+        dy_a2a.start_all()
         g_wu.start_a()
         g_wd.start_a()
         for g in (g_bs, g_wq, g_wo):
@@ -559,8 +572,8 @@
 
         fetch(jnp.int32(0))
         cps = []
+        dy_a2a.finish_all()
         for s in range(NS):
-            dy_a2a.finish(s)
             cps.append(pltpu.make_async_copy(r.dys.at[s], dy_v.at[pl.ds(s * S, S)], r.tmp.at[s]))
             cps[s].start()
         clear(yacc, r.dacc, r.gbu)
@@ -627,9 +640,9 @@
             cp = pltpu.make_async_copy(dy_v.at[rows], r.y_seq.at[s], r.tmp.at[NS + s])
             cp.start()
             stores.append(cp)
-        for s in range(NS):
-            stores[s].wait()
-            y_a2a.start(s)
+        for cp in stores:
+            cp.wait()
+        y_a2a.start_all()
 
     tok = vm(NS * S, D, dtype=bf16)
 
@@ -801,10 +814,8 @@
                 cp.start()
                 cp.wait()
             rs.own_part(b0, b1, r.tmp)
-            for s in range(NS):
-                y_a2a.finish(s)
-            for s in range(NS):
-                gx_a2a.finish(s)
+            y_a2a.finish_all()
+            gx_a2a.finish_all()
             rs.sent_first()
             own.wait()
             for sem in (r.s_ss.at[1], r.s_rs.at[1]):

time: 499 us -> 498 us (level)
  no operation moved by 1% of the time
where the time goes in v8:
time: 498 us
  Pallas kernels  478 us (96%)
  waiting for transfers between devices  11.8 us (2%)
  other arithmetic  5.28 us (1%)
    pallas_call x1, Pallas kernels, layer_call(): pl.pallas_call(layer_kernel, in_specs=[ANY] * len(IN_NAMES), out_specs=[A...  469 us
  transfers between devices with their start and end apart: 2, of which 2 were waited for; matrix products, arithmetic and copies ran while one was open for 1% of the time, Pallas kernels for 2%

profile of v8, /device:TPU:0, one launch (start us, length us, event | category | flops | bytes accessed | tf_op | source)
XLA Modules:
  0.0 497.8 jit_solution(6257856300065243824)
XLA Ops:
  0.7 469.2 %layer.1 = (bf16[32,64,1024]{2,1,0:T(8,128)(2,1)}, bf16[32,64,1024]{2,1,0:T(8,128)(2,1)}, f32[4,8,1024]{2,1,0:T(8,128)}, f32[512,1024]{1,0:T(8,128)}, f32[1024,5...) custom-call(bf16[32,64,1024]{2,1,0:T(8,128)(2,1)} %refs_0_.1, ...), custom_call_target="tpu_custom_call" | custom-call | tf_op jit(solution)/shard_map/layer/pallas_call | solution.py:831
  469.9 1.5 collective-permute-start
  471.4 0.5 collective-permute-start.1
  471.9 8.8 %results.1 = (bf16[32,64,1024]{2,1,0:T(8,128)(2,1)}, bf16[32,64,1024]{2,1,0:T(8,128)(2,1)}, f32[512,1024]{1,0:T(8,128)}, f32[1024,512]{1,0:T(8,128)}, f32[3,2,64...) custom-call(bf16[32,64,1024]{2,1,0:T(8,128)(2,1)} %get-tuple-element, ...), custom_call_target="tpu_custom_call" | custom-call | flops 10000000000 | bytes 30000000 | tf_op jit(solution)/shard_map/results/pallas_call | solution.py:887
  480.8 9.5 %collective-permute-done = f32[384,1024]{1,0:T(8,128)} collective-permute-done((f32[384,1024]{1,0:T(8,128)}, f32[384,1024]{1,0:T(8,128)}, u32[]{:S(2)}, u32[]{:S(2)}) %collective-permute-start) | collective-permute-done | bytes 1572896 | tf_op jit(solution)/shard_map/ppermute | solution.py:925
  490.3 3.4 bitcast_add_fusion
  493.7 2.2 collective-permute-done.1
  495.9 1.9 bitcast_add_fusion.1
Async XLA Ops:
  469.9 20.4 %collective-permute-start = (f32[384,1024]{1,0:T(8,128)}, f32[384,1024]{1,0:T(8,128)}, u32[]{:S(2)}, u32[]{:S(2)}) collective-permute-start(f32[384,1024]{1,0:T(8,128)} %get-tuple-element.46), channel_id=1, source_target_pairs={{0,4},{1,3},{2,6},{3,1},{4,0},{5,7},{6,2},{7,5}} | collective-permute-start | bytes 4718600 | tf_op jit(solution)/shard_map/ppermute | solution.py:925
  471.4 24.5 %collective-permute-start.1 = (f32[128,1024]{1,0:T(8,128)}, f32[128,1024]{1,0:T(8,128)S(1)}, u32[]{:S(2)}, u32[]{:S(2)}) collective-permute-start(f32[128,1024]{1,0:T(8,128)} %get-tuple-element.50), channel_id=1, source_target_pairs={{0,4},{1,3},{2,6},{3,1},{4,0},{5,7},{6,2},{7,5}} | collective-permute-start | bytes 1572872 | tf_op jit(solution)/shard_map/ppermute | solution.py:926

commit v9 on v8

--- a/solution.py
+++ b/solution.py
@@ -306,14 +306,14 @@
     def send_second(self):
         self._second().start()
 
-    def own_part(self, b0, b1, sem):
+    def own_part(self, b0, b1, sem, dsts):
         wait_for(self.r1.at[0], self.sem.at[4])
         for cp in load_all([(self.stage.at[3], b0), (self.r1.at[0], b1)], sem):
             cp.wait()
         row_add(b0, [b1])
-        cp = pltpu.make_async_copy(b0, self.stage.at[3], sem.at[0])
-        cp.start()
-        cp.wait()
+        n = dsts[0].shape[0]
+        for cp in load_all(list(zip((b0.at[pl.ds(0, n)], b0.at[pl.ds(n, PW)]), dsts)), sem):
+            cp.wait()
 
     def sent_first(self):
         for j in range(2):
@@ -372,7 +372,7 @@
 IN_NAMES = ("x_in", "dy_in", "wq", "wo", "wu", "wd") + tuple("in_" + k for k in SMALL)
 OUT_SHAPES = {
     "y_out": ((TP * NS, SL, D), bf16), "gx_out": ((TP * NS, SL, D), bf16), "msgs": ((TP // 2, ROWS, D), f32), "gd": ((FB, D), f32), "gu": ((D, FB), f32),
-    "a_stage": ((4, R3 + PW, D), f32), "gq_b": ((R3, D), f32), "go_b": ((PW, D), f32), "a_r1": ((2, R3 + PW, D), f32),
+    "gq_own": ((R3, D), f32), "go_own": ((PW, D), f32), "gq_b": ((R3, D), f32), "go_b": ((PW, D), f32), "a_stage": ((4, R3 + PW, D), f32), "a_r1": ((2, R3 + PW, D), f32),
     "m_r0": ((2 * FB, D), f32), "m_stage": ((4, 2 * FB, D), f32), "m_r1": ((2, 2 * FB, D), f32), "m_r2": ((2 * FB, D), f32),
     "xs": ((NS, S, D), bf16), "dys": ((NS, S, D), bf16), "wq_all": ((TP, R3, D), bf16), "wo_all": ((TP, PW, D), bf16),
     "wu_all": ((TP, D, FB), bf16), "wd_all": ((TP, FB, D), bf16),
@@ -813,7 +813,7 @@
                     cp = pltpu.make_async_copy(turned, r.gu, r.tmp.at[0])
                 cp.start()
                 cp.wait()
-            rs.own_part(b0, b1, r.tmp)
+            rs.own_part(b0, b1, r.tmp, (r.gq_own, r.go_own))
             y_a2a.finish_all()
             gx_a2a.finish_all()
             rs.sent_first()
@@ -837,7 +837,7 @@
         compiler_params=pltpu.CompilerParams(collective_id=0, has_side_effects=True, vmem_limit_bytes=VMEM_LIMIT),
         name="layer",
     )(*args)
-    return out[:8]
+    return out[:9]
 
 
 FINAL = {"y": ((TP * NS, SL, D), bf16), "gx": ((TP * NS, SL, D), bf16), "gd": ((FB, D), f32), "gu": ((D, FB), f32),
@@ -920,12 +920,12 @@
         parts = layer_call(
             x_in, grad_y, wq, w_out.reshape(PW, D), w_up, w_down, b_qkv, row(b_up), pad_mask, cos, sin,
             row(ln1_gain), row(ln1_bias), row(ln2_gain), row(ln2_bias), row(b_out), row(b_down))
-        *parts, stage, gq_b, go_b = parts
+        *parts, gq_own, go_own, gq_b, go_b = parts
         to_b = [(i, i ^ (4 - 2 * (i % 2))) for i in range(TP)]
-        gq = stage[-1, :R3] + lax.ppermute(gq_b, 'tp', to_b)
+        gq = gq_own + lax.ppermute(gq_b, 'tp', to_b)
         go = lax.ppermute(go_b, 'tp', to_b)
-        gq, stage = lax.optimization_barrier((gq, stage))
-        go = stage[-1, R3:] + go
+        gq, go_own = lax.optimization_barrier((gq, go_own))
+        go = go_own + go
         y, gx, gd, gu, gbq, gbu, *vecs = final_call(*parts)
         bd, g2, b2, bo, g1, b1 = (v.reshape(D) for v in vecs)
         return (y, gx, g1, b1, gq.reshape(3, 2, HD, D).transpose(0, 3, 1, 2), gbq, go.reshape(2, HD, D), bo, g2, b2,

time: 498 us -> 497 us (level)
  no operation moved by 1% of the time
where the time goes in v9:
time: 497 us
  Pallas kernels  478 us (96%)
  waiting for transfers between devices  11.8 us (2%)
    pallas_call x1, Pallas kernels, layer_call(): pl.pallas_call(layer_kernel, in_specs=[ANY] * len(IN_NAMES), out_specs=[A...  469 us
  transfers between devices with their start and end apart: 2, of which 2 were waited for; matrix products, arithmetic and copies ran while one was open for 1% of the time, Pallas kernels for 2%

profile of v9, /device:TPU:0, one launch (start us, length us, event | category | flops | bytes accessed | tf_op | source)
XLA Modules:
  0.0 496.8 jit_solution(14804892993603868782)
XLA Ops:
  0.7 469.2 %layer.1 = (bf16[32,64,1024]{2,1,0:T(8,128)(2,1)}, bf16[32,64,1024]{2,1,0:T(8,128)(2,1)}, f32[4,8,1024]{2,1,0:T(8,128)}, f32[512,1024]{1,0:T(8,128)}, f32[1024,5...) custom-call(bf16[32,64,1024]{2,1,0:T(8,128)(2,1)} %refs_0_.1, ...), custom_call_target="tpu_custom_call" | custom-call | tf_op jit(solution)/shard_map/layer/pallas_call | solution.py:831
  469.9 1.5 collective-permute-start
  471.4 0.5 collective-permute-start.1
  471.9 8.8 %results.1 = (bf16[32,64,1024]{2,1,0:T(8,128)(2,1)}, bf16[32,64,1024]{2,1,0:T(8,128)(2,1)}, f32[512,1024]{1,0:T(8,128)}, f32[1024,512]{1,0:T(8,128)}, f32[3,2,64...) custom-call(bf16[32,64,1024]{2,1,0:T(8,128)(2,1)} %get-tuple-element, ...), custom_call_target="tpu_custom_call" | custom-call | flops 10000000000 | bytes 30000000 | tf_op jit(solution)/shard_map/results/pallas_call | solution.py:887
  480.8 0.0 copy-start
  480.8 9.5 %collective-permute-done = f32[384,1024]{1,0:T(8,128)} collective-permute-done((f32[384,1024]{1,0:T(8,128)}, f32[384,1024]{1,0:T(8,128)}, u32[]{:S(2)}, u32[]{:S(2)}) %collective-permute-start) | collective-permute-done | bytes 1572896 | tf_op jit(solution)/shard_map/ppermute | solution.py:925
  490.3 3.4 add.6
  493.7 2.2 collective-permute-done.1
  495.9 0.0 copy-done
  495.9 0.9 add.7
Async XLA Ops:
  469.9 20.4 %collective-permute-start = (f32[384,1024]{1,0:T(8,128)}, f32[384,1024]{1,0:T(8,128)}, u32[]{:S(2)}, u32[]{:S(2)}) collective-permute-start(f32[384,1024]{1,0:T(8,128)} %get-tuple-element.47), channel_id=1, source_target_pairs={{0,4},{1,3},{2,6},{3,1},{4,0},{5,7},{6,2},{7,5}} | collective-permute-start | bytes 4718600 | tf_op jit(solution)/shard_map/ppermute | solution.py:925
  471.4 24.5 %collective-permute-start.1 = (f32[128,1024]{1,0:T(8,128)}, f32[128,1024]{1,0:T(8,128)S(1)}, u32[]{:S(2)}, u32[]{:S(2)}) collective-permute-start(f32[128,1024]{1,0:T(8,128)} %get-tuple-element.52), channel_id=1, source_target_pairs={{0,4},{1,3},{2,6},{3,1},{4,0},{5,7},{6,2},{7,5}} | collective-permute-start | bytes 1572872 | tf_op jit(solution)/shard_map/ppermute | solution.py:926
  480.8 15.2 %copy-start = (f32[128,1024]{1,0:T(8,128)S(1)}, f32[128,1024]{1,0:T(8,128)}, u32[]{:S(2)}) copy-start(f32[128,1024]{1,0:T(8,128)} %get-tuple-element.51) | copy-start | bytes 1572868
